TPU v7x, 256 devices: a whole 4x4x8 slice. The times are simulated.
256 devices in a mesh: ba: 8 (over x, core), ma: 16 (over z, y_hi), row: 2 (over y_lo).
Axes of the slice: x: 4, y: 4 (y_hi: 2, y_lo: 2; y = y_hi * 2 + y_lo), z: 8, core: 2. Of those that a mesh axis runs over, the one named last changes fastest.
Arguments:
- tokens: bfloat16 [16, 256, 4096], P(('ba', 'row'), None, 'ma'), may hold values from -6 to 6
- attn_gain: bfloat16 [4096], P('ma'), may hold values from 0.25 to 1.75
- query_weight: bfloat16 [4096, 4096], P('row', 'ma'), may hold values from -0.046875 to 0.046875
- key_weight: bfloat16 [4096, 4096], P('row', 'ma'), may hold values from -0.046875 to 0.046875
- value_projection_matrix: bfloat16 [4096, 4096], P('row', 'ma'), may hold values from -0.09375 to 0.09375
- attention_output_matrix: bfloat16 [4096, 4096], P('ma', 'row'), may hold values from -0.125 to 0.125
- bucket_bias_matrix: float32 [32, 64], P(None, 'ma'), may hold values from -6 to 215, as said below
- ffn_gain: bfloat16 [4096], P('ma'), may hold values from 0.25 to 1.75
- gate_weight: bfloat16 [4096, 8192], P(None, ('ma', 'row')), may hold values from -0.09375 to 0.09375
- up_weight: bfloat16 [4096, 8192], P(None, ('ma', 'row')), may hold values from -0.09375 to 0.09375
- down_projection_weight: bfloat16 [8192, 4096], P(('ma', 'row')), may hold values from -0.125 to 0.125
Outputs:
- encoded: bfloat16 [16, 256, 4096], P(('ba', 'row'), None, 'ma')
Inputs may be any that keep to these rules, and one draw needn't show every extreme that they name: `bucket_bias_matrix`: entries of the relative position table.
All inputs are finite; a program needn't handle non-finite values.
Results may differ from a plain program's by a relative error of at most 0.017.
Values may be sent and summed in bfloat16 or wider, within the bound.
No kernel may reach another device: no remote copies, remote signals or barrier semaphores. Data moves between devices by JAX's collectives and lax.ppermute only.
A program may use at most 128 MiB of HBM per device.

v0:
```python
import functools

import jax
import jax.numpy as jnp
from jax import lax
from jax.experimental import pallas as pl
from jax.experimental.pallas import tpu as pltpu
from jax.sharding import Mesh
from jax.sharding import PartitionSpec as P

MA = ("ma_0", "ma_1")
MA_ROW = ("ma_0", "ma_1", "row")

bucket_thresholds = (1, 2, 3, 4, 5, 6, 7, 8, 11, 16, 23, 32, 45, 64, 91, 128)
epsilon = 1e-06
RING = 8
SWAP = [(0, 1), (1, 0)]
UP = [(i, (i + 1) % RING) for i in range(RING)]
DOWN = [(i, (i - 1) % RING) for i in range(RING)]


def tied(value, *after):
    return lax.optimization_barrier((value, *after))[0]


def pair_order(mine, theirs, axis):
    first = lax.axis_index("ma_1") == 0
    return jnp.where(
        first,
        jnp.concatenate([mine, theirs], axis=axis),
        jnp.concatenate([theirs, mine], axis=axis),
    )


def ring_gather(block):
    held = {0: block}
    above = below = block
    for step in range(1, RING // 2 + 1):
        above = lax.ppermute(above, "ma_0", DOWN)
        held[step] = above
        if step < RING // 2:
            below = lax.ppermute(below, "ma_0", UP)
            held[RING - step] = below
    return held


SEND = (4, 5, 3, 6, 2, 7, 1, 0)


def ring_sum(stack):
    def block(owner):
        return stack[SEND.index(owner % RING)].astype(jnp.float32)

    up, down = stack[0], stack[1]
    got_down = None
    for step in range(1, RING // 2 + 1):
        got_up = lax.ppermute(up, "ma_0", UP)
        if step > 1:
            got_down = lax.ppermute(down, "ma_0", DOWN)
        if step < RING // 2:
            up = (got_up.astype(jnp.float32) + block(4 - step)).astype(jnp.bfloat16)
            if got_down is not None:
                down = (got_down.astype(jnp.float32) + block(step - 4)).astype(jnp.bfloat16)
    return got_up.astype(jnp.float32) + got_down.astype(jnp.float32) + block(0)


def bias_kernel(bucket_ref, table_ref, bias_ref):
    heads, rows, columns = bias_ref.shape
    row = bucket_ref[0:1, :]
    for h in range(heads):
        line = jnp.zeros(row.shape, jnp.float32)
        for b in range(table_ref.shape[0]):
            line = jnp.where(row == b, table_ref[b : b + 1, h : h + 1], line)
        wide = jnp.broadcast_to(line, (rows, row.shape[1]))
        bias_ref[h] = pltpu.roll(wide, 0, 1, stride=1, stride_axis=0)[:, :columns]


def position_bias(table, length):
    offset = jnp.arange(2 * length, dtype=jnp.int32)
    offset = jnp.where(offset < length, offset, offset - 2 * length)
    distance = jnp.abs(offset)
    bucket = jnp.where(offset > 0, 15, 0)
    for threshold in bucket_thresholds[:15]:
        bucket = bucket + (distance >= threshold).astype(jnp.int32)
    last = (distance >= bucket_thresholds[15]) & (offset > 0)
    bucket = bucket + last.astype(jnp.int32)
    heads = table.shape[1]
    return pl.pallas_call(
        bias_kernel,
        out_shape=jax.ShapeDtypeStruct((heads, length, length), jnp.float32),
        cost_estimate=pl.CostEstimate(flops=10**8, bytes_accessed=10**6, transcendentals=0),
        name="position_bias",
    )(jnp.broadcast_to(bucket[None], (8, 2 * length)), table)


def as_column(line):
    size = line.shape[1]
    at_row = lax.broadcasted_iota(jnp.int32, (size, size), 0)
    at_column = lax.broadcasted_iota(jnp.int32, (size, size), 1)
    spread_out = jnp.where(at_row == at_column, jnp.broadcast_to(line, (size, size)), 0.0)
    return jnp.sum(spread_out, axis=1, keepdims=True)


def dot(a, b):
    return jnp.dot(a, b, preferred_element_type=jnp.float32)


def attention_kernel(width, at_ref, *refs):
    blocks = refs[:RING]
    own = refs[RING : RING + 3]
    other_ref, own_out_ref, other_out_ref, bias_ref = refs[RING + 3 : RING + 7]
    out_ref, x_ref, w_ref, o_ref, acc_ref, attended_ref = refs[RING + 7 : RING + 13]
    x_sem, own_sem, other_sem, o_sem = refs[RING + 13 :]
    length = acc_ref.shape[0]
    inner = attended_ref.shape[1]
    wide = x_ref.shape[2]
    parts = RING // 2
    rows = parts * wide

    own_copies = [
        pltpu.make_async_copy(
            own[k], w_ref.at[pl.ds(0, rows), pl.ds(k * inner, inner)], own_sem.at[k]
        )
        for k in range(3)
    ]
    x_copies = [
        pltpu.make_async_copy(blocks[k], x_ref.at[k], x_sem.at[k]) for k in range(RING)
    ]
    other_copies = [
        pltpu.make_async_copy(
            other_ref.at[pl.ds(k * wide, wide), :],
            w_ref.at[pl.ds(rows + k * wide, wide), :],
            other_sem.at[k],
        )
        for k in range(parts)
    ]
    o_copies = [
        pltpu.make_async_copy(ref, o_ref.at[k], o_sem.at[k])
        for k, ref in enumerate((own_out_ref, other_out_ref))
    ]
    for copy in x_copies + own_copies + other_copies + o_copies:
        copy.start()
    for copy in x_copies:
        copy.wait()
    squares = x_ref[0, length : length + 1, :length].astype(jnp.float32)
    for k in range(1, RING):
        squares += x_ref[k, length : length + 1, :length].astype(jnp.float32)
    scale = as_column(lax.rsqrt(squares / width + epsilon))
    for copy in own_copies:
        copy.wait()
    acc_ref[...] = jnp.zeros_like(acc_ref)

    def add_slot(slot, unused):
        weights = w_ref[pl.ds(pl.multiple_of(slot * wide, wide), wide), :]
        acc_ref[...] += dot(x_ref[at_ref[slot], :length, :], weights)
        return unused

    lax.fori_loop(0, parts, add_slot, 0)
    for copy in other_copies:
        copy.wait()
    lax.fori_loop(parts, RING, add_slot, 0)

    query, key, value = (
        (acc_ref[:, k * inner : (k + 1) * inner] * scale).astype(jnp.bfloat16) for k in range(3)
    )
    heads = bias_ref.shape[0]
    size = inner // heads
    for h in range(heads):
        at = slice(h * size, (h + 1) * size)
        scores = (
            lax.dot_general(
                query[:, at],
                key[:, at],
                (((1,), (1,)), ((), ())),
                preferred_element_type=jnp.float32,
            )
            + bias_ref[h]
        )
        exponent = jnp.exp(scores - jnp.max(scores, axis=-1, keepdims=True))
        weights = exponent / jnp.sum(exponent, axis=-1, keepdims=True)
        attended_ref[:, at] = dot(weights.astype(jnp.bfloat16), value[:, at]).astype(jnp.bfloat16)

    for copy in o_copies:
        copy.wait()

    def out_block(j, unused):
        slot = at_ref[RING + j]
        which = slot // parts
        column = pl.multiple_of((slot - which * parts) * wide, wide)
        out_ref[j] = dot(attended_ref[...], o_ref[which, :, pl.ds(column, wide)]).astype(
            jnp.bfloat16
        )
        return unused

    lax.fori_loop(0, RING, out_block, 0)


ANY = pl.BlockSpec(memory_space=pl.ANY)
SMEM = pl.BlockSpec(memory_space=pltpu.SMEM)
IN_VMEM = pl.BlockSpec(memory_space=pltpu.VMEM)


def attention(held, bias, own, other, own_out, other_out, ring_at, half):
    length = bias.shape[1]
    inner = own[0].shape[1]
    rows, wide = held[0].shape
    parts = RING // 2
    slot = jnp.arange(RING, dtype=jnp.int32)
    block_of = jnp.mod(slot + half * parts - ring_at, RING)
    slot_of = jnp.mod(jnp.asarray(SEND, jnp.int32) + ring_at + half * parts, RING)
    table = jnp.concatenate([block_of, slot_of]).astype(jnp.int32)
    return pl.pallas_call(
        functools.partial(attention_kernel, float(wide * RING)),
        in_specs=[SMEM] + [ANY] * (RING + 6) + [IN_VMEM],
        out_specs=IN_VMEM,
        scratch_shapes=[
            pltpu.VMEM((RING, rows, wide), jnp.bfloat16),
            pltpu.VMEM((RING * wide, 3 * inner), jnp.bfloat16),
            pltpu.VMEM((2, *own_out.shape), jnp.bfloat16),
            pltpu.VMEM((length, 3 * inner), jnp.float32),
            pltpu.VMEM((length, inner), jnp.bfloat16),
            pltpu.SemaphoreType.DMA((RING,)),
            pltpu.SemaphoreType.DMA((3,)),
            pltpu.SemaphoreType.DMA((parts,)),
            pltpu.SemaphoreType.DMA((2,)),
        ],
        out_shape=jax.ShapeDtypeStruct((RING, length, wide), jnp.bfloat16),
        cost_estimate=pl.CostEstimate(
            flops=2 * length * wide * RING * 4 * inner, bytes_accessed=10**7, transcendentals=0
        ),
        name="attention",
    )(
        table,
        *[held[k] for k in range(RING)],
        *own,
        other,
        own_out,
        other_out,
        bias,
    )


EARLY = (0, 1, 7, 2, 6)
LATE = (3, 5, 4)


def gate_copies(at_ref, blocks, gate_ref, up_ref, other_ref, x_ref, w_ref, x_sem, w_sem):
    wide, hidden = x_ref.shape[2], gate_ref.shape[1]
    copies = []
    for k, block in enumerate(blocks):
        row = pl.ds(pl.multiple_of(at_ref[k] * wide, wide), wide)
        copies.append(
            (
                pltpu.make_async_copy(block, x_ref.at[k], x_sem.at[k]),
                pltpu.make_async_copy(
                    gate_ref.at[row, :], w_ref.at[k, :, pl.ds(0, hidden)], w_sem.at[k, 0]
                ),
                pltpu.make_async_copy(
                    up_ref.at[row, :], w_ref.at[k, :, pl.ds(hidden, hidden)], w_sem.at[k, 1]
                ),
                pltpu.make_async_copy(
                    other_ref.at[at_ref[k], pl.ds(0, wide), :],
                    w_ref.at[k, :, pl.ds(2 * hidden, 2 * hidden)],
                    w_sem.at[k, 2],
                ),
            )
        )
    return copies


def start(copies):
    for group in copies:
        for copy in group:
            copy.start()


def gate_products(copies, x_ref, w_ref, acc_ref, squares_ref):
    length = acc_ref.shape[0]
    for group in copies:
        for copy in group:
            copy.wait()

    def add_block(k, unused):
        squares_ref[...] += x_ref[k, length : length + 8, :length].astype(jnp.float32)
        acc_ref[...] += dot(x_ref[k, :length, :], w_ref[k])
        return unused

    lax.fori_loop(0, len(copies), add_block, 0)


def gate_kernel(at_ref, *refs):
    count = len(EARLY)
    blocks = refs[:count]
    gate_ref, up_ref, other_ref, acc_ref, squares_ref, x_ref, w_ref, x_sem, w_sem = refs[count:]
    copies = gate_copies(at_ref, blocks, gate_ref, up_ref, other_ref, x_ref, w_ref, x_sem, w_sem)
    start(copies)
    acc_ref[...] = jnp.zeros_like(acc_ref)
    squares_ref[...] = jnp.zeros_like(squares_ref)
    gate_products(copies, x_ref, w_ref, acc_ref, squares_ref)


def down_kernel(width, at_ref, *refs):
    count = len(LATE)
    blocks = refs[:count]
    gate_ref, up_ref, other_ref, down_ref, acc_in_ref, squares_in_ref = refs[count : count + 6]
    out_ref, x_ref, w_ref, d_ref, acc_ref, squares_ref, hidden_ref = refs[count + 6 : count + 13]
    x_sem, w_sem, d_sem = refs[count + 13 :]
    size = gate_ref.shape[1]
    wide = x_ref.shape[2]
    copies = gate_copies(at_ref, blocks, gate_ref, up_ref, other_ref, x_ref, w_ref, x_sem, w_sem)
    start(copies)
    down_copies = []
    for j in range(RING):
        slot = at_ref[count + j]
        column = pl.ds(pl.multiple_of(slot * wide, wide), wide)
        down_copies.append(
            (
                pltpu.make_async_copy(
                    down_ref.at[:, column], d_ref.at[j, pl.ds(0, size), :], d_sem.at[j, 0]
                ),
                pltpu.make_async_copy(
                    other_ref.at[slot, pl.ds(wide, size), :],
                    d_ref.at[j, pl.ds(size, size), :],
                    d_sem.at[j, 1],
                ),
            )
        )
    start(down_copies)
    acc_ref[...] = acc_in_ref[...]
    squares_ref[...] = squares_in_ref[...]
    gate_products(copies, x_ref, w_ref, acc_ref, squares_ref)
    mean = squares_ref[0:1, :] / width
    scale = as_column(lax.rsqrt(mean + epsilon))
    for k in range(2):
        gate = acc_ref[:, 2 * k * size : (2 * k + 1) * size] * scale
        up = acc_ref[:, (2 * k + 1) * size : (2 * k + 2) * size] * scale
        hidden_ref[:, k * size : (k + 1) * size] = (
            jax.nn.gelu(gate, approximate=True) * up
        ).astype(jnp.bfloat16)
    for group in down_copies:
        for copy in group:
            copy.wait()

    def out_block(j, unused):
        out_ref[j] = dot(hidden_ref[...], d_ref[j]).astype(jnp.bfloat16)
        return unused

    lax.fori_loop(0, RING, out_block, 0)


def feed_forward(held, gate, up, down, other, ring_at):
    rows, wide = held[0].shape
    hidden = gate.shape[1]
    length = rows - 8

    def slots(owners):
        return jnp.mod(jnp.asarray(owners, jnp.int32) + ring_at, RING).astype(jnp.int32)

    def scratch(count):
        return [
            pltpu.VMEM((count, rows, wide), jnp.bfloat16),
            pltpu.VMEM((count, wide, 4 * hidden), jnp.bfloat16),
        ]

    sums = [
        jax.ShapeDtypeStruct((length, 4 * hidden), jnp.float32),
        jax.ShapeDtypeStruct((8, length), jnp.float32),
    ]
    early, late = len(EARLY), len(LATE)
    acc, squares = pl.pallas_call(
        gate_kernel,
        in_specs=[SMEM] + [ANY] * (early + 3),
        out_specs=[IN_VMEM] * 2,
        scratch_shapes=scratch(early)
        + [pltpu.SemaphoreType.DMA((early,)), pltpu.SemaphoreType.DMA((early, 3))],
        out_shape=sums,
        cost_estimate=pl.CostEstimate(
            flops=2 * length * wide * 4 * hidden * early,
            bytes_accessed=5 * 10**6,
            transcendentals=0,
        ),
        name="gate_early",
    )(slots(EARLY), *[held[k] for k in EARLY], gate, up, other)

    return pl.pallas_call(
        functools.partial(down_kernel, float(wide * RING)),
        in_specs=[SMEM] + [ANY] * (late + 4) + [IN_VMEM] * 2,
        out_specs=IN_VMEM,
        scratch_shapes=scratch(late)
        + [
            pltpu.VMEM((RING, 2 * hidden, wide), jnp.bfloat16),
            pltpu.VMEM((length, 4 * hidden), jnp.float32),
            pltpu.VMEM((8, length), jnp.float32),
            pltpu.VMEM((length, 2 * hidden), jnp.bfloat16),
            pltpu.SemaphoreType.DMA((late,)),
            pltpu.SemaphoreType.DMA((late, 3)),
            pltpu.SemaphoreType.DMA((RING, 2)),
        ],
        out_shape=jax.ShapeDtypeStruct((RING, length, wide), jnp.bfloat16),
        cost_estimate=pl.CostEstimate(
            flops=2 * length * wide * hidden * (4 * late + 2 * RING),
            bytes_accessed=7 * 10**6,
            transcendentals=0,
        ),
        name="gate_late_and_down",
    )(slots(LATE + SEND), *[held[k] for k in LATE], gate, up, other, down, acc, squares)


def spread(values, gain):
    rows, width = values.shape
    as_float = values.astype(jnp.float32)
    squares = jnp.sum(as_float * as_float, axis=1)
    gained = (as_float * gain.astype(jnp.float32)).astype(jnp.bfloat16)
    line = jnp.concatenate([squares, jnp.zeros((width - rows,), jnp.float32)])
    tail = jnp.broadcast_to(line.astype(jnp.bfloat16)[None], (8, width))
    return ring_gather(jnp.concatenate([gained, tail], axis=0))


def layer(
    tokens,
    attn_gain,
    query_weight,
    key_weight,
    value_projection_matrix,
    attention_output_matrix,
    bucket_bias_matrix,
    ffn_gain,
    gate_weight,
    up_weight,
    down_projection_weight,
):
    sequences, length, part = tokens.shape
    half = lax.axis_index("row")
    ring_at = lax.axis_index("ma_0")
    copy_at = lax.axis_index("ba")
    copies = lax.axis_size("ba")
    token_rows = tokens.reshape(length, part)

    gains = jnp.concatenate(
        [attn_gain[None], ffn_gain[None], jnp.zeros((6, part), jnp.bfloat16)], axis=0
    )
    mine = jnp.concatenate([token_rows, gains], axis=0)
    theirs = lax.ppermute(mine, "ma_1", SWAP)

    half_rows = query_weight.shape[0]
    depth = half_rows // copies
    share = [
        lax.dynamic_slice_in_dim(w, copy_at * depth, depth, 0)
        for w in (query_weight, key_weight, value_projection_matrix)
    ]
    first_share = lax.ppermute(jnp.concatenate(share, axis=1), "row", SWAP)
    other_first = lax.all_gather(first_share, "ba", axis=0, tiled=True)
    other_out = lax.ppermute(tied(attention_output_matrix, theirs), "row", SWAP)

    gate_depth = gate_weight.shape[0] // copies
    gate_share = [
        lax.dynamic_slice_in_dim(w, copy_at * gate_depth, gate_depth, 0)
        for w in (gate_weight, up_weight)
    ]
    down_width = down_projection_weight.shape[1] // copies
    down_share = lax.dynamic_slice_in_dim(
        down_projection_weight, copy_at * down_width, down_width, 1
    )
    second_share = jnp.concatenate([jnp.concatenate(gate_share, axis=1), down_share], axis=0)

    wide = pair_order(mine, theirs, 1)
    wide_tokens = wide[:length]
    wide_attn_gain = wide[length]
    wide_ffn_gain = wide[length + 1]

    held = spread(wide_tokens, wide_attn_gain)
    second_share = lax.ppermute(tied(second_share, held[1]), "row", SWAP)
    out_blocks = attention(
        held,
        position_bias(bucket_bias_matrix, length),
        (query_weight, key_weight, value_projection_matrix),
        other_first,
        attention_output_matrix,
        other_out,
        ring_at,
        half,
    )
    second_share = tied(second_share, out_blocks)
    other_second = lax.all_gather(second_share, "ba", axis=0, tiled=False)
    summed = ring_sum(out_blocks).astype(jnp.bfloat16)
    partner = lax.ppermute(summed, "ma_1", SWAP)
    attn_out = summed.astype(jnp.float32) + partner.astype(jnp.float32)
    residual = (wide_tokens.astype(jnp.float32) + attn_out).astype(jnp.bfloat16)
    first = lax.axis_index("ma_1") == 0
    own_residual = jnp.where(first, residual[:, :part], residual[:, part:])

    held = spread(residual, wide_ffn_gain)
    summed = ring_sum(
        feed_forward(held, gate_weight, up_weight, down_projection_weight, other_second, ring_at)
    )
    low, high = summed[:, :part], summed[:, part:]
    keep = jnp.where(first, low, high)
    give = jnp.where(first, high, low).astype(jnp.bfloat16)
    got = lax.ppermute(give, "ma_1", SWAP)
    encoded = own_residual.astype(jnp.float32) + keep + got.astype(jnp.float32)
    return encoded.astype(jnp.bfloat16).reshape(sequences, length, part)


def solution(mesh):
    split = Mesh(
        mesh.devices.reshape(mesh.shape["ba"], RING, 2, mesh.shape["row"]),
        ("ba", "ma_0", "ma_1", "row"),
    )
    return jax.shard_map(
        layer,
        mesh=split,
        in_specs=(
            P(("ba", "row"), None, MA),
            P(MA),
            P("row", MA),
            P("row", MA),
            P("row", MA),
            P(MA, "row"),
            P(None, MA),
            P(MA),
            P(None, MA_ROW),
            P(None, MA_ROW),
            P(MA_ROW, None),
        ),
        out_specs=P(("ba", "row"), None, MA),
        check_vma=False,
    )
```

profile of v0, /device:TPU:6, one launch (start us, length us, event | category | flops | bytes accessed | tf_op | source)
XLA Modules:
  0.0 224.4 jit_solution(9286519665306062945)
XLA Ops:
  6.5 1.0 constant_dynamic-slice_fusion.5
  7.6 1.0 constant_dynamic-slice_fusion.3
  8.6 1.7 collective-permute-start.8
  10.3 9.3 %collective-permute-done.8 = bf16[256,768]{1,0:T(8,128)(2,1)S(1)} collective-permute-done((bf16[256,768]{1,0:T(8,128)(2,1)S(1)}, bf16[256,768]{1,0:T(8,128)(2,1)S(1)}, u32[]{:S(2)}, u32[]{:S(2)}) %collective-permute-start.8) | collective-permute-done | bytes 393248 | tf_op jit(solution)/shard_map/ppermute | solution.py:451
  19.5 0.8 copy-done.5
  20.4 0.7 broadcast_in_dim.18
  21.0 0.7 broadcast_in_dim.19
  21.7 0.9 pad_maximum_fusion.4
  22.6 3.3 %collective-permute-start = (bf16[264,256]{1,0:T(8,128)(2,1)S(1)}, bf16[264,256]{1,0:T(8,128)(2,1)S(1)}, u32[]{:S(2)}, u32[]{:S(2)}) collective-permute-start(bf16[264,256]{1,0:T(8,128)(2,1)S(1)} %pad_maximum_fusion.4), channel_id=1, source_target_pairs={{0,2},{2,0},{1,3},{3,1},{4,6},{6,4},{5,7},{7,5},{8,10},{10,8},{9,1... | collective-permute-start | bytes 405512 | tf_op jit(solution)/shard_map/ppermute | solution.py:443
  25.9 3.3 %collective-permute-done = bf16[264,256]{1,0:T(8,128)(2,1)S(1)} collective-permute-done((bf16[264,256]{1,0:T(8,128)(2,1)S(1)}, bf16[264,256]{1,0:T(8,128)(2,1)S(1)}, u32[]{:S(2)}, u32[]{:S(2)}) %collective-permute-start) | collective-permute-done | bytes 135200 | tf_op jit(solution)/shard_map/ppermute | solution.py:443
  29.6 5.9 %collective-permute-start.1 = (bf16[264,512]{1,0:T(8,128)(2,1)S(1)}, bf16[264,512]{1,0:T(8,128)(2,1)S(1)}, u32[]{:S(2)}, u32[]{:S(2)}) collective-permute-start(bf16[264,512]{1,0:T(8,128)(2,1)S(1)} %pad_maximum_fusion.2.refs_0_), channel_id=1, source_target_pairs={{0,28},{4,0},{8,4},{12,8},{16,12},{20,16},{24,20},{28,24},{1,29},{... | collective-permute-start | bytes 811016 | tf_op jit(solution)/shard_map/ppermute | solution.py:39
  35.5 1.6 collective-permute-start.9
  37.1 2.4 %collective-permute-done.1.refs_1_ = bf16[264,512]{1,0:T(8,128)(2,1)S(1)} collective-permute-done((bf16[264,512]{1,0:T(8,128)(2,1)S(1)}, bf16[264,512]{1,0:T(8,128)(2,1)S(1)}, u32[]{:S(2)}, u32[]{:S(2)}) %collective-permute-start.1) | collective-permute-done | bytes 270368 | tf_op jit(solution)/shard_map/ppermute | solution.py:39
  39.5 3.7 %collective-permute-start.2 = (bf16[264,512]{1,0:T(8,128)(2,1)S(1)}, bf16[264,512]{1,0:T(8,128)(2,1)S(1)}, u32[]{:S(2)}, u32[]{:S(2)}) collective-permute-start(bf16[264,512]{1,0:T(8,128)(2,1)S(1)} %collective-permute-done.1.refs_1_), channel_id=1, source_target_pairs={{0,28},{4,0},{8,4},{12,8},{16,12},{20,16},{24,20},{28,24},{1,29},{... | collective-permute-start | bytes 811016 | tf_op jit(solution)/shard_map/ppermute | solution.py:39
  43.2 1.0 constant_dynamic-slice_fusion
  44.2 1.1 constant_dynamic-slice_fusion.1
  45.4 2.1 collective-permute-done.2.refs_2_
  47.4 3.7 %collective-permute-start.3 = (bf16[264,512]{1,0:T(8,128)(2,1)S(1)}, bf16[264,512]{1,0:T(8,128)(2,1)}, u32[]{:S(2)}, u32[]{:S(2)}) collective-permute-start(bf16[264,512]{1,0:T(8,128)(2,1)S(1)} %collective-permute-done.2.refs_2_), channel_id=1, source_target_pairs={{0,28},{4,0},{8,4},{12,8},{16,12},{20,16},{24,20},{28,24},{1,29},{... | collective-permute-start | bytes 811016 | tf_op jit(solution)/shard_map/ppermute | solution.py:39
  51.1 0.9 pad_maximum_fusion
  52.0 1.6 collective-permute-start.25
  53.6 0.7 copy.15.table_ref
  54.3 0.6 broadcast_in_dim.40.bucket_ref
  54.9 2.5 %position_bias.1.refs_14_ = f32[4,256,256]{2,1,0:T(8,128)} custom-call(s32[8,512]{1,0:T(8,128)} %broadcast_in_dim.40.bucket_ref, f32[32,4]{1,0:T(8,128)} %copy.15.table_ref), custom_call_target="tpu_custom_call" | custom-call | flops 100000000 | bytes 1000000 | tf_op jit(solution)/shard_map/position_bias/pallas_call | solution.py:88
  57.5 3.2 %collective-permute-start.4 = (bf16[264,512]{1,0:T(8,128)(2,1)}, bf16[264,512]{1,0:T(8,128)(2,1)S(1)}, u32[]{:S(2)}, u32[]{:S(2)}) collective-permute-start(bf16[264,512]{1,0:T(8,128)(2,1)} %collective-permute-done.3.refs_3_), channel_id=1, source_target_pairs={{0,28},{4,0},{8,4},{12,8},{16,12},{20,16},{24,20},{28,24},{1,29},{... | collective-permute-start | bytes 811016 | tf_op jit(solution)/shard_map/ppermute | solution.py:39
  60.8 0.6 pad_add_fusion.at_ref
  61.3 4.0 %collective-permute-done.7.refs_5_ = bf16[264,512]{1,0:T(8,128)(2,1)S(1)} collective-permute-done((bf16[264,512]{1,0:T(8,128)(2,1)}, bf16[264,512]{1,0:T(8,128)(2,1)S(1)}, u32[]{:S(2)}, u32[]{:S(2)}) %collective-permute-start.7) | collective-permute-done | bytes 270368 | tf_op jit(solution)/shard_map/ppermute | solution.py:42
  65.4 0.6 copy-done.14
  66.2 12.4 %attention.1 = bf16[8,256,512]{2,1,0:T(8,128)(2,1)} custom-call(s32[16]{0:T(128)} %pad_add_fusion.at_ref, bf16[264,512]{1,0:T(8,128)(2,1)} %copy-done.2, bf16[264,512]{1,0:T(8,128)(2,1)} %copy-done.10, bf16[264,512]{1,0:T(8,128)(2,1)} %copy-done.12, bf16[264,512]{1,0:T(8,128)(2,1)} %collective-permute-done.3.refs_3_, bf16[264,512]{1,0:T(8,128)(2,1)} %copy-done.15, ...), custom_call_target="tpu_custom_call" | custom-call | flops 2147483648 | bytes 10000000 | tf_op jit(solution)/shard_map/attention/pallas_call | solution.py:212
  78.7 1.2 slice_bitcast_fusion.15
  80.0 3.4 %collective-permute-start.14 = (bf16[256,512]{1,0:T(8,128)(2,1)S(1)}, bf16[256,512]{1,0:T(8,128)(2,1)S(1)}, u32[]{:S(2)}, u32[]{:S(2)}) collective-permute-start(bf16[256,512]{1,0:T(8,128)(2,1)S(1)} %get-tuple-element.28), channel_id=1, source_target_pairs={{0,28},{4,0},{8,4},{12,8},{16,12},{20,16},{24,20},{28,24},{1,29},{... | collective-permute-start | bytes 786440 | tf_op jit(solution)/shard_map/ppermute | solution.py:59
  83.4 6.4 %collective-permute-done.10 = bf16[256,512]{1,0:T(8,128)(2,1)S(1)} collective-permute-done((bf16[256,512]{1,0:T(8,128)(2,1)S(1)}, bf16[256,512]{1,0:T(8,128)(2,1)S(1)}, u32[]{:S(2)}, u32[]{:S(2)}) %collective-permute-start.10) | collective-permute-done | bytes 262176 | tf_op jit(solution)/shard_map/ppermute | solution.py:57
  89.8 1.0 fusion.15
  90.9 8.9 %collective-permute-done.11 = bf16[256,512]{1,0:T(8,128)(2,1)S(1)} collective-permute-done((bf16[256,512]{1,0:T(8,128)(2,1)S(1)}, bf16[256,512]{1,0:T(8,128)(2,1)S(1)}, u32[]{:S(2)}, u32[]{:S(2)}) %collective-permute-start.11) | collective-permute-done | bytes 262176 | tf_op jit(solution)/shard_map/ppermute | solution.py:57
  100.1 3.2 %collective-permute-start.15 = (bf16[256,512]{1,0:T(8,128)(2,1)S(1)}, bf16[256,512]{1,0:T(8,128)(2,1)S(1)}, u32[]{:S(2)}, u32[]{:S(2)}) collective-permute-start(bf16[256,512]{1,0:T(8,128)(2,1)S(1)} %get-tuple-element.26), channel_id=1, source_target_pairs={{0,28},{4,0},{8,4},{12,8},{16,12},{20,16},{24,20},{28,24},{1,29},{... | collective-permute-start | bytes 786440 | tf_op jit(solution)/shard_map/ppermute | solution.py:59
  103.3 4.9 %collective-permute-done.12 = bf16[256,512]{1,0:T(8,128)(2,1)S(1)} collective-permute-done((bf16[256,512]{1,0:T(8,128)(2,1)S(1)}, bf16[256,512]{1,0:T(8,128)(2,1)S(1)}, u32[]{:S(2)}, u32[]{:S(2)}) %collective-permute-start.12) | collective-permute-done | bytes 262176 | tf_op jit(solution)/shard_map/ppermute | solution.py:57
  108.4 3.2 %collective-permute-start.16 = (bf16[256,512]{1,0:T(8,128)(2,1)S(1)}, bf16[256,512]{1,0:T(8,128)(2,1)S(1)}, u32[]{:S(2)}, u32[]{:S(2)}) collective-permute-start(bf16[256,512]{1,0:T(8,128)(2,1)S(1)} %get-tuple-element.24), channel_id=1, source_target_pairs={{0,28},{4,0},{8,4},{12,8},{16,12},{20,16},{24,20},{28,24},{1,29},{... | collective-permute-start | bytes 786440 | tf_op jit(solution)/shard_map/ppermute | solution.py:59
  111.6 4.3 %collective-permute-done.13 = bf16[256,512]{1,0:T(8,128)(2,1)S(1)} collective-permute-done((bf16[256,512]{1,0:T(8,128)(2,1)S(1)}, bf16[256,512]{1,0:T(8,128)(2,1)S(1)}, u32[]{:S(2)}, u32[]{:S(2)}) %collective-permute-start.13) | collective-permute-done | bytes 262176 | tf_op jit(solution)/shard_map/ppermute | solution.py:57
  116.1 3.0 %collective-permute-start.17 = (bf16[256,512]{1,0:T(8,128)(2,1)S(1)}, bf16[256,512]{1,0:T(8,128)(2,1)S(1)}, u32[]{:S(2)}, u32[]{:S(2)}) collective-permute-start(bf16[256,512]{1,0:T(8,128)(2,1)S(1)} %fusion.10), channel_id=1, source_target_pairs={{0,2},{2,0},{1,3},{3,1},{4,6},{6,4},{5,7},{7,5},{8,10},{10,8},{9,1... | collective-permute-start | bytes 786440 | tf_op jit(solution)/shard_map/ppermute | solution.py:486
  119.0 5.0 %collective-permute-done.17 = bf16[256,512]{1,0:T(8,128)(2,1)S(1)} collective-permute-done((bf16[256,512]{1,0:T(8,128)(2,1)S(1)}, bf16[256,512]{1,0:T(8,128)(2,1)S(1)}, u32[]{:S(2)}, u32[]{:S(2)}) %collective-permute-start.17) | collective-permute-done | bytes 262176 | tf_op jit(solution)/shard_map/ppermute | solution.py:486
  124.4 3.3 %collective-permute-start.18 = (bf16[264,512]{1,0:T(8,128)(2,1)S(1)}, bf16[264,512]{1,0:T(8,128)(2,1)S(1)}, u32[]{:S(2)}, u32[]{:S(2)}) collective-permute-start(bf16[264,512]{1,0:T(8,128)(2,1)S(1)} %pad_maximum_fusion.3.refs_0_), channel_id=1, source_target_pairs={{0,28},{4,0},{8,4},{12,8},{16,12},{20,16},{24,20},{28,24},{1,29},{... | collective-permute-start | bytes 811016 | tf_op jit(solution)/shard_map/ppermute | solution.py:39
  127.7 6.3 %collective-permute-done.18.refs_1_ = bf16[264,512]{1,0:T(8,128)(2,1)S(1)} collective-permute-done((bf16[264,512]{1,0:T(8,128)(2,1)S(1)}, bf16[264,512]{1,0:T(8,128)(2,1)S(1)}, u32[]{:S(2)}, u32[]{:S(2)}) %collective-permute-start.18) | collective-permute-done | bytes 270368 | tf_op jit(solution)/shard_map/ppermute | solution.py:39
  134.0 3.7 %collective-permute-start.19 = (bf16[264,512]{1,0:T(8,128)(2,1)S(1)}, bf16[264,512]{1,0:T(8,128)(2,1)S(1)}, u32[]{:S(2)}, u32[]{:S(2)}) collective-permute-start(bf16[264,512]{1,0:T(8,128)(2,1)S(1)} %collective-permute-done.18.refs_1_), channel_id=1, source_target_pairs={{0,28},{4,0},{8,4},{12,8},{16,12},{20,16},{24,20},{28,24},{1,29},{... | collective-permute-start | bytes 811016 | tf_op jit(solution)/shard_map/ppermute | solution.py:39
  137.7 6.3 %collective-permute-done.19.refs_3_ = bf16[264,512]{1,0:T(8,128)(2,1)S(1)} collective-permute-done((bf16[264,512]{1,0:T(8,128)(2,1)S(1)}, bf16[264,512]{1,0:T(8,128)(2,1)S(1)}, u32[]{:S(2)}, u32[]{:S(2)}) %collective-permute-start.19) | collective-permute-done | bytes 270368 | tf_op jit(solution)/shard_map/ppermute | solution.py:39
  144.0 3.7 %collective-permute-start.20 = (bf16[264,512]{1,0:T(8,128)(2,1)S(1)}, bf16[264,512]{1,0:T(8,128)(2,1)S(1)}, u32[]{:S(2)}, u32[]{:S(2)}) collective-permute-start(bf16[264,512]{1,0:T(8,128)(2,1)S(1)} %collective-permute-done.19.refs_3_), channel_id=1, source_target_pairs={{0,28},{4,0},{8,4},{12,8},{16,12},{20,16},{24,20},{28,24},{1,29},{... | collective-permute-start | bytes 811016 | tf_op jit(solution)/shard_map/ppermute | solution.py:39
  148.2 3.5 %collective-permute-done.20.refs_0_ = bf16[264,512]{1,0:T(8,128)(2,1)S(1)} collective-permute-done((bf16[264,512]{1,0:T(8,128)(2,1)S(1)}, bf16[264,512]{1,0:T(8,128)(2,1)S(1)}, u32[]{:S(2)}, u32[]{:S(2)}) %collective-permute-start.20) | collective-permute-done | bytes 270368 | tf_op jit(solution)/shard_map/ppermute | solution.py:39
  151.6 3.7 %collective-permute-start.24 = (bf16[264,512]{1,0:T(8,128)(2,1)S(1)}, bf16[264,512]{1,0:T(8,128)(2,1)S(1)}, u32[]{:S(2)}, u32[]{:S(2)}) collective-permute-start(bf16[264,512]{1,0:T(8,128)(2,1)S(1)} %collective-permute-done.20.refs_0_), channel_id=1, source_target_pairs={{0,28},{4,0},{8,4},{12,8},{16,12},{20,16},{24,20},{28,24},{1,29},{... | collective-permute-start | bytes 811016 | tf_op jit(solution)/shard_map/ppermute | solution.py:39
  155.9 7.0 %gate_early.1 = (f32[256,1024]{1,0:T(8,128)}, f32[8,256]{1,0:T(8,128)}) custom-call(s32[5]{0:T(128)} %and_select_fusion.at_ref, bf16[264,512]{1,0:T(8,128)(2,1)} %copy-done.1, bf16[264,512]{1,0:T(8,128)(2,1)} %copy-done.6, bf16[264,512]{1,0:T(8,128)(2,1)} %copy-done.7, bf16[264,512]{1,0:T(8,128)(2,1)} %copy-done.8, bf16[264,512]{1,0:T(8,128)(2,1)} %copy-done.9, ...), custom_call_target="tpu_custom_call" | custom-call | flops 1342177280 | bytes 5000000 | tf_op jit(solution)/shard_map/gate_early/pallas_call | solution.py:370
  162.9 0.7 copy-done.16
  163.7 10.1 %gate_late_and_down.1 = bf16[8,256,512]{2,1,0:T(8,128)(2,1)} custom-call(s32[11]{0:T(128)} %and_select_fusion.1.at_ref, bf16[264,512]{1,0:T(8,128)(2,1)} %copy-done.13, bf16[264,512]{1,0:T(8,128)(2,1)} %copy-done.16, bf16[264,512]{1,0:T(8,128)(2,1)} %copy-done.17, bf16[4096,256]{1,0:T(8,128)(2,1)} %refs_3_.1, bf16[4096,256]{1,0:T(8,128)(2,1)} %refs_4_.1, ...), custom_call_target="tpu_custom_call" | custom-call | flops 1879048192 | bytes 7000000 | tf_op jit(solution)/shard_map/gate_late_and_down/pallas_call | solution.py:385
  173.8 1.1 slice_bitcast_fusion.7
  175.2 3.2 %collective-permute-start.30 = (bf16[256,512]{1,0:T(8,128)(2,1)S(1)}, bf16[256,512]{1,0:T(8,128)(2,1)S(1)}, u32[]{:S(2)}, u32[]{:S(2)}) collective-permute-start(bf16[256,512]{1,0:T(8,128)(2,1)S(1)} %get-tuple-element.22), channel_id=1, source_target_pairs={{0,28},{4,0},{8,4},{12,8},{16,12},{20,16},{24,20},{28,24},{1,29},{... | collective-permute-start | bytes 786440 | tf_op jit(solution)/shard_map/ppermute | solution.py:59
  178.5 4.3 %collective-permute-done.26 = bf16[256,512]{1,0:T(8,128)(2,1)S(1)} collective-permute-done((bf16[256,512]{1,0:T(8,128)(2,1)S(1)}, bf16[256,512]{1,0:T(8,128)(2,1)S(1)}, u32[]{:S(2)}, u32[]{:S(2)}) %collective-permute-start.26) | collective-permute-done | bytes 262176 | tf_op jit(solution)/shard_map/ppermute | solution.py:57
  182.8 1.0 fusion.9
  183.9 7.6 %collective-permute-done.27 = bf16[256,512]{1,0:T(8,128)(2,1)S(1)} collective-permute-done((bf16[256,512]{1,0:T(8,128)(2,1)S(1)}, bf16[256,512]{1,0:T(8,128)(2,1)S(1)}, u32[]{:S(2)}, u32[]{:S(2)}) %collective-permute-start.27) | collective-permute-done | bytes 262176 | tf_op jit(solution)/shard_map/ppermute | solution.py:57
  191.5 1.2 fusion.8
  192.7 3.2 %collective-permute-start.31 = (bf16[256,512]{1,0:T(8,128)(2,1)S(1)}, bf16[256,512]{1,0:T(8,128)(2,1)S(1)}, u32[]{:S(2)}, u32[]{:S(2)}) collective-permute-start(bf16[256,512]{1,0:T(8,128)(2,1)S(1)} %get-tuple-element.20), channel_id=1, source_target_pairs={{0,28},{4,0},{8,4},{12,8},{16,12},{20,16},{24,20},{28,24},{1,29},{... | collective-permute-start | bytes 786440 | tf_op jit(solution)/shard_map/ppermute | solution.py:59
  196.0 4.3 %collective-permute-done.28 = bf16[256,512]{1,0:T(8,128)(2,1)S(1)} collective-permute-done((bf16[256,512]{1,0:T(8,128)(2,1)S(1)}, bf16[256,512]{1,0:T(8,128)(2,1)S(1)}, u32[]{:S(2)}, u32[]{:S(2)}) %collective-permute-start.28) | collective-permute-done | bytes 262176 | tf_op jit(solution)/shard_map/ppermute | solution.py:57
  200.3 1.2 fusion.7
  201.6 3.3 %collective-permute-start.32 = (bf16[256,512]{1,0:T(8,128)(2,1)S(1)}, bf16[256,512]{1,0:T(8,128)(2,1)S(1)}, u32[]{:S(2)}, u32[]{:S(2)}) collective-permute-start(bf16[256,512]{1,0:T(8,128)(2,1)S(1)} %get-tuple-element.18), channel_id=1, source_target_pairs={{0,28},{4,0},{8,4},{12,8},{16,12},{20,16},{24,20},{28,24},{1,29},{... | collective-permute-start | bytes 786440 | tf_op jit(solution)/shard_map/ppermute | solution.py:59
  204.9 4.3 %collective-permute-done.29 = bf16[256,512]{1,0:T(8,128)(2,1)S(1)} collective-permute-done((bf16[256,512]{1,0:T(8,128)(2,1)S(1)}, bf16[256,512]{1,0:T(8,128)(2,1)S(1)}, u32[]{:S(2)}, u32[]{:S(2)}) %collective-permute-start.29) | collective-permute-done | bytes 262176 | tf_op jit(solution)/shard_map/ppermute | solution.py:57
  209.1 1.0 convert_add_fusion.1
  210.2 3.0 %collective-permute-start.33 = (bf16[256,256]{1,0:T(8,128)(2,1)S(1)}, bf16[256,256]{1,0:T(8,128)(2,1)S(1)}, u32[]{:S(2)}, u32[]{:S(2)}) collective-permute-start(bf16[256,256]{1,0:T(8,128)(2,1)S(1)} %select_convert_fusion), channel_id=1, source_target_pairs={{0,2},{2,0},{1,3},{3,1},{4,6},{6,4},{5,7},{7,5},{8,10},{10,8},{9,1... | collective-permute-start | bytes 393224 | tf_op jit(solution)/shard_map/ppermute | solution.py:499
  213.2 3.6 %collective-permute-done.33 = bf16[256,256]{1,0:T(8,128)(2,1)S(1)} collective-permute-done((bf16[256,256]{1,0:T(8,128)(2,1)S(1)}, bf16[256,256]{1,0:T(8,128)(2,1)S(1)}, u32[]{:S(2)}, u32[]{:S(2)}) %collective-permute-start.33) | collective-permute-done | bytes 131104 | tf_op jit(solution)/shard_map/ppermute | solution.py:499
  216.8 0.7 fusion.16
  (98 shorter events, 3.6 us)
Async XLA Ops:
  6.5 22.7 %copy-start.4 = (bf16[1,256,256]{2,1,0:T(8,128)(2,1)S(1)}, bf16[1,256,256]{2,1,0:T(8,128)(2,1)}, u32[]{:S(2)}) copy-start(bf16[1,256,256]{2,1,0:T(8,128)(2,1)} %param.14) | copy-start | bytes 393220
  6.5 29.0 %copy-start.3 = (bf16[256,2048]{1,0:T(8,128)(2,1)S(1)}, bf16[256,2048]{1,0:T(8,128)(2,1)}, u32[]{:S(2)}) copy-start(bf16[256,2048]{1,0:T(8,128)(2,1)} %refs_12_.1) | copy-start | bytes 3145732
  6.5 58.9 %all-gather.4.cloned.1.call-start = ((), (), s32[]{:S(2)}) async-start(), calls=%async_computation | async-start | bytes 3538944 | tf_op jit(solution)/shard_map/all_gather | solution.py:452
  8.6 10.9 %collective-permute-start.8 = (bf16[256,768]{1,0:T(8,128)(2,1)S(1)}, bf16[256,768]{1,0:T(8,128)(2,1)S(1)}, u32[]{:S(2)}, u32[]{:S(2)}) collective-permute-start(bf16[256,768]{1,0:T(8,128)(2,1)S(1)} %pad_maximum_fusion.1), channel_id=1, source_target_pairs={{0,1},{1,0},{2,3},{3,2},{4,5},{5,4},{6,7},{7,6},{8,9},{9,8},{10,11... | collective-permute-start | bytes 1179656 | tf_op jit(solution)/shard_map/ppermute | solution.py:451
  19.5 0.8 copy-start.5
  20.3 135.6 %all-gather.6.cloned.1.call-start = ((), (), s32[]{:S(2)}) async-start(), calls=%async_computation.1 | async-start | bytes 7077888 | tf_op jit(solution)/shard_map/all_gather | solution.py:484
  22.6 6.6 %collective-permute-start = (bf16[264,256]{1,0:T(8,128)(2,1)S(1)}, bf16[264,256]{1,0:T(8,128)(2,1)S(1)}, u32[]{:S(2)}, u32[]{:S(2)}) collective-permute-start(bf16[264,256]{1,0:T(8,128)(2,1)S(1)} %pad_maximum_fusion.4), channel_id=1, source_target_pairs={{0,2},{2,0},{1,3},{3,1},{4,6},{6,4},{5,7},{7,5},{8,10},{10,8},{9,1... | collective-permute-start | bytes 405512 | tf_op jit(solution)/shard_map/ppermute | solution.py:443
  29.3 24.3 %copy-start.18 = (f32[32,4]{0,1:T(4,128)S(1)}, f32[32,4]{0,1:T(4,128)}, u32[]{:S(2)}) copy-start(f32[32,4]{0,1:T(4,128)} %param.20) | copy-start | bytes 1540
  29.6 27.8 %copy-start.2 = (bf16[264,512]{1,0:T(8,128)(2,1)}, bf16[264,512]{1,0:T(8,128)(2,1)S(1)}, u32[]{:S(2)}) copy-start(bf16[264,512]{1,0:T(8,128)(2,1)S(1)} %pad_maximum_fusion.2.refs_0_) | copy-start | bytes 811012
  29.6 9.9 %collective-permute-start.1 = (bf16[264,512]{1,0:T(8,128)(2,1)S(1)}, bf16[264,512]{1,0:T(8,128)(2,1)S(1)}, u32[]{:S(2)}, u32[]{:S(2)}) collective-permute-start(bf16[264,512]{1,0:T(8,128)(2,1)S(1)} %pad_maximum_fusion.2.refs_0_), channel_id=1, source_target_pairs={{0,28},{4,0},{8,4},{12,8},{16,12},{20,16},{24,20},{28,24},{1,29},{... | collective-permute-start | bytes 811016 | tf_op jit(solution)/shard_map/ppermute | solution.py:39
  35.5 29.9 %collective-permute-start.9 = (bf16[256,2048]{1,0:T(8,128)(2,1)S(1)}, bf16[256,2048]{1,0:T(8,128)(2,1)}, u32[]{:S(2)}, u32[]{:S(2)}) collective-permute-start(bf16[256,2048]{1,0:T(8,128)(2,1)S(1)} %copy-done.3), channel_id=1, source_target_pairs={{0,1},{1,0},{2,3},{3,2},{4,5},{5,4},{6,7},{7,6},{8,9},{9,8},{10,11... | collective-permute-start | bytes 3145736 | tf_op jit(solution)/shard_map/ppermute | solution.py:453
  37.1 8.2 %collective-permute-start.5 = (bf16[264,512]{1,0:T(8,128)(2,1)S(1)}, bf16[264,512]{1,0:T(8,128)(2,1)S(1)}, u32[]{:S(2)}, u32[]{:S(2)}) collective-permute-start(bf16[264,512]{1,0:T(8,128)(2,1)S(1)} %pad_maximum_fusion.2.refs_0_), channel_id=1, source_target_pairs={{0,4},{4,8},{8,12},{12,16},{16,20},{20,24},{24,28},{28,0},{1,5},{5... | collective-permute-start | bytes 811016 | tf_op jit(solution)/shard_map/ppermute | solution.py:42
  39.5 17.9 %copy-start.10 = (bf16[264,512]{1,0:T(8,128)(2,1)}, bf16[264,512]{1,0:T(8,128)(2,1)S(1)}, u32[]{:S(2)}) copy-start(bf16[264,512]{1,0:T(8,128)(2,1)S(1)} %collective-permute-done.1.refs_1_) | copy-start | bytes 811012
  39.5 7.9 %collective-permute-start.2 = (bf16[264,512]{1,0:T(8,128)(2,1)S(1)}, bf16[264,512]{1,0:T(8,128)(2,1)S(1)}, u32[]{:S(2)}, u32[]{:S(2)}) collective-permute-start(bf16[264,512]{1,0:T(8,128)(2,1)S(1)} %collective-permute-done.1.refs_1_), channel_id=1, source_target_pairs={{0,28},{4,0},{8,4},{12,8},{16,12},{20,16},{24,20},{28,24},{1,29},{... | collective-permute-start | bytes 811016 | tf_op jit(solution)/shard_map/ppermute | solution.py:39
  43.2 17.6 %copy-start.19 = (s32[8]{0:T(128)S(1)}, s32[8]{0:T(128)}, u32[]{:S(2)}) copy-start(s32[8]{0:T(128)} %constant.111.clone) | copy-start | bytes 100
  45.3 20.2 %copy-start.11 = (bf16[264,512]{1,0:T(8,128)(2,1)}, bf16[264,512]{1,0:T(8,128)(2,1)S(1)}, u32[]{:S(2)}) copy-start(bf16[264,512]{1,0:T(8,128)(2,1)S(1)} %collective-permute-done.5.refs_7_) | copy-start | bytes 811012
  45.3 12.2 %collective-permute-start.6 = (bf16[264,512]{1,0:T(8,128)(2,1)S(1)}, bf16[264,512]{1,0:T(8,128)(2,1)}, u32[]{:S(2)}, u32[]{:S(2)}) collective-permute-start(bf16[264,512]{1,0:T(8,128)(2,1)S(1)} %collective-permute-done.5.refs_7_), channel_id=1, source_target_pairs={{0,4},{4,8},{8,12},{12,16},{16,20},{20,24},{24,28},{28,0},{1,5},{5... | collective-permute-start | bytes 811016 | tf_op jit(solution)/shard_map/ppermute | solution.py:42
  47.4 18.0 %copy-start.12 = (bf16[264,512]{1,0:T(8,128)(2,1)}, bf16[264,512]{1,0:T(8,128)(2,1)S(1)}, u32[]{:S(2)}) copy-start(bf16[264,512]{1,0:T(8,128)(2,1)S(1)} %collective-permute-done.2.refs_2_) | copy-start | bytes 811012
  47.4 10.1 %collective-permute-start.3 = (bf16[264,512]{1,0:T(8,128)(2,1)S(1)}, bf16[264,512]{1,0:T(8,128)(2,1)}, u32[]{:S(2)}, u32[]{:S(2)}) collective-permute-start(bf16[264,512]{1,0:T(8,128)(2,1)S(1)} %collective-permute-done.2.refs_2_), channel_id=1, source_target_pairs={{0,28},{4,0},{8,4},{12,8},{16,12},{20,16},{24,20},{28,24},{1,29},{... | collective-permute-start | bytes 811016 | tf_op jit(solution)/shard_map/ppermute | solution.py:39
  52.0 26.6 %collective-permute-start.25 = (bf16[768,512]{1,0:T(8,128)(2,1)}, bf16[768,512]{1,0:T(8,128)(2,1)}, u32[]{:S(2)}, u32[]{:S(2)}) collective-permute-start(bf16[768,512]{1,0:T(8,128)(2,1)} %pad_maximum_fusion), channel_id=1, source_target_pairs={{0,1},{1,0},{2,3},{3,2},{4,5},{5,4},{6,7},{7,6},{8,9},{9,8},{10,11... | collective-permute-start | bytes 2359304 | tf_op jit(solution)/shard_map/ppermute | solution.py:472
  57.4 8.0 %collective-permute-start.7 = (bf16[264,512]{1,0:T(8,128)(2,1)}, bf16[264,512]{1,0:T(8,128)(2,1)S(1)}, u32[]{:S(2)}, u32[]{:S(2)}) collective-permute-start(bf16[264,512]{1,0:T(8,128)(2,1)} %collective-permute-done.6.refs_6_), channel_id=1, source_target_pairs={{0,4},{4,8},{8,12},{12,16},{16,20},{20,24},{24,28},{28,0},{1,5},{5... | collective-permute-start | bytes 811016 | tf_op jit(solution)/shard_map/ppermute | solution.py:42
  57.5 7.9 %collective-permute-start.4 = (bf16[264,512]{1,0:T(8,128)(2,1)}, bf16[264,512]{1,0:T(8,128)(2,1)S(1)}, u32[]{:S(2)}, u32[]{:S(2)}) collective-permute-start(bf16[264,512]{1,0:T(8,128)(2,1)} %collective-permute-done.3.refs_3_), channel_id=1, source_target_pairs={{0,28},{4,0},{8,4},{12,8},{16,12},{20,16},{24,20},{28,24},{1,29},{... | collective-permute-start | bytes 811016 | tf_op jit(solution)/shard_map/ppermute | solution.py:39
  65.4 0.7 copy-start.14
  65.4 0.8 copy-start.15
  78.6 21.2 %copy-start = (bf16[8,256,512]{2,1,0:T(8,128)(2,1)S(1)}, bf16[8,256,512]{2,1,0:T(8,128)(2,1)}, u32[]{:S(2)}) copy-start(bf16[8,256,512]{2,1,0:T(8,128)(2,1)} %attention.1) | copy-start | bytes 6291460
  79.9 9.9 %collective-permute-start.10 = (bf16[256,512]{1,0:T(8,128)(2,1)S(1)}, bf16[256,512]{1,0:T(8,128)(2,1)S(1)}, u32[]{:S(2)}, u32[]{:S(2)}) collective-permute-start(bf16[256,512]{1,0:T(8,128)(2,1)S(1)} %get-tuple-element.27), channel_id=1, source_target_pairs={{0,4},{4,8},{8,12},{12,16},{16,20},{20,24},{24,28},{28,0},{1,5},{5... | collective-permute-start | bytes 786440 | tf_op jit(solution)/shard_map/ppermute | solution.py:57
  80.0 11.0 %collective-permute-start.14 = (bf16[256,512]{1,0:T(8,128)(2,1)S(1)}, bf16[256,512]{1,0:T(8,128)(2,1)S(1)}, u32[]{:S(2)}, u32[]{:S(2)}) collective-permute-start(bf16[256,512]{1,0:T(8,128)(2,1)S(1)} %get-tuple-element.28), channel_id=1, source_target_pairs={{0,28},{4,0},{8,4},{12,8},{16,12},{20,16},{24,20},{28,24},{1,29},{... | collective-permute-start | bytes 786440 | tf_op jit(solution)/shard_map/ppermute | solution.py:59
  90.8 9.0 %collective-permute-start.11 = (bf16[256,512]{1,0:T(8,128)(2,1)S(1)}, bf16[256,512]{1,0:T(8,128)(2,1)S(1)}, u32[]{:S(2)}, u32[]{:S(2)}) collective-permute-start(bf16[256,512]{1,0:T(8,128)(2,1)S(1)} %fusion.15), channel_id=1, source_target_pairs={{0,4},{4,8},{8,12},{12,16},{16,20},{20,24},{24,28},{28,0},{1,5},{5... | collective-permute-start | bytes 786440 | tf_op jit(solution)/shard_map/ppermute | solution.py:57
  99.9 8.2 %collective-permute-start.12 = (bf16[256,512]{1,0:T(8,128)(2,1)S(1)}, bf16[256,512]{1,0:T(8,128)(2,1)S(1)}, u32[]{:S(2)}, u32[]{:S(2)}) collective-permute-start(bf16[256,512]{1,0:T(8,128)(2,1)S(1)} %get-tuple-element.25), channel_id=1, source_target_pairs={{0,4},{4,8},{8,12},{12,16},{16,20},{20,24},{24,28},{28,0},{1,5},{5... | collective-permute-start | bytes 786440 | tf_op jit(solution)/shard_map/ppermute | solution.py:57
  100.0 47.6 %copy-start.21 = (s32[5]{0:T(128)S(1)}, s32[5]{0:T(128)}, u32[]{:S(2)}) copy-start(s32[5]{0:T(128)} %constant.112.clone) | copy-start | bytes 64
  100.0 55.3 %copy-start.20 = (s32[11]{0:T(128)S(1)}, s32[11]{0:T(128)}, u32[]{:S(2)}) copy-start(s32[11]{0:T(128)} %constant.113.clone) | copy-start | bytes 136
  100.1 8.1 %collective-permute-start.15 = (bf16[256,512]{1,0:T(8,128)(2,1)S(1)}, bf16[256,512]{1,0:T(8,128)(2,1)S(1)}, u32[]{:S(2)}, u32[]{:S(2)}) collective-permute-start(bf16[256,512]{1,0:T(8,128)(2,1)S(1)} %get-tuple-element.26), channel_id=1, source_target_pairs={{0,28},{4,0},{8,4},{12,8},{16,12},{20,16},{24,20},{28,24},{1,29},{... | collective-permute-start | bytes 786440 | tf_op jit(solution)/shard_map/ppermute | solution.py:59
  108.3 7.7 %collective-permute-start.13 = (bf16[256,512]{1,0:T(8,128)(2,1)S(1)}, bf16[256,512]{1,0:T(8,128)(2,1)S(1)}, u32[]{:S(2)}, u32[]{:S(2)}) collective-permute-start(bf16[256,512]{1,0:T(8,128)(2,1)S(1)} %get-tuple-element.23), channel_id=1, source_target_pairs={{0,4},{4,8},{8,12},{12,16},{16,20},{20,24},{24,28},{28,0},{1,5},{5... | collective-permute-start | bytes 786440 | tf_op jit(solution)/shard_map/ppermute | solution.py:57
  108.4 7.6 %collective-permute-start.16 = (bf16[256,512]{1,0:T(8,128)(2,1)S(1)}, bf16[256,512]{1,0:T(8,128)(2,1)S(1)}, u32[]{:S(2)}, u32[]{:S(2)}) collective-permute-start(bf16[256,512]{1,0:T(8,128)(2,1)S(1)} %get-tuple-element.24), channel_id=1, source_target_pairs={{0,28},{4,0},{8,4},{12,8},{16,12},{20,16},{24,20},{28,24},{1,29},{... | collective-permute-start | bytes 786440 | tf_op jit(solution)/shard_map/ppermute | solution.py:59
  116.1 8.0 %collective-permute-start.17 = (bf16[256,512]{1,0:T(8,128)(2,1)S(1)}, bf16[256,512]{1,0:T(8,128)(2,1)S(1)}, u32[]{:S(2)}, u32[]{:S(2)}) collective-permute-start(bf16[256,512]{1,0:T(8,128)(2,1)S(1)} %fusion.10), channel_id=1, source_target_pairs={{0,2},{2,0},{1,3},{3,1},{4,6},{6,4},{5,7},{7,5},{8,10},{10,8},{9,1... | collective-permute-start | bytes 786440 | tf_op jit(solution)/shard_map/ppermute | solution.py:486
  124.3 31.5 %copy-start.1 = (bf16[264,512]{1,0:T(8,128)(2,1)}, bf16[264,512]{1,0:T(8,128)(2,1)S(1)}, u32[]{:S(2)}) copy-start(bf16[264,512]{1,0:T(8,128)(2,1)S(1)} %pad_maximum_fusion.3.refs_0_) | copy-start | bytes 811012
  124.4 9.6 %collective-permute-start.18 = (bf16[264,512]{1,0:T(8,128)(2,1)S(1)}, bf16[264,512]{1,0:T(8,128)(2,1)S(1)}, u32[]{:S(2)}, u32[]{:S(2)}) collective-permute-start(bf16[264,512]{1,0:T(8,128)(2,1)S(1)} %pad_maximum_fusion.3.refs_0_), channel_id=1, source_target_pairs={{0,28},{4,0},{8,4},{12,8},{16,12},{20,16},{24,20},{28,24},{1,29},{... | collective-permute-start | bytes 811016 | tf_op jit(solution)/shard_map/ppermute | solution.py:39
  127.7 10.0 %collective-permute-start.21 = (bf16[264,512]{1,0:T(8,128)(2,1)S(1)}, bf16[264,512]{1,0:T(8,128)(2,1)S(1)}, u32[]{:S(2)}, u32[]{:S(2)}) collective-permute-start(bf16[264,512]{1,0:T(8,128)(2,1)S(1)} %pad_maximum_fusion.3.refs_0_), channel_id=1, source_target_pairs={{0,4},{4,8},{8,12},{12,16},{16,20},{20,24},{24,28},{28,0},{1,5},{5... | collective-permute-start | bytes 811016 | tf_op jit(solution)/shard_map/ppermute | solution.py:42
  134.0 21.9 %copy-start.6 = (bf16[264,512]{1,0:T(8,128)(2,1)}, bf16[264,512]{1,0:T(8,128)(2,1)S(1)}, u32[]{:S(2)}) copy-start(bf16[264,512]{1,0:T(8,128)(2,1)S(1)} %collective-permute-done.18.refs_1_) | copy-start | bytes 811012
  134.0 10.0 %collective-permute-start.19 = (bf16[264,512]{1,0:T(8,128)(2,1)S(1)}, bf16[264,512]{1,0:T(8,128)(2,1)S(1)}, u32[]{:S(2)}, u32[]{:S(2)}) collective-permute-start(bf16[264,512]{1,0:T(8,128)(2,1)S(1)} %collective-permute-done.18.refs_1_), channel_id=1, source_target_pairs={{0,28},{4,0},{8,4},{12,8},{16,12},{20,16},{24,20},{28,24},{1,29},{... | collective-permute-start | bytes 811016 | tf_op jit(solution)/shard_map/ppermute | solution.py:39
  137.7 18.2 %copy-start.7 = (bf16[264,512]{1,0:T(8,128)(2,1)}, bf16[264,512]{1,0:T(8,128)(2,1)S(1)}, u32[]{:S(2)}) copy-start(bf16[264,512]{1,0:T(8,128)(2,1)S(1)} %collective-permute-done.21.refs_2_) | copy-start | bytes 811012
  137.7 10.5 %collective-permute-start.22 = (bf16[264,512]{1,0:T(8,128)(2,1)S(1)}, bf16[264,512]{1,0:T(8,128)(2,1)S(1)}, u32[]{:S(2)}, u32[]{:S(2)}) collective-permute-start(bf16[264,512]{1,0:T(8,128)(2,1)S(1)} %collective-permute-done.21.refs_2_), channel_id=1, source_target_pairs={{0,4},{4,8},{8,12},{12,16},{16,20},{20,24},{24,28},{28,0},{1,5},{5... | collective-permute-start | bytes 811016 | tf_op jit(solution)/shard_map/ppermute | solution.py:42
  144.0 11.9 %copy-start.8 = (bf16[264,512]{1,0:T(8,128)(2,1)}, bf16[264,512]{1,0:T(8,128)(2,1)S(1)}, u32[]{:S(2)}) copy-start(bf16[264,512]{1,0:T(8,128)(2,1)S(1)} %collective-permute-done.19.refs_3_) | copy-start | bytes 811012
  144.0 7.7 %collective-permute-start.20 = (bf16[264,512]{1,0:T(8,128)(2,1)S(1)}, bf16[264,512]{1,0:T(8,128)(2,1)S(1)}, u32[]{:S(2)}, u32[]{:S(2)}) collective-permute-start(bf16[264,512]{1,0:T(8,128)(2,1)S(1)} %collective-permute-done.19.refs_3_), channel_id=1, source_target_pairs={{0,28},{4,0},{8,4},{12,8},{16,12},{20,16},{24,20},{28,24},{1,29},{... | collective-permute-start | bytes 811016 | tf_op jit(solution)/shard_map/ppermute | solution.py:39
  148.2 7.7 %copy-start.9 = (bf16[264,512]{1,0:T(8,128)(2,1)}, bf16[264,512]{1,0:T(8,128)(2,1)S(1)}, u32[]{:S(2)}) copy-start(bf16[264,512]{1,0:T(8,128)(2,1)S(1)} %collective-permute-done.22.refs_4_) | copy-start | bytes 811012
  148.2 14.7 %collective-permute-start.23 = (bf16[264,512]{1,0:T(8,128)(2,1)S(1)}, bf16[264,512]{1,0:T(8,128)(2,1)S(1)}, u32[]{:S(2)}, u32[]{:S(2)}) collective-permute-start(bf16[264,512]{1,0:T(8,128)(2,1)S(1)} %collective-permute-done.22.refs_4_), channel_id=1, source_target_pairs={{0,4},{4,8},{8,12},{12,16},{16,20},{20,24},{24,28},{28,0},{1,5},{5... | collective-permute-start | bytes 811016 | tf_op jit(solution)/shard_map/ppermute | solution.py:42
  151.6 11.3 %copy-start.13 = (bf16[264,512]{1,0:T(8,128)(2,1)}, bf16[264,512]{1,0:T(8,128)(2,1)S(1)}, u32[]{:S(2)}) copy-start(bf16[264,512]{1,0:T(8,128)(2,1)S(1)} %collective-permute-done.20.refs_0_) | copy-start | bytes 811012
  151.6 11.3 %collective-permute-start.24 = (bf16[264,512]{1,0:T(8,128)(2,1)S(1)}, bf16[264,512]{1,0:T(8,128)(2,1)S(1)}, u32[]{:S(2)}, u32[]{:S(2)}) collective-permute-start(bf16[264,512]{1,0:T(8,128)(2,1)S(1)} %collective-permute-done.20.refs_0_), channel_id=1, source_target_pairs={{0,28},{4,0},{8,4},{12,8},{16,12},{20,16},{24,20},{28,24},{1,29},{... | collective-permute-start | bytes 811016 | tf_op jit(solution)/shard_map/ppermute | solution.py:39
  162.9 0.7 copy-start.16
  162.9 0.8 copy-start.17
  174.9 7.9 %collective-permute-start.26 = (bf16[256,512]{1,0:T(8,128)(2,1)S(1)}, bf16[256,512]{1,0:T(8,128)(2,1)S(1)}, u32[]{:S(2)}, u32[]{:S(2)}) collective-permute-start(bf16[256,512]{1,0:T(8,128)(2,1)S(1)} %get-tuple-element.21), channel_id=1, source_target_pairs={{0,4},{4,8},{8,12},{12,16},{16,20},{20,24},{24,28},{28,0},{1,5},{5... | collective-permute-start | bytes 786440 | tf_op jit(solution)/shard_map/ppermute | solution.py:57
  175.2 8.7 %collective-permute-start.30 = (bf16[256,512]{1,0:T(8,128)(2,1)S(1)}, bf16[256,512]{1,0:T(8,128)(2,1)S(1)}, u32[]{:S(2)}, u32[]{:S(2)}) collective-permute-start(bf16[256,512]{1,0:T(8,128)(2,1)S(1)} %get-tuple-element.22), channel_id=1, source_target_pairs={{0,28},{4,0},{8,4},{12,8},{16,12},{20,16},{24,20},{28,24},{1,29},{... | collective-permute-start | bytes 786440 | tf_op jit(solution)/shard_map/ppermute | solution.py:59
  183.8 7.7 %collective-permute-start.27 = (bf16[256,512]{1,0:T(8,128)(2,1)S(1)}, bf16[256,512]{1,0:T(8,128)(2,1)S(1)}, u32[]{:S(2)}, u32[]{:S(2)}) collective-permute-start(bf16[256,512]{1,0:T(8,128)(2,1)S(1)} %fusion.9), channel_id=1, source_target_pairs={{0,4},{4,8},{8,12},{12,16},{16,20},{20,24},{24,28},{28,0},{1,5},{5... | collective-permute-start | bytes 786440 | tf_op jit(solution)/shard_map/ppermute | solution.py:57
  192.6 7.7 %collective-permute-start.28 = (bf16[256,512]{1,0:T(8,128)(2,1)S(1)}, bf16[256,512]{1,0:T(8,128)(2,1)S(1)}, u32[]{:S(2)}, u32[]{:S(2)}) collective-permute-start(bf16[256,512]{1,0:T(8,128)(2,1)S(1)} %get-tuple-element.19), channel_id=1, source_target_pairs={{0,4},{4,8},{8,12},{12,16},{16,20},{20,24},{24,28},{28,0},{1,5},{5... | collective-permute-start | bytes 786440 | tf_op jit(solution)/shard_map/ppermute | solution.py:57
  192.7 7.6 %collective-permute-start.31 = (bf16[256,512]{1,0:T(8,128)(2,1)S(1)}, bf16[256,512]{1,0:T(8,128)(2,1)S(1)}, u32[]{:S(2)}, u32[]{:S(2)}) collective-permute-start(bf16[256,512]{1,0:T(8,128)(2,1)S(1)} %get-tuple-element.20), channel_id=1, source_target_pairs={{0,28},{4,0},{8,4},{12,8},{16,12},{20,16},{24,20},{28,24},{1,29},{... | collective-permute-start | bytes 786440 | tf_op jit(solution)/shard_map/ppermute | solution.py:59
  201.5 7.7 %collective-permute-start.29 = (bf16[256,512]{1,0:T(8,128)(2,1)S(1)}, bf16[256,512]{1,0:T(8,128)(2,1)S(1)}, u32[]{:S(2)}, u32[]{:S(2)}) collective-permute-start(bf16[256,512]{1,0:T(8,128)(2,1)S(1)} %get-tuple-element.17), channel_id=1, source_target_pairs={{0,4},{4,8},{8,12},{12,16},{16,20},{20,24},{24,28},{28,0},{1,5},{5... | collective-permute-start | bytes 786440 | tf_op jit(solution)/shard_map/ppermute | solution.py:57
  201.6 7.6 %collective-permute-start.32 = (bf16[256,512]{1,0:T(8,128)(2,1)S(1)}, bf16[256,512]{1,0:T(8,128)(2,1)S(1)}, u32[]{:S(2)}, u32[]{:S(2)}) collective-permute-start(bf16[256,512]{1,0:T(8,128)(2,1)S(1)} %get-tuple-element.18), channel_id=1, source_target_pairs={{0,28},{4,0},{8,4},{12,8},{16,12},{20,16},{24,20},{28,24},{1,29},{... | collective-permute-start | bytes 786440 | tf_op jit(solution)/shard_map/ppermute | solution.py:59
  210.2 6.6 %collective-permute-start.33 = (bf16[256,256]{1,0:T(8,128)(2,1)S(1)}, bf16[256,256]{1,0:T(8,128)(2,1)S(1)}, u32[]{:S(2)}, u32[]{:S(2)}) collective-permute-start(bf16[256,256]{1,0:T(8,128)(2,1)S(1)} %select_convert_fusion), channel_id=1, source_target_pairs={{0,2},{2,0},{1,3},{3,1},{4,6},{6,4},{5,7},{7,5},{8,10},{10,8},{9,1... | collective-permute-start | bytes 393224 | tf_op jit(solution)/shard_map/ppermute | solution.py:499
Sparse Core Ops, SparseCore 0:
  20.4 32.0 all-gather.3
  78.8 40.4 all-gather.5
where the time goes:
time: 225 us; the launch traced here: 224 us
  waiting for transfers between devices  90.9 us (40%)
  starting transfers between devices  65.7 us (29%)
  Pallas kernels  32 us (14%)
  between operations  13.9 us (6%)
  local copies, waits for them, and re-layouts  11.3 us (5%)
  other arithmetic  10.7 us (5%)
    ppermute x8, waiting for transfers between devices, ring_sum(): got_up = lax.ppermute(up, 'ma_0', UP)  45 us
    ppermute x8, starting transfers between devices, ring_gather(): above = lax.ppermute(above, 'ma_0', DOWN)  30.9 us
    ppermute x8, waiting for transfers between devices, ring_gather(): above = lax.ppermute(above, 'ma_0', DOWN)  20.5 us
    ppermute x6, starting transfers between devices, ring_sum(): got_down = lax.ppermute(down, 'ma_0', DOWN)  19.6 us
    pallas_call x1, Pallas kernels, attention(): pl.pallas_call(functools.partial(attention_kernel, float(wide * RING)), i...  12.4 us
    pallas_call x1, Pallas kernels, feed_forward(): pl.pallas_call(functools.partial(down_kernel, float(wide * RING)), in_spe...  10.1 us
    ppermute x1, waiting for transfers between devices, layer(): first_share = lax.ppermute(jnp.concatenate(share, axis=1), 'row', SWAP)  9.28 us
    pallas_call x1, Pallas kernels, feed_forward(): pl.pallas_call(gate_kernel, in_specs=[SMEM] + [ANY] * (early + 3), out_sp...  6.97 us
  transfers between devices with their start and end apart: 36, of which 18 were waited for; matrix products, arithmetic and copies ran while one was open for 6% of the time, Pallas kernels for 10%

commit v1 on v0

v1 whole, which is shorter than its diff:
```python
import functools

import jax
import jax.numpy as jnp
from jax import lax
from jax.experimental import pallas as pl
from jax.experimental.pallas import tpu as pltpu
from jax.sharding import Mesh
from jax.sharding import PartitionSpec as P

MA = ("ma_0", "ma_1")
MA_ROW = ("ma_0", "ma_1", "row")

bucket_thresholds = (1, 2, 3, 4, 5, 6, 7, 8, 11, 16, 23, 32, 45, 64, 91, 128)
epsilon = 1e-06
RING = 8
SWAP = [(0, 1), (1, 0)]
UP = [(i, (i + 1) % RING) for i in range(RING)]
DOWN = [(i, (i - 1) % RING) for i in range(RING)]


def tied(value, *after):
    return lax.optimization_barrier((value, *after))[0]


def pair_order(mine, theirs, axis):
    first = lax.axis_index("ma_1") == 0
    return jnp.where(
        first,
        jnp.concatenate([mine, theirs], axis=axis),
        jnp.concatenate([theirs, mine], axis=axis),
    )


def ring_gather(block):
    held = {0: block}
    above = below = block
    for step in range(1, RING // 2 + 1):
        above = lax.ppermute(above, "ma_0", DOWN)
        held[step] = above
        if step < RING // 2:
            below = lax.ppermute(below, "ma_0", UP)
            held[RING - step] = below
    return held


SEND = (4, 5, 0, 1, 2, 3, 6, 7)


def ring_sum(first, second, rest):
    blocks = [first, second, *(rest[k] for k in range(RING - 2))]

    def block(owner):
        return blocks[SEND.index(owner % RING)].astype(jnp.float32)

    up, down = blocks[0], blocks[1]
    got_down = None
    for step in range(1, RING // 2 + 1):
        got_up = lax.ppermute(up, "ma_0", UP)
        if step > 1:
            got_down = lax.ppermute(down, "ma_0", DOWN)
        if step < RING // 2:
            up = (got_up.astype(jnp.float32) + block(4 - step)).astype(jnp.bfloat16)
            if got_down is not None:
                down = (got_down.astype(jnp.float32) + block(step - 4)).astype(jnp.bfloat16)
    return got_up.astype(jnp.float32) + got_down.astype(jnp.float32) + block(0)


def bias_kernel(bucket_ref, table_ref, bias_ref):
    heads, rows, columns = bias_ref.shape
    bucket = bucket_ref[...]
    lines = jnp.zeros(bucket.shape, jnp.float32)
    for b in range(table_ref.shape[1]):
        lines = jnp.where(bucket == b, table_ref[:, b : b + 1], lines)
    for h in range(heads):
        wide = jnp.broadcast_to(lines[h : h + 1, :], (rows, bucket.shape[1]))
        bias_ref[h] = pltpu.roll(wide, 0, 1, stride=1, stride_axis=0)[:, :columns]


def position_bias(table, length):
    offset = jnp.arange(2 * length, dtype=jnp.int32)
    offset = jnp.where(offset < length, offset, offset - 2 * length)
    distance = jnp.abs(offset)
    bucket = jnp.where(offset > 0, 15, 0)
    for threshold in bucket_thresholds[:15]:
        bucket = bucket + (distance >= threshold).astype(jnp.int32)
    last = (distance >= bucket_thresholds[15]) & (offset > 0)
    bucket = bucket + last.astype(jnp.int32)
    heads = table.shape[1]
    return pl.pallas_call(
        bias_kernel,
        out_shape=jax.ShapeDtypeStruct((heads, length, length), jnp.float32),
        cost_estimate=pl.CostEstimate(flops=10**8, bytes_accessed=10**6, transcendentals=0),
        name="position_bias",
    )(jnp.broadcast_to(bucket[None], (heads, 2 * length)), table.T)


def as_column(line):
    size = line.shape[1]
    at_row = lax.broadcasted_iota(jnp.int32, (size, size), 0)
    at_column = lax.broadcasted_iota(jnp.int32, (size, size), 1)
    spread_out = jnp.where(at_row == at_column, jnp.broadcast_to(line, (size, size)), 0.0)
    return jnp.sum(spread_out, axis=1, keepdims=True)


def dot(a, b):
    return jnp.dot(a, b, preferred_element_type=jnp.float32)


def attention_kernel(width, *refs):
    ring_at, half = lax.axis_index("ma_0"), lax.axis_index("row")
    blocks = refs[:RING]
    own = refs[RING : RING + 3]
    other_ref, own_out_ref, other_out_ref, bias_ref = refs[RING + 3 : RING + 7]
    out_refs = refs[RING + 7 : RING + 10]
    x_ref, w_ref, o_ref, acc_ref, attended_ref, both_ref = refs[RING + 10 : RING + 16]
    x_sem, own_sem, other_sem, o_sem = refs[RING + 16 :]
    length = acc_ref.shape[0]
    inner = attended_ref.shape[1]
    wide = x_ref.shape[2]
    parts = RING // 2
    rows = parts * wide

    own_copies = [
        pltpu.make_async_copy(
            own[k], w_ref.at[pl.ds(0, rows), pl.ds(k * inner, inner)], own_sem.at[k]
        )
        for k in range(3)
    ]
    x_copies = [
        pltpu.make_async_copy(blocks[k], x_ref.at[k], x_sem.at[k]) for k in range(RING)
    ]
    other_copies = [
        pltpu.make_async_copy(
            other_ref.at[pl.ds(k * wide, wide), :],
            w_ref.at[pl.ds(rows + k * wide, wide), :],
            other_sem.at[k],
        )
        for k in range(parts)
    ]
    o_copies = [
        pltpu.make_async_copy(ref, o_ref.at[k], o_sem.at[k])
        for k, ref in enumerate((own_out_ref, other_out_ref))
    ]
    for copy in x_copies + own_copies + other_copies + o_copies:
        copy.start()
    for copy in x_copies:
        copy.wait()
    squares = x_ref[0, length : length + 1, :length].astype(jnp.float32)
    for k in range(1, RING):
        squares += x_ref[k, length : length + 1, :length].astype(jnp.float32)
    scale = as_column(lax.rsqrt(squares / width + epsilon))
    for copy in own_copies:
        copy.wait()
    acc_ref[...] = jnp.zeros_like(acc_ref)

    def add_slot(slot, unused):
        weights = w_ref[pl.ds(pl.multiple_of(slot * wide, wide), wide), :]
        block = lax.rem(slot + half * parts + RING - ring_at, RING)
        acc_ref[...] += dot(x_ref[block, :length, :], weights)
        return unused

    lax.fori_loop(0, parts, add_slot, 0)
    for copy in other_copies:
        copy.wait()
    lax.fori_loop(parts, RING, add_slot, 0)

    heads = bias_ref.shape[0]
    size = inner // heads
    pair = 2 * size

    def two_heads(n, unused):
        query, key, value = (
            (acc_ref[:, pl.ds(pl.multiple_of(k * inner + n * pair, pair), pair)] * scale).astype(
                jnp.bfloat16
            )
            for k in range(3)
        )
        for h in range(2):
            at = slice(h * size, (h + 1) * size)
            scores = (
                lax.dot_general(
                    query[:, at],
                    key[:, at],
                    (((1,), (1,)), ((), ())),
                    preferred_element_type=jnp.float32,
                )
                + bias_ref[2 * n + h]
            )
            exponent = jnp.exp(scores - jnp.max(scores, axis=-1, keepdims=True))
            weights = exponent / jnp.sum(exponent, axis=-1, keepdims=True)
            both_ref[:, at] = dot(weights.astype(jnp.bfloat16), value[:, at]).astype(jnp.bfloat16)
        attended_ref[:, pl.ds(pl.multiple_of(n * pair, pair), pair)] = both_ref[...]
        return unused

    lax.fori_loop(0, heads // 2, two_heads, 0)

    for copy in o_copies:
        copy.wait()

    def out_block(owner):
        slot = lax.rem(ring_at + owner + half * parts, RING)
        which = slot // parts
        column = pl.multiple_of((slot - which * parts) * wide, wide)
        product = dot(attended_ref[...], o_ref[which, :, pl.ds(column, wide)])
        return product.astype(jnp.bfloat16)

    store_blocks(out_block, out_refs)


def store_blocks(block, out_refs):
    first_ref, second_ref, rest_ref = out_refs
    first_ref[...] = block(SEND[0])
    second_ref[...] = block(SEND[1])

    def store(k, unused):
        rest_ref[k] = block(jnp.where(k < 4, k, k + 2))
        return unused

    lax.fori_loop(0, RING - 2, store, 0)


def block_shapes(length, width):
    one = jax.ShapeDtypeStruct((length, width), jnp.bfloat16)
    return [one, one, jax.ShapeDtypeStruct((RING - 2, length, width), jnp.bfloat16)]


ANY = pl.BlockSpec(memory_space=pl.ANY)
IN_VMEM = pl.BlockSpec(memory_space=pltpu.VMEM)


def attention(held, bias, own, other, own_out, other_out):
    length = bias.shape[1]
    inner = own[0].shape[1]
    rows, wide = held[0].shape
    parts = RING // 2
    return pl.pallas_call(
        functools.partial(attention_kernel, float(wide * RING)),
        in_specs=[ANY] * (RING + 6) + [IN_VMEM],
        out_specs=[IN_VMEM] * 3,
        scratch_shapes=[
            pltpu.VMEM((RING, rows, wide), jnp.bfloat16),
            pltpu.VMEM((RING * wide, 3 * inner), jnp.bfloat16),
            pltpu.VMEM((2, *own_out.shape), jnp.bfloat16),
            pltpu.VMEM((length, 3 * inner), jnp.float32),
            pltpu.VMEM((length, inner), jnp.bfloat16),
            pltpu.VMEM((length, 2 * inner // bias.shape[0]), jnp.bfloat16),
            pltpu.SemaphoreType.DMA((RING,)),
            pltpu.SemaphoreType.DMA((3,)),
            pltpu.SemaphoreType.DMA((parts,)),
            pltpu.SemaphoreType.DMA((2,)),
        ],
        out_shape=block_shapes(length, wide),
        cost_estimate=pl.CostEstimate(
            flops=2 * length * wide * RING * 4 * inner, bytes_accessed=10**7, transcendentals=0
        ),
        name="attention",
    )(
        *[held[k] for k in range(RING)],
        *own,
        other,
        own_out,
        other_out,
        bias,
    )


FIRST = (0, 1, 7)
SECOND = (2, 6, 3, 5)
LAST = (4,)


def gate_copies(owners, blocks, gate_ref, up_ref, other_ref, x_ref, w_ref, x_sem, w_sem):
    wide, hidden = x_ref.shape[2], gate_ref.shape[1]
    ring_at = lax.axis_index("ma_0")
    copies = []
    for k, (owner, block) in enumerate(zip(owners, blocks)):
        slot = lax.rem(ring_at + owner, RING)
        row = pl.ds(pl.multiple_of(slot * wide, wide), wide)
        copies.append(pltpu.make_async_copy(block, x_ref.at[k], x_sem.at[k]))
        sources = [
            gate_ref.at[row, :],
            up_ref.at[row, :],
            other_ref.at[slot, pl.ds(0, wide), :],
            other_ref.at[slot, pl.ds(wide, wide), :],
        ]
        for n, source in enumerate(sources):
            copies.append(
                pltpu.make_async_copy(
                    source, w_ref.at[k, :, pl.ds(n * hidden, hidden)], w_sem.at[k, n]
                )
            )
    return copies


def gate_kernel(owners, more, *refs):
    count = len(owners)
    blocks = refs[:count]
    gate_ref, up_ref, other_ref = refs[count : count + 3]
    refs = refs[count + 3 :]
    if more:
        acc_in_ref, squares_in_ref, refs = refs[0], refs[1], refs[2:]
    acc_ref, squares_ref, x_ref, w_ref, x_sem, w_sem = refs
    length = acc_ref.shape[0]
    copies = gate_copies(owners, blocks, gate_ref, up_ref, other_ref, x_ref, w_ref, x_sem, w_sem)
    for copy in copies:
        copy.start()
    if more:
        acc_ref[...] = acc_in_ref[...]
        squares_ref[...] = squares_in_ref[...]
    else:
        acc_ref[...] = jnp.zeros_like(acc_ref)
        squares_ref[...] = jnp.zeros_like(squares_ref)
    for copy in copies:
        copy.wait()

    def add_block(k, unused):
        squares_ref[...] += x_ref[k, length : length + 8, :length].astype(jnp.float32)
        acc_ref[...] += dot(x_ref[k, :length, :], w_ref[k])
        return unused

    lax.fori_loop(0, count, add_block, 0)


def hidden_kernel(width, *refs):
    count = len(LAST)
    blocks = refs[:count]
    gate_ref, up_ref, other_ref, acc_in_ref, squares_in_ref = refs[count : count + 5]
    hidden_ref, x_ref, w_ref, x_sem, w_sem = refs[count + 5 :]
    size = gate_ref.shape[1]
    length = hidden_ref.shape[0]
    copies = gate_copies(LAST, blocks, gate_ref, up_ref, other_ref, x_ref, w_ref, x_sem, w_sem)
    for copy in copies:
        copy.start()
    for copy in copies:
        copy.wait()
    rows = x_ref[0, :length, :]
    squares = squares_in_ref[0:1, :] + x_ref[0, length : length + 1, :length].astype(jnp.float32)
    scale = as_column(lax.rsqrt(squares / width + epsilon))
    for k in range(2):
        sums = []
        for n in (2 * k, 2 * k + 1):
            at = slice(n * size, (n + 1) * size)
            sums.append((acc_in_ref[:, at] + dot(rows, w_ref[0, :, at])) * scale)
        hidden_ref[:, k * size : (k + 1) * size] = (
            jax.nn.gelu(sums[0], approximate=True) * sums[1]
        ).astype(jnp.bfloat16)


def down_copies(first_refs, d_ref, d_sem):
    copies = []
    ring_at = lax.axis_index("ma_0")
    for j in range(RING):
        slot = lax.rem(ring_at + j, RING)
        for n, source in enumerate(first_refs(slot)):
            rows = source.shape[0]
            copies.append(
                pltpu.make_async_copy(source, d_ref.at[j, pl.ds(n * rows, rows), :], d_sem.at[j, n])
            )
    return copies


def own_down_kernel(hidden_ref, down_ref, other_ref, out_ref, d_ref, d_sem):
    size = d_ref.shape[1] // 2
    part = d_ref.shape[2]
    pair_at = lax.axis_index("ma_1")

    def sources(slot):
        column = pl.multiple_of((slot * 2 + pair_at) * part, part)
        return down_ref.at[:, pl.ds(column, part)], other_ref.at[slot, pl.ds(4 * size, size), :]

    copies = down_copies(sources, d_ref, d_sem)
    for copy in copies:
        copy.start()
    for copy in copies:
        copy.wait()

    def block(j, unused):
        out_ref[j] = dot(hidden_ref[...], d_ref[j])
        return unused

    lax.fori_loop(0, RING, block, 0)


def pair_down_kernel(hidden_ref, other_ref, own_ref, *refs):
    out_refs, (d_ref, own_in_ref, d_sem, own_sem) = refs[:3], refs[3:]
    size = d_ref.shape[1] // 2
    own_copy = pltpu.make_async_copy(own_ref, own_in_ref, own_sem)
    own_copy.start()

    def sources(slot):
        return [other_ref.at[slot, pl.ds((5 + n) * size, size), :] for n in range(2)]

    copies = down_copies(sources, d_ref, d_sem)
    for copy in copies:
        copy.start()
    own_copy.wait()
    for copy in copies:
        copy.wait()

    def block(owner):
        return (own_in_ref[owner] + dot(hidden_ref[...], d_ref[owner])).astype(jnp.bfloat16)

    store_blocks(block, out_refs)


def feed_forward(held, gate, up, down, other):
    rows, wide = held[0].shape
    hidden = gate.shape[1]
    length = rows - 8
    part = wide // 2
    sums = [
        jax.ShapeDtypeStruct((length, 4 * hidden), jnp.float32),
        jax.ShapeDtypeStruct((8, length), jnp.float32),
    ]

    def scratch(count):
        return [
            pltpu.VMEM((count, rows, wide), jnp.bfloat16),
            pltpu.VMEM((count, wide, 4 * hidden), jnp.bfloat16),
            pltpu.SemaphoreType.DMA((count,)),
            pltpu.SemaphoreType.DMA((count, 4)),
        ]

    def cost(count, extra=0):
        return pl.CostEstimate(
            flops=2 * length * wide * 4 * hidden * count + extra,
            bytes_accessed=10**6 * (count + 1),
            transcendentals=0,
        )

    def gate_sums(owners, before):
        return pl.pallas_call(
            functools.partial(gate_kernel, owners, bool(before)),
            in_specs=[ANY] * (len(owners) + 3) + [IN_VMEM] * len(before),
            out_specs=[IN_VMEM] * 2,
            scratch_shapes=scratch(len(owners)),
            out_shape=sums,
            cost_estimate=cost(len(owners)),
        )(*[held[k] for k in owners], gate, up, other, *before)

    before = gate_sums(FIRST, ())
    before = gate_sums(SECOND, before)
    mine = pl.pallas_call(
        functools.partial(hidden_kernel, float(wide * RING)),
        in_specs=[ANY] * (len(LAST) + 3) + [IN_VMEM] * 2,
        out_specs=IN_VMEM,
        scratch_shapes=scratch(len(LAST)),
        out_shape=jax.ShapeDtypeStruct((length, 2 * hidden), jnp.bfloat16),
        cost_estimate=cost(1),
        name="hidden",
    )(*[held[k] for k in LAST], gate, up, other, *before)
    theirs = lax.ppermute(mine, "ma_1", SWAP)
    weights = [
        pltpu.VMEM((RING, 2 * hidden, part), jnp.bfloat16),
        pltpu.SemaphoreType.DMA((RING, 2)),
    ]
    own = pl.pallas_call(
        own_down_kernel,
        in_specs=[IN_VMEM, ANY, ANY],
        out_specs=IN_VMEM,
        scratch_shapes=weights,
        out_shape=jax.ShapeDtypeStruct((RING, length, part), jnp.float32),
        cost_estimate=cost(2),
        name="own_down",
    )(mine, down, other)
    return pl.pallas_call(
        pair_down_kernel,
        in_specs=[IN_VMEM, ANY, ANY],
        out_specs=[IN_VMEM] * 3,
        scratch_shapes=[
            weights[0],
            pltpu.VMEM((RING, length, part), jnp.float32),
            weights[1],
            pltpu.SemaphoreType.DMA,
        ],
        out_shape=block_shapes(length, part),
        cost_estimate=cost(2),
        name="pair_down",
    )(theirs, other, own)


def spread(values, gain):
    rows, width = values.shape
    as_float = values.astype(jnp.float32)
    squares = jnp.sum(as_float * as_float, axis=1)
    gained = (as_float * gain.astype(jnp.float32)).astype(jnp.bfloat16)
    line = jnp.concatenate([squares, jnp.zeros((width - rows,), jnp.float32)])
    tail = jnp.broadcast_to(line.astype(jnp.bfloat16)[None], (8, width))
    block = jnp.concatenate([gained, tail], axis=0)
    return ring_gather(block)


def layer(
    tokens,
    attn_gain,
    query_weight,
    key_weight,
    value_projection_matrix,
    attention_output_matrix,
    bucket_bias_matrix,
    ffn_gain,
    gate_weight,
    up_weight,
    down_projection_weight,
):
    sequences, length, part = tokens.shape
    copy_at = lax.axis_index("ba")
    copies = lax.axis_size("ba")
    token_rows = tokens.reshape(length, part)

    gains = jnp.concatenate(
        [attn_gain[None], ffn_gain[None], jnp.zeros((6, part), jnp.bfloat16)], axis=0
    )
    mine = jnp.concatenate([token_rows, gains], axis=0)
    theirs = lax.ppermute(mine, "ma_1", SWAP)

    half_rows = query_weight.shape[0]
    depth = half_rows // copies
    share = [
        lax.dynamic_slice_in_dim(w, copy_at * depth, depth, 0)
        for w in (query_weight, key_weight, value_projection_matrix)
    ]
    first_share = lax.ppermute(jnp.concatenate(share, axis=1), "row", SWAP)
    other_first = lax.all_gather(first_share, "ba", axis=0, tiled=True)
    other_out = lax.ppermute(tied(attention_output_matrix, theirs), "row", SWAP)

    gate_depth = gate_weight.shape[0] // copies
    gate_share = [
        lax.dynamic_slice_in_dim(w, copy_at * gate_depth, gate_depth, 0)
        for w in (gate_weight, up_weight)
    ]
    down_width = down_projection_weight.shape[1] // copies
    pair_at = lax.axis_index("ma_1")

    def down_share(pair):
        at = copy_at * down_width + pair * part
        return lax.dynamic_slice_in_dim(down_projection_weight, at, part, 1)

    row_share = jnp.concatenate([*gate_share, down_share(pair_at)], axis=0)
    pair_share = down_share(1 - pair_at)

    wide = pair_order(mine, theirs, 1)
    wide_tokens = wide[:length]
    wide_attn_gain = wide[length]
    wide_ffn_gain = wide[length + 1]

    held = spread(wide_tokens, wide_attn_gain)
    row_share = lax.ppermute(tied(row_share, held[1]), "row", SWAP)
    pair_share = tied(pair_share, held[2])
    cross = [(0, 3), (3, 0), (1, 2), (2, 1)]
    cross_share = lax.ppermute(pair_share, ("ma_1", "row"), cross)
    pair_share = lax.ppermute(pair_share, "ma_1", SWAP)
    out_blocks = attention(
        held,
        position_bias(bucket_bias_matrix, length),
        (query_weight, key_weight, value_projection_matrix),
        other_first,
        attention_output_matrix,
        other_out,
    )
    second_share = jnp.concatenate([row_share, pair_share, cross_share], axis=0)
    second_share = tied(second_share, out_blocks[0])
    other_second = lax.all_gather(second_share, "ba", axis=0, tiled=False)
    summed = ring_sum(*out_blocks).astype(jnp.bfloat16)
    partner = lax.ppermute(summed, "ma_1", SWAP)
    attn_out = summed.astype(jnp.float32) + partner.astype(jnp.float32)
    residual = (wide_tokens.astype(jnp.float32) + attn_out).astype(jnp.bfloat16)
    first = lax.axis_index("ma_1") == 0
    own_residual = jnp.where(first, residual[:, :part], residual[:, part:])

    held = spread(residual, wide_ffn_gain)
    summed = ring_sum(
        *feed_forward(held, gate_weight, up_weight, down_projection_weight, other_second)
    )
    encoded = own_residual.astype(jnp.float32) + summed
    return encoded.astype(jnp.bfloat16).reshape(sequences, length, part)


def solution(mesh):
    split = Mesh(
        mesh.devices.reshape(mesh.shape["ba"], RING, 2, mesh.shape["row"]),
        ("ba", "ma_0", "ma_1", "row"),
    )
    return jax.shard_map(
        layer,
        mesh=split,
        in_specs=(
            P(("ba", "row"), None, MA),
            P(MA),
            P("row", MA),
            P("row", MA),
            P("row", MA),
            P(MA, "row"),
            P(None, MA),
            P(MA),
            P(None, MA_ROW),
            P(None, MA_ROW),
            P(MA_ROW, None),
        ),
        out_specs=P(("ba", "row"), None, MA),
        check_vma=False,
    )
```

time: 225 us -> 246 us (1.093)
  the two profiles are of different devices: /device:TPU:6 before, /device:TPU:2 now
where the time goes in v1:
time: 246 us
  waiting for transfers between devices  105 us (43%)
  starting transfers between devices  65.8 us (27%)
  Pallas kernels  42 us (17%)
  between operations  13.8 us (6%)
  local copies, waits for them, and re-layouts  9.91 us (4%)
  other arithmetic  9.26 us (4%)
    ppermute x8, waiting for transfers between devices, ring_sum(): got_up = lax.ppermute(up, 'ma_0', UP)  41.8 us
    ppermute x8, starting transfers between devices, ring_gather(): above = lax.ppermute(above, 'ma_0', DOWN)  30.4 us
    ppermute x1, waiting for transfers between devices, layer(): pair_share = lax.ppermute(pair_share, 'ma_1', SWAP)  22.8 us
    ppermute x6, starting transfers between devices, ring_sum(): got_down = lax.ppermute(down, 'ma_0', DOWN)  19.4 us
    ppermute x8, waiting for transfers between devices, ring_gather(): above = lax.ppermute(above, 'ma_0', DOWN)  17.4 us
    pallas_call x1, Pallas kernels, attention(): pl.pallas_call(functools.partial(attention_kernel, float(wide * RING)), i...  13 us
    pallas_call x2, Pallas kernels, gate_sums(): pl.pallas_call(functools.partial(gate_kernel, owners, bool(before)), in_s...  11.2 us
    ppermute x1, waiting for transfers between devices, layer(): first_share = lax.ppermute(jnp.concatenate(share, axis=1), 'row', SWAP)  9.28 us
  transfers between devices with their start and end apart: 38, of which 19 were waited for; matrix products, arithmetic and copies ran while one was open for 4% of the time, Pallas kernels for 8%

profile of v1, /device:TPU:2, one launch (start us, length us, event | category | flops | bytes accessed | tf_op | source)
XLA Modules:
  0.0 245.9 jit_solution(5523056572354428635)
XLA Ops:
  6.5 0.9 constant_dynamic-slice_fusion.6
  7.5 1.0 constant_dynamic-slice_fusion.4
  8.5 1.7 collective-permute-start.8
  10.2 9.3 %collective-permute-done.8 = bf16[256,768]{1,0:T(8,128)(2,1)S(1)} collective-permute-done((bf16[256,768]{1,0:T(8,128)(2,1)S(1)}, bf16[256,768]{1,0:T(8,128)(2,1)S(1)}, u32[]{:S(2)}, u32[]{:S(2)}) %collective-permute-start.8) | collective-permute-done | bytes 393248 | tf_op jit(solution)/shard_map/ppermute | solution.py:524
  19.5 0.7 copy-done.6
  20.4 3.3 %collective-permute-start = (bf16[264,256]{1,0:T(8,128)(2,1)S(1)}, bf16[264,256]{1,0:T(8,128)(2,1)S(1)}, u32[]{:S(2)}, u32[]{:S(2)}) collective-permute-start(bf16[264,256]{1,0:T(8,128)(2,1)S(1)} %pad_maximum_fusion.5), channel_id=1, source_target_pairs={{0,2},{2,0},{1,3},{3,1},{4,6},{6,4},{5,7},{7,5},{8,10},{10,8},{9,1... | collective-permute-start | bytes 405512 | tf_op jit(solution)/shard_map/ppermute | solution.py:516
  23.7 3.3 %collective-permute-done = bf16[264,256]{1,0:T(8,128)(2,1)S(1)} collective-permute-done((bf16[264,256]{1,0:T(8,128)(2,1)S(1)}, bf16[264,256]{1,0:T(8,128)(2,1)S(1)}, u32[]{:S(2)}, u32[]{:S(2)}) %collective-permute-start) | collective-permute-done | bytes 135200 | tf_op jit(solution)/shard_map/ppermute | solution.py:516
  27.9 5.9 %collective-permute-start.1 = (bf16[264,512]{1,0:T(8,128)(2,1)S(1)}, bf16[264,512]{1,0:T(8,128)(2,1)}, u32[]{:S(2)}, u32[]{:S(2)}) collective-permute-start(bf16[264,512]{1,0:T(8,128)(2,1)S(1)} %pad_maximum_fusion.3.refs_0_), channel_id=1, source_target_pairs={{0,28},{4,0},{8,4},{12,8},{16,12},{20,16},{24,20},{28,24},{1,29},{... | collective-permute-start | bytes 811016 | tf_op jit(solution)/shard_map/ppermute | solution.py:39
  33.8 1.7 constant_dynamic-slice_fusion.1
  35.5 1.1 constant_dynamic-slice_fusion.2
  36.7 1.7 collective-permute-start.9
  38.4 3.3 %collective-permute-start.2 = (bf16[264,512]{1,0:T(8,128)(2,1)}, bf16[264,512]{1,0:T(8,128)(2,1)S(1)}, u32[]{:S(2)}, u32[]{:S(2)}) collective-permute-start(bf16[264,512]{1,0:T(8,128)(2,1)} %collective-permute-done.1.refs_1_), channel_id=1, source_target_pairs={{0,28},{4,0},{8,4},{12,8},{16,12},{20,16},{24,20},{28,24},{1,29},{... | collective-permute-start | bytes 811016 | tf_op jit(solution)/shard_map/ppermute | solution.py:39
  41.6 0.9 pad_maximum_fusion.1
  42.5 1.6 collective-permute-start.22
  44.3 0.7 copy-done.10
  45.0 1.4 collective-permute-done.2.refs_2_
  46.4 3.6 %collective-permute-start.3 = (bf16[264,512]{1,0:T(8,128)(2,1)S(1)}, bf16[264,512]{1,0:T(8,128)(2,1)}, u32[]{:S(2)}, u32[]{:S(2)}) collective-permute-start(bf16[264,512]{1,0:T(8,128)(2,1)S(1)} %collective-permute-done.2.refs_2_), channel_id=1, source_target_pairs={{0,28},{4,0},{8,4},{12,8},{16,12},{20,16},{24,20},{28,24},{1,29},{... | collective-permute-start | bytes 811016 | tf_op jit(solution)/shard_map/ppermute | solution.py:39
  50.0 3.3 %collective-permute-start.23 = (bf16[256,256]{1,0:T(8,128)(2,1)}, bf16[256,256]{1,0:T(8,128)(2,1)S(1)}, u32[]{:S(2)}, u32[]{:S(2)}) collective-permute-start(bf16[256,256]{1,0:T(8,128)(2,1)} %get-tuple-element.24), channel_id=1, source_target_pairs={{0,2},{2,0},{1,3},{3,1},{4,6},{6,4},{5,7},{7,5},{8,10},{10,8},{9,1... | collective-permute-start | bytes 393224 | tf_op jit(solution)/shard_map/ppermute | solution.py:553
  53.4 2.5 %collective-permute-start.24 = (bf16[256,256]{1,0:T(8,128)(2,1)}, bf16[256,256]{1,0:T(8,128)(2,1)S(1)}, u32[]{:S(2)}, u32[]{:S(2)}) collective-permute-start(bf16[256,256]{1,0:T(8,128)(2,1)} %get-tuple-element.24), channel_id=1, source_target_pairs={{0,3},{3,0},{1,2},{2,1},{4,7},{7,4},{5,6},{6,5},{8,11},{11,8},{9,1... | collective-permute-start | bytes 393224 | tf_op jit(solution)/shard_map/ppermute | solution.py:552
  55.9 22.8 %collective-permute-done.23 = bf16[256,256]{1,0:T(8,128)(2,1)S(1)} collective-permute-done((bf16[256,256]{1,0:T(8,128)(2,1)}, bf16[256,256]{1,0:T(8,128)(2,1)S(1)}, u32[]{:S(2)}, u32[]{:S(2)}) %collective-permute-start.23) | collective-permute-done | bytes 131104 | tf_op jit(solution)/shard_map/ppermute | solution.py:553
  78.7 3.2 %collective-permute-start.4 = (bf16[264,512]{1,0:T(8,128)(2,1)}, bf16[264,512]{1,0:T(8,128)(2,1)}, u32[]{:S(2)}, u32[]{:S(2)}) collective-permute-start(bf16[264,512]{1,0:T(8,128)(2,1)} %collective-permute-done.3.refs_3_), channel_id=1, source_target_pairs={{0,28},{4,0},{8,4},{12,8},{16,12},{20,16},{24,20},{28,24},{1,29},{... | collective-permute-start | bytes 811016 | tf_op jit(solution)/shard_map/ppermute | solution.py:39
  81.9 0.6 broadcast_in_dim.40.bucket_ref
  82.5 2.1 position_bias.1.refs_14_
  84.7 1.0 pad_maximum_fusion
  85.7 1.0 collective-permute-done.7.refs_5_
  86.7 1.0 copy-done.4
  87.7 13.0 %attention.1 = (bf16[256,512]{1,0:T(8,128)(2,1)}, bf16[256,512]{1,0:T(8,128)(2,1)}, bf16[6,256,512]{2,1,0:T(8,128)(2,1)}) custom-call(bf16[264,512]{1,0:T(8,128)(2,1)} %copy-done.2, bf16[264,512]{1,0:T(8,128)(2,1)} %collective-permute-done.1.refs_1_, bf16[264,512]{1,0:T(8,128)(2,1)} %copy-done.11, bf16[264,512]{1,0:T(8,128)(2,1)} %collective-permute-done.3.refs_3_, ...), custom_call_target="tpu_custom_call" | custom-call | flops 2147483648 | bytes 10000000 | tf_op jit(solution)/shard_map/attention/pallas_call | solution.py:237
  101.0 3.2 %collective-permute-start.14 = (bf16[256,512]{1,0:T(8,128)(2,1)}, bf16[256,512]{1,0:T(8,128)(2,1)S(1)}, u32[]{:S(2)}, u32[]{:S(2)}) collective-permute-start(bf16[256,512]{1,0:T(8,128)(2,1)} %get-tuple-element.22), channel_id=1, source_target_pairs={{0,28},{4,0},{8,4},{12,8},{16,12},{20,16},{24,20},{28,24},{1,29},{... | collective-permute-start | bytes 786440 | tf_op jit(solution)/shard_map/ppermute | solution.py:61
  104.2 5.7 %collective-permute-done.10 = bf16[256,512]{1,0:T(8,128)(2,1)S(1)} collective-permute-done((bf16[256,512]{1,0:T(8,128)(2,1)}, bf16[256,512]{1,0:T(8,128)(2,1)S(1)}, u32[]{:S(2)}, u32[]{:S(2)}) %collective-permute-start.10) | collective-permute-done | bytes 262176 | tf_op jit(solution)/shard_map/ppermute | solution.py:59
  109.8 1.1 fusion.10
  111.0 10.0 %collective-permute-done.11 = bf16[256,512]{1,0:T(8,128)(2,1)S(1)} collective-permute-done((bf16[256,512]{1,0:T(8,128)(2,1)S(1)}, bf16[256,512]{1,0:T(8,128)(2,1)S(1)}, u32[]{:S(2)}, u32[]{:S(2)}) %collective-permute-start.11) | collective-permute-done | bytes 262176 | tf_op jit(solution)/shard_map/ppermute | solution.py:59
  121.2 3.2 %collective-permute-start.15 = (bf16[256,512]{1,0:T(8,128)(2,1)S(1)}, bf16[256,512]{1,0:T(8,128)(2,1)S(1)}, u32[]{:S(2)}, u32[]{:S(2)}) collective-permute-start(bf16[256,512]{1,0:T(8,128)(2,1)S(1)} %get-tuple-element.40), channel_id=1, source_target_pairs={{0,28},{4,0},{8,4},{12,8},{16,12},{20,16},{24,20},{28,24},{1,29},{... | collective-permute-start | bytes 786440 | tf_op jit(solution)/shard_map/ppermute | solution.py:61
  124.5 5.9 %collective-permute-done.12 = bf16[256,512]{1,0:T(8,128)(2,1)S(1)} collective-permute-done((bf16[256,512]{1,0:T(8,128)(2,1)S(1)}, bf16[256,512]{1,0:T(8,128)(2,1)S(1)}, u32[]{:S(2)}, u32[]{:S(2)}) %collective-permute-start.12) | collective-permute-done | bytes 262176 | tf_op jit(solution)/shard_map/ppermute | solution.py:59
  130.6 3.2 %collective-permute-start.16 = (bf16[256,512]{1,0:T(8,128)(2,1)S(1)}, bf16[256,512]{1,0:T(8,128)(2,1)S(1)}, u32[]{:S(2)}, u32[]{:S(2)}) collective-permute-start(bf16[256,512]{1,0:T(8,128)(2,1)S(1)} %get-tuple-element.38), channel_id=1, source_target_pairs={{0,28},{4,0},{8,4},{12,8},{16,12},{20,16},{24,20},{28,24},{1,29},{... | collective-permute-start | bytes 786440 | tf_op jit(solution)/shard_map/ppermute | solution.py:61
  133.8 4.3 %collective-permute-done.13 = bf16[256,512]{1,0:T(8,128)(2,1)S(1)} collective-permute-done((bf16[256,512]{1,0:T(8,128)(2,1)S(1)}, bf16[256,512]{1,0:T(8,128)(2,1)S(1)}, u32[]{:S(2)}, u32[]{:S(2)}) %collective-permute-start.13) | collective-permute-done | bytes 262176 | tf_op jit(solution)/shard_map/ppermute | solution.py:59
  138.3 0.8 collective-permute-start.17
  139.1 7.1 %collective-permute-done.17 = bf16[256,512]{1,0:T(8,128)(2,1)S(1)} collective-permute-done((bf16[256,512]{1,0:T(8,128)(2,1)S(1)}, bf16[256,512]{1,0:T(8,128)(2,1)S(1)}, u32[]{:S(2)}, u32[]{:S(2)}) %collective-permute-start.17) | collective-permute-done | bytes 262176 | tf_op jit(solution)/shard_map/ppermute | solution.py:566
  146.6 3.3 %collective-permute-start.18 = (bf16[264,512]{1,0:T(8,128)(2,1)S(1)}, bf16[264,512]{1,0:T(8,128)(2,1)S(1)}, u32[]{:S(2)}, u32[]{:S(2)}) collective-permute-start(bf16[264,512]{1,0:T(8,128)(2,1)S(1)} %pad_maximum_fusion.4.refs_0_), channel_id=1, source_target_pairs={{0,28},{4,0},{8,4},{12,8},{16,12},{20,16},{24,20},{28,24},{1,29},{... | collective-permute-start | bytes 811016 | tf_op jit(solution)/shard_map/ppermute | solution.py:39
  149.9 5.4 %collective-permute-done.18.refs_1_ = bf16[264,512]{1,0:T(8,128)(2,1)S(1)} collective-permute-done((bf16[264,512]{1,0:T(8,128)(2,1)S(1)}, bf16[264,512]{1,0:T(8,128)(2,1)S(1)}, u32[]{:S(2)}, u32[]{:S(2)}) %collective-permute-start.18) | collective-permute-done | bytes 270368 | tf_op jit(solution)/shard_map/ppermute | solution.py:39
  155.3 3.7 %collective-permute-start.19 = (bf16[264,512]{1,0:T(8,128)(2,1)S(1)}, bf16[264,512]{1,0:T(8,128)(2,1)S(1)}, u32[]{:S(2)}, u32[]{:S(2)}) collective-permute-start(bf16[264,512]{1,0:T(8,128)(2,1)S(1)} %collective-permute-done.18.refs_1_), channel_id=1, source_target_pairs={{0,28},{4,0},{8,4},{12,8},{16,12},{20,16},{24,20},{28,24},{1,29},{... | collective-permute-start | bytes 811016 | tf_op jit(solution)/shard_map/ppermute | solution.py:39
  159.0 6.6 %collective-permute-done.19.refs_0_ = bf16[264,512]{1,0:T(8,128)(2,1)S(1)} collective-permute-done((bf16[264,512]{1,0:T(8,128)(2,1)S(1)}, bf16[264,512]{1,0:T(8,128)(2,1)S(1)}, u32[]{:S(2)}, u32[]{:S(2)}) %collective-permute-start.19) | collective-permute-done | bytes 270368 | tf_op jit(solution)/shard_map/ppermute | solution.py:39
  165.6 3.7 %collective-permute-start.20 = (bf16[264,512]{1,0:T(8,128)(2,1)S(1)}, bf16[264,512]{1,0:T(8,128)(2,1)S(1)}, u32[]{:S(2)}, u32[]{:S(2)}) collective-permute-start(bf16[264,512]{1,0:T(8,128)(2,1)S(1)} %collective-permute-done.19.refs_0_), channel_id=1, source_target_pairs={{0,28},{4,0},{8,4},{12,8},{16,12},{20,16},{24,20},{28,24},{1,29},{... | collective-permute-start | bytes 811016 | tf_op jit(solution)/shard_map/ppermute | solution.py:39
  169.3 4.0 %collective-permute-done.20.refs_2_ = bf16[264,512]{1,0:T(8,128)(2,1)S(1)} collective-permute-done((bf16[264,512]{1,0:T(8,128)(2,1)S(1)}, bf16[264,512]{1,0:T(8,128)(2,1)S(1)}, u32[]{:S(2)}, u32[]{:S(2)}) %collective-permute-start.20) | collective-permute-done | bytes 270368 | tf_op jit(solution)/shard_map/ppermute | solution.py:39
  173.3 3.7 %collective-permute-start.21 = (bf16[264,512]{1,0:T(8,128)(2,1)S(1)}, bf16[264,512]{1,0:T(8,128)(2,1)S(1)}, u32[]{:S(2)}, u32[]{:S(2)}) collective-permute-start(bf16[264,512]{1,0:T(8,128)(2,1)S(1)} %collective-permute-done.20.refs_2_), channel_id=1, source_target_pairs={{0,28},{4,0},{8,4},{12,8},{16,12},{20,16},{24,20},{28,24},{1,29},{... | collective-permute-start | bytes 811016 | tf_op jit(solution)/shard_map/ppermute | solution.py:39
  177.0 4.6 %shard_map.109 = (f32[256,1024]{1,0:T(8,128)}, f32[8,256]{1,0:T(8,128)}) custom-call(bf16[264,512]{1,0:T(8,128)(2,1)} %copy-done.1, bf16[264,512]{1,0:T(8,128)(2,1)} %copy-done.7, bf16[264,512]{1,0:T(8,128)(2,1)} %copy-done.8, bf16[4096,256]{1,0:T(8,128)(2,1)} %refs_1_.1, bf16[4096,256]{1,0:T(8,128)(2,1)} %refs_2_.1, bf16[8,1792,256]{2,1,0:T(8,128)(2,1)} %bitcast.43), custom_call_target="tpu_custom_call" | custom-call | flops 805306368 | bytes 4000000 | tf_op jit(solution)/shard_map/pallas_call | solution.py:433
  181.7 0.7 copy-done.15
  182.4 6.6 %shard_map.110 = (f32[256,1024]{1,0:T(8,128)}, f32[8,256]{1,0:T(8,128)}) custom-call(bf16[264,512]{1,0:T(8,128)(2,1)} %copy-done.12, bf16[264,512]{1,0:T(8,128)(2,1)} %copy-done.13, bf16[264,512]{1,0:T(8,128)(2,1)} %copy-done.14, bf16[264,512]{1,0:T(8,128)(2,1)} %copy-done.15, bf16[4096,256]{1,0:T(8,128)(2,1)} %refs_1_.1, bf16[4096,256]{1,0:T(8,128)(2,1)} %refs_2_.1, ...), custom_call_target="tpu_custom_call" | custom-call | flops 1073741824 | bytes 5000000 | tf_op jit(solution)/shard_map/pallas_call | solution.py:433
  189.0 0.7 copy-done.9
  189.7 3.7 %hidden.1.hidden_ref = bf16[256,512]{1,0:T(8,128)(2,1)} custom-call(bf16[264,512]{1,0:T(8,128)(2,1)} %copy-done.9, bf16[4096,256]{1,0:T(8,128)(2,1)} %refs_1_.1, bf16[4096,256]{1,0:T(8,128)(2,1)} %refs_2_.1, bf16[8,1792,256]{2,1,0:T(8,128)(2,1)} %bitcast.45, f32[256,1024]{1,0:T(8,128)} %get-tuple-element.28.refs_4_, f32[8,256]{1,0:T(8,128)} %get-tuple-element.29.refs_5_), custom_call_target="tpu_custom_call" | custom-call | flops 268435456 | bytes 2000000 | tf_op jit(solution)/shard_map/hidden/pallas_call | solution.py:444
  193.6 5.9 %own_down.1.own_ref = f32[8,256,256]{2,1,0:T(8,128)} custom-call(bf16[256,512]{1,0:T(8,128)(2,1)} %hidden.1.hidden_ref, bf16[256,4096]{1,0:T(8,128)(2,1)} %down_ref.1, bf16[8,1792,256]{2,1,0:T(8,128)(2,1)} %bitcast.46), custom_call_target="tpu_custom_call" | custom-call | flops 536870912 | bytes 3000000 | tf_op jit(solution)/shard_map/own_down/pallas_call | solution.py:458
  199.5 2.1 collective-permute-done.28.hidden_ref
  201.6 0.7 copy-done.16
  202.3 6.0 %pair_down.1 = (bf16[256,256]{1,0:T(8,128)(2,1)}, bf16[256,256]{1,0:T(8,128)(2,1)}, bf16[6,256,256]{2,1,0:T(8,128)(2,1)}) custom-call(bf16[256,512]{1,0:T(8,128)(2,1)} %copy-done.16, bf16[8,1792,256]{2,1,0:T(8,128)(2,1)} %bitcast.47, f32[8,256,256]{2,1,0:T(8,128)} %own_down.1.own_ref), custom_call_target="tpu_custom_call" | custom-call | flops 536870912 | bytes 3000000 | tf_op jit(solution)/shard_map/pair_down/pallas_call | solution.py:467
  208.4 3.2 %collective-permute-start.33 = (bf16[256,256]{1,0:T(8,128)(2,1)}, bf16[256,256]{1,0:T(8,128)(2,1)S(1)}, u32[]{:S(2)}, u32[]{:S(2)}) collective-permute-start(bf16[256,256]{1,0:T(8,128)(2,1)} %get-tuple-element.32), channel_id=1, source_target_pairs={{0,28},{4,0},{8,4},{12,8},{16,12},{20,16},{24,20},{28,24},{1,29},{... | collective-permute-start | bytes 393224 | tf_op jit(solution)/shard_map/ppermute | solution.py:61
  211.7 4.0 %collective-permute-done.29 = bf16[256,256]{1,0:T(8,128)(2,1)S(1)} collective-permute-done((bf16[256,256]{1,0:T(8,128)(2,1)}, bf16[256,256]{1,0:T(8,128)(2,1)S(1)}, u32[]{:S(2)}, u32[]{:S(2)}) %collective-permute-start.29) | collective-permute-done | bytes 131104 | tf_op jit(solution)/shard_map/ppermute | solution.py:59
  215.6 0.9 fusion.17
  216.7 6.2 %collective-permute-done.30 = bf16[256,256]{1,0:T(8,128)(2,1)S(1)} collective-permute-done((bf16[256,256]{1,0:T(8,128)(2,1)S(1)}, bf16[256,256]{1,0:T(8,128)(2,1)S(1)}, u32[]{:S(2)}, u32[]{:S(2)}) %collective-permute-start.30) | collective-permute-done | bytes 131104 | tf_op jit(solution)/shard_map/ppermute | solution.py:59
  222.8 1.0 fusion.16
  224.0 3.2 %collective-permute-start.34 = (bf16[256,256]{1,0:T(8,128)(2,1)S(1)}, bf16[256,256]{1,0:T(8,128)(2,1)S(1)}, u32[]{:S(2)}, u32[]{:S(2)}) collective-permute-start(bf16[256,256]{1,0:T(8,128)(2,1)S(1)} %get-tuple-element.44), channel_id=1, source_target_pairs={{0,28},{4,0},{8,4},{12,8},{16,12},{20,16},{24,20},{28,24},{1,29},{... | collective-permute-start | bytes 393224 | tf_op jit(solution)/shard_map/ppermute | solution.py:61
  227.2 2.9 %collective-permute-done.31 = bf16[256,256]{1,0:T(8,128)(2,1)S(1)} collective-permute-done((bf16[256,256]{1,0:T(8,128)(2,1)S(1)}, bf16[256,256]{1,0:T(8,128)(2,1)S(1)}, u32[]{:S(2)}, u32[]{:S(2)}) %collective-permute-start.31) | collective-permute-done | bytes 131104 | tf_op jit(solution)/shard_map/ppermute | solution.py:59
  230.1 1.0 fusion.15
  231.3 3.3 %collective-permute-start.35 = (bf16[256,256]{1,0:T(8,128)(2,1)S(1)}, bf16[256,256]{1,0:T(8,128)(2,1)S(1)}, u32[]{:S(2)}, u32[]{:S(2)}) collective-permute-start(bf16[256,256]{1,0:T(8,128)(2,1)S(1)} %get-tuple-element.42), channel_id=1, source_target_pairs={{0,28},{4,0},{8,4},{12,8},{16,12},{20,16},{24,20},{28,24},{1,29},{... | collective-permute-start | bytes 393224 | tf_op jit(solution)/shard_map/ppermute | solution.py:61
  234.6 2.9 %collective-permute-done.32 = bf16[256,256]{1,0:T(8,128)(2,1)S(1)} collective-permute-done((bf16[256,256]{1,0:T(8,128)(2,1)S(1)}, bf16[256,256]{1,0:T(8,128)(2,1)S(1)}, u32[]{:S(2)}, u32[]{:S(2)}) %collective-permute-start.32) | collective-permute-done | bytes 131104 | tf_op jit(solution)/shard_map/ppermute | solution.py:59
  237.4 1.7 fusion.18
  (93 shorter events, 3.1 us)
Async XLA Ops:
  6.5 13.8 %copy-start.18 = (bf16[256]{0:T(256)(128)(2,1)S(1)}, bf16[256]{0:T(256)(128)(2,1)}, u32[]{:S(2)}) copy-start(bf16[256]{0:T(256)(128)(2,1)} %param.12) | copy-start | bytes 1540
  6.5 13.8 %copy-start.19 = (bf16[256]{0:T(256)(128)(2,1)S(1)}, bf16[256]{0:T(256)(128)(2,1)}, u32[]{:S(2)}) copy-start(bf16[256]{0:T(256)(128)(2,1)} %param.18) | copy-start | bytes 1540
  6.5 13.8 %copy-start.5 = (bf16[1,256,256]{2,1,0:T(8,128)(2,1)S(1)}, bf16[1,256,256]{2,1,0:T(8,128)(2,1)}, u32[]{:S(2)}) copy-start(bf16[1,256,256]{2,1,0:T(8,128)(2,1)} %param.11) | copy-start | bytes 393220
  6.5 80.1 %all-gather.4.cloned.1.call-start = ((), (), s32[]{:S(2)}) async-start(), calls=%async_computation | async-start | bytes 3538944 | tf_op jit(solution)/shard_map/all_gather | solution.py:525
  8.5 10.9 %collective-permute-start.8 = (bf16[256,768]{1,0:T(8,128)(2,1)S(1)}, bf16[256,768]{1,0:T(8,128)(2,1)S(1)}, u32[]{:S(2)}, u32[]{:S(2)}) collective-permute-start(bf16[256,768]{1,0:T(8,128)(2,1)S(1)} %pad_maximum_fusion.2), channel_id=1, source_target_pairs={{0,1},{1,0},{2,3},{3,2},{4,5},{5,4},{6,7},{7,6},{8,9},{9,8},{10,11... | collective-permute-start | bytes 1179656 | tf_op jit(solution)/shard_map/ppermute | solution.py:524
  19.5 0.7 copy-start.6
  20.2 16.4 %copy-start.3 = (bf16[256,2048]{1,0:T(8,128)(2,1)S(1)}, bf16[256,2048]{1,0:T(8,128)(2,1)}, u32[]{:S(2)}) copy-start(bf16[256,2048]{1,0:T(8,128)(2,1)} %refs_12_.1) | copy-start | bytes 3145732
  20.3 156.7 %all-gather.6.cloned.1.call-start = ((), (), s32[]{:S(2)}) async-start(), calls=%async_computation.1 | async-start | bytes 8257536 | tf_op jit(solution)/shard_map/all_gather | solution.py:564
  20.4 6.6 %collective-permute-start = (bf16[264,256]{1,0:T(8,128)(2,1)S(1)}, bf16[264,256]{1,0:T(8,128)(2,1)S(1)}, u32[]{:S(2)}, u32[]{:S(2)}) collective-permute-start(bf16[264,256]{1,0:T(8,128)(2,1)S(1)} %pad_maximum_fusion.5), channel_id=1, source_target_pairs={{0,2},{2,0},{1,3},{3,1},{4,6},{6,4},{5,7},{7,5},{8,10},{10,8},{9,1... | collective-permute-start | bytes 405512 | tf_op jit(solution)/shard_map/ppermute | solution.py:516
  27.9 56.8 %copy-start.2 = (bf16[264,512]{1,0:T(8,128)(2,1)}, bf16[264,512]{1,0:T(8,128)(2,1)S(1)}, u32[]{:S(2)}) copy-start(bf16[264,512]{1,0:T(8,128)(2,1)S(1)} %pad_maximum_fusion.3.refs_0_) | copy-start | bytes 811012
  27.9 10.4 %collective-permute-start.1 = (bf16[264,512]{1,0:T(8,128)(2,1)S(1)}, bf16[264,512]{1,0:T(8,128)(2,1)}, u32[]{:S(2)}, u32[]{:S(2)}) collective-permute-start(bf16[264,512]{1,0:T(8,128)(2,1)S(1)} %pad_maximum_fusion.3.refs_0_), channel_id=1, source_target_pairs={{0,28},{4,0},{8,4},{12,8},{16,12},{20,16},{24,20},{28,24},{1,29},{... | collective-permute-start | bytes 811016 | tf_op jit(solution)/shard_map/ppermute | solution.py:39
  36.6 7.7 %collective-permute-start.5 = (bf16[264,512]{1,0:T(8,128)(2,1)S(1)}, bf16[264,512]{1,0:T(8,128)(2,1)S(1)}, u32[]{:S(2)}, u32[]{:S(2)}) collective-permute-start(bf16[264,512]{1,0:T(8,128)(2,1)S(1)} %pad_maximum_fusion.3.refs_0_), channel_id=1, source_target_pairs={{0,4},{4,8},{8,12},{12,16},{16,20},{20,24},{24,28},{28,0},{1,5},{5... | collective-permute-start | bytes 811016 | tf_op jit(solution)/shard_map/ppermute | solution.py:42
  36.7 50.0 %collective-permute-start.9 = (bf16[256,2048]{1,0:T(8,128)(2,1)S(1)}, bf16[256,2048]{1,0:T(8,128)(2,1)S(1)}, u32[]{:S(2)}, u32[]{:S(2)}) collective-permute-start(bf16[256,2048]{1,0:T(8,128)(2,1)S(1)} %copy-done.3), channel_id=1, source_target_pairs={{0,1},{1,0},{2,3},{3,2},{4,5},{5,4},{6,7},{7,6},{8,9},{9,8},{10,11... | collective-permute-start | bytes 3145736 | tf_op jit(solution)/shard_map/ppermute | solution.py:526
  38.4 8.1 %collective-permute-start.2 = (bf16[264,512]{1,0:T(8,128)(2,1)}, bf16[264,512]{1,0:T(8,128)(2,1)S(1)}, u32[]{:S(2)}, u32[]{:S(2)}) collective-permute-start(bf16[264,512]{1,0:T(8,128)(2,1)} %collective-permute-done.1.refs_1_), channel_id=1, source_target_pairs={{0,28},{4,0},{8,4},{12,8},{16,12},{20,16},{24,20},{28,24},{1,29},{... | collective-permute-start | bytes 811016 | tf_op jit(solution)/shard_map/ppermute | solution.py:39
  42.5 42.1 %collective-permute-start.22 = (bf16[1280,256]{1,0:T(8,128)(2,1)}, bf16[1280,256]{1,0:T(8,128)(2,1)S(1)}, u32[]{:S(2)}, u32[]{:S(2)}) collective-permute-start(bf16[1280,256]{1,0:T(8,128)(2,1)} %pad_maximum_fusion.1), channel_id=1, source_target_pairs={{0,1},{1,0},{2,3},{3,2},{4,5},{5,4},{6,7},{7,6},{8,9},{9,8},{10,11... | collective-permute-start | bytes 1966088 | tf_op jit(solution)/shard_map/ppermute | solution.py:549
  44.3 0.7 copy-start.10
  45.0 8.3 %collective-permute-start.6 = (bf16[264,512]{1,0:T(8,128)(2,1)S(1)}, bf16[264,512]{1,0:T(8,128)(2,1)}, u32[]{:S(2)}, u32[]{:S(2)}) collective-permute-start(bf16[264,512]{1,0:T(8,128)(2,1)S(1)} %collective-permute-done.5.refs_7_), channel_id=1, source_target_pairs={{0,4},{4,8},{8,12},{12,16},{16,20},{20,24},{24,28},{28,0},{1,5},{5... | collective-permute-start | bytes 811016 | tf_op jit(solution)/shard_map/ppermute | solution.py:42
  46.4 6.9 %copy-start.11 = (bf16[264,512]{1,0:T(8,128)(2,1)}, bf16[264,512]{1,0:T(8,128)(2,1)S(1)}, u32[]{:S(2)}) copy-start(bf16[264,512]{1,0:T(8,128)(2,1)S(1)} %collective-permute-done.2.refs_2_) | copy-start | bytes 811012
  46.4 32.2 %collective-permute-start.3 = (bf16[264,512]{1,0:T(8,128)(2,1)S(1)}, bf16[264,512]{1,0:T(8,128)(2,1)}, u32[]{:S(2)}, u32[]{:S(2)}) collective-permute-start(bf16[264,512]{1,0:T(8,128)(2,1)S(1)} %collective-permute-done.2.refs_2_), channel_id=1, source_target_pairs={{0,28},{4,0},{8,4},{12,8},{16,12},{20,16},{24,20},{28,24},{1,29},{... | collective-permute-start | bytes 811016 | tf_op jit(solution)/shard_map/ppermute | solution.py:39
  50.0 28.6 %collective-permute-start.23 = (bf16[256,256]{1,0:T(8,128)(2,1)}, bf16[256,256]{1,0:T(8,128)(2,1)S(1)}, u32[]{:S(2)}, u32[]{:S(2)}) collective-permute-start(bf16[256,256]{1,0:T(8,128)(2,1)} %get-tuple-element.24), channel_id=1, source_target_pairs={{0,2},{2,0},{1,3},{3,1},{4,6},{6,4},{5,7},{7,5},{8,10},{10,8},{9,1... | collective-permute-start | bytes 393224 | tf_op jit(solution)/shard_map/ppermute | solution.py:553
  53.4 31.3 %collective-permute-start.24 = (bf16[256,256]{1,0:T(8,128)(2,1)}, bf16[256,256]{1,0:T(8,128)(2,1)S(1)}, u32[]{:S(2)}, u32[]{:S(2)}) collective-permute-start(bf16[256,256]{1,0:T(8,128)(2,1)} %get-tuple-element.24), channel_id=1, source_target_pairs={{0,3},{3,0},{1,2},{2,1},{4,7},{7,4},{5,6},{6,5},{8,11},{11,8},{9,1... | collective-permute-start | bytes 393224 | tf_op jit(solution)/shard_map/ppermute | solution.py:552
  78.7 8.0 %collective-permute-start.7 = (bf16[264,512]{1,0:T(8,128)(2,1)}, bf16[264,512]{1,0:T(8,128)(2,1)}, u32[]{:S(2)}, u32[]{:S(2)}) collective-permute-start(bf16[264,512]{1,0:T(8,128)(2,1)} %collective-permute-done.6.refs_6_), channel_id=1, source_target_pairs={{0,4},{4,8},{8,12},{12,16},{16,20},{20,24},{24,28},{28,0},{1,5},{5... | collective-permute-start | bytes 811016 | tf_op jit(solution)/shard_map/ppermute | solution.py:42
  78.7 8.0 %collective-permute-start.4 = (bf16[264,512]{1,0:T(8,128)(2,1)}, bf16[264,512]{1,0:T(8,128)(2,1)}, u32[]{:S(2)}, u32[]{:S(2)}) collective-permute-start(bf16[264,512]{1,0:T(8,128)(2,1)} %collective-permute-done.3.refs_3_), channel_id=1, source_target_pairs={{0,28},{4,0},{8,4},{12,8},{16,12},{20,16},{24,20},{28,24},{1,29},{... | collective-permute-start | bytes 811016 | tf_op jit(solution)/shard_map/ppermute | solution.py:39
  86.7 1.0 copy-start.4
  100.6 20.4 %copy-start = (bf16[6,256,512]{2,1,0:T(8,128)(2,1)S(1)}, bf16[6,256,512]{2,1,0:T(8,128)(2,1)}, u32[]{:S(2)}) copy-start(bf16[6,256,512]{2,1,0:T(8,128)(2,1)} %get-tuple-element.21) | copy-start | bytes 4718596
  100.7 9.2 %collective-permute-start.10 = (bf16[256,512]{1,0:T(8,128)(2,1)}, bf16[256,512]{1,0:T(8,128)(2,1)S(1)}, u32[]{:S(2)}, u32[]{:S(2)}) collective-permute-start(bf16[256,512]{1,0:T(8,128)(2,1)} %get-tuple-element.20), channel_id=1, source_target_pairs={{0,4},{4,8},{8,12},{12,16},{16,20},{20,24},{24,28},{28,0},{1,5},{5... | collective-permute-start | bytes 786440 | tf_op jit(solution)/shard_map/ppermute | solution.py:59
  101.0 10.1 %collective-permute-start.14 = (bf16[256,512]{1,0:T(8,128)(2,1)}, bf16[256,512]{1,0:T(8,128)(2,1)S(1)}, u32[]{:S(2)}, u32[]{:S(2)}) collective-permute-start(bf16[256,512]{1,0:T(8,128)(2,1)} %get-tuple-element.22), channel_id=1, source_target_pairs={{0,28},{4,0},{8,4},{12,8},{16,12},{20,16},{24,20},{28,24},{1,29},{... | collective-permute-start | bytes 786440 | tf_op jit(solution)/shard_map/ppermute | solution.py:61
  110.9 35.3 %copy-start.17 = (f32[1,512]{1,0:T(1,128)S(1)}, f32[1,512]{1,0:T(1,128)}, u32[]{:S(2)}) copy-start(f32[1,512]{1,0:T(1,128)} %get-tuple-element.48) | copy-start | bytes 6148
  110.9 10.1 %collective-permute-start.11 = (bf16[256,512]{1,0:T(8,128)(2,1)S(1)}, bf16[256,512]{1,0:T(8,128)(2,1)S(1)}, u32[]{:S(2)}, u32[]{:S(2)}) collective-permute-start(bf16[256,512]{1,0:T(8,128)(2,1)S(1)} %fusion.10), channel_id=1, source_target_pairs={{0,4},{4,8},{8,12},{12,16},{16,20},{20,24},{24,28},{28,0},{1,5},{5... | collective-permute-start | bytes 786440 | tf_op jit(solution)/shard_map/ppermute | solution.py:59
  121.1 9.2 %collective-permute-start.12 = (bf16[256,512]{1,0:T(8,128)(2,1)S(1)}, bf16[256,512]{1,0:T(8,128)(2,1)S(1)}, u32[]{:S(2)}, u32[]{:S(2)}) collective-permute-start(bf16[256,512]{1,0:T(8,128)(2,1)S(1)} %get-tuple-element.39), channel_id=1, source_target_pairs={{0,4},{4,8},{8,12},{12,16},{16,20},{20,24},{24,28},{28,0},{1,5},{5... | collective-permute-start | bytes 786440 | tf_op jit(solution)/shard_map/ppermute | solution.py:59
  121.2 9.1 %collective-permute-start.15 = (bf16[256,512]{1,0:T(8,128)(2,1)S(1)}, bf16[256,512]{1,0:T(8,128)(2,1)S(1)}, u32[]{:S(2)}, u32[]{:S(2)}) collective-permute-start(bf16[256,512]{1,0:T(8,128)(2,1)S(1)} %get-tuple-element.40), channel_id=1, source_target_pairs={{0,28},{4,0},{8,4},{12,8},{16,12},{20,16},{24,20},{28,24},{1,29},{... | collective-permute-start | bytes 786440 | tf_op jit(solution)/shard_map/ppermute | solution.py:61
  130.5 7.7 %collective-permute-start.13 = (bf16[256,512]{1,0:T(8,128)(2,1)S(1)}, bf16[256,512]{1,0:T(8,128)(2,1)S(1)}, u32[]{:S(2)}, u32[]{:S(2)}) collective-permute-start(bf16[256,512]{1,0:T(8,128)(2,1)S(1)} %get-tuple-element.37), channel_id=1, source_target_pairs={{0,4},{4,8},{8,12},{12,16},{16,20},{20,24},{24,28},{28,0},{1,5},{5... | collective-permute-start | bytes 786440 | tf_op jit(solution)/shard_map/ppermute | solution.py:59
  130.6 7.6 %collective-permute-start.16 = (bf16[256,512]{1,0:T(8,128)(2,1)S(1)}, bf16[256,512]{1,0:T(8,128)(2,1)S(1)}, u32[]{:S(2)}, u32[]{:S(2)}) collective-permute-start(bf16[256,512]{1,0:T(8,128)(2,1)S(1)} %get-tuple-element.38), channel_id=1, source_target_pairs={{0,28},{4,0},{8,4},{12,8},{16,12},{20,16},{24,20},{28,24},{1,29},{... | collective-permute-start | bytes 786440 | tf_op jit(solution)/shard_map/ppermute | solution.py:61
  138.3 8.0 %collective-permute-start.17 = (bf16[256,512]{1,0:T(8,128)(2,1)S(1)}, bf16[256,512]{1,0:T(8,128)(2,1)S(1)}, u32[]{:S(2)}, u32[]{:S(2)}) collective-permute-start(bf16[256,512]{1,0:T(8,128)(2,1)S(1)} %fusion.5), channel_id=1, source_target_pairs={{0,2},{2,0},{1,3},{3,1},{4,6},{6,4},{5,7},{7,5},{8,10},{10,8},{9,1... | collective-permute-start | bytes 786440 | tf_op jit(solution)/shard_map/ppermute | solution.py:566
  146.6 30.4 %copy-start.1 = (bf16[264,512]{1,0:T(8,128)(2,1)}, bf16[264,512]{1,0:T(8,128)(2,1)S(1)}, u32[]{:S(2)}) copy-start(bf16[264,512]{1,0:T(8,128)(2,1)S(1)} %pad_maximum_fusion.4.refs_0_) | copy-start | bytes 811012
  146.6 8.7 %collective-permute-start.18 = (bf16[264,512]{1,0:T(8,128)(2,1)S(1)}, bf16[264,512]{1,0:T(8,128)(2,1)S(1)}, u32[]{:S(2)}, u32[]{:S(2)}) collective-permute-start(bf16[264,512]{1,0:T(8,128)(2,1)S(1)} %pad_maximum_fusion.4.refs_0_), channel_id=1, source_target_pairs={{0,28},{4,0},{8,4},{12,8},{16,12},{20,16},{24,20},{28,24},{1,29},{... | collective-permute-start | bytes 811016 | tf_op jit(solution)/shard_map/ppermute | solution.py:39
  149.9 9.1 %collective-permute-start.25 = (bf16[264,512]{1,0:T(8,128)(2,1)S(1)}, bf16[264,512]{1,0:T(8,128)(2,1)S(1)}, u32[]{:S(2)}, u32[]{:S(2)}) collective-permute-start(bf16[264,512]{1,0:T(8,128)(2,1)S(1)} %pad_maximum_fusion.4.refs_0_), channel_id=1, source_target_pairs={{0,4},{4,8},{8,12},{12,16},{16,20},{20,24},{24,28},{28,0},{1,5},{5... | collective-permute-start | bytes 811016 | tf_op jit(solution)/shard_map/ppermute | solution.py:42
  155.3 21.7 %copy-start.7 = (bf16[264,512]{1,0:T(8,128)(2,1)}, bf16[264,512]{1,0:T(8,128)(2,1)S(1)}, u32[]{:S(2)}) copy-start(bf16[264,512]{1,0:T(8,128)(2,1)S(1)} %collective-permute-done.18.refs_1_) | copy-start | bytes 811012
  155.3 10.3 %collective-permute-start.19 = (bf16[264,512]{1,0:T(8,128)(2,1)S(1)}, bf16[264,512]{1,0:T(8,128)(2,1)S(1)}, u32[]{:S(2)}, u32[]{:S(2)}) collective-permute-start(bf16[264,512]{1,0:T(8,128)(2,1)S(1)} %collective-permute-done.18.refs_1_), channel_id=1, source_target_pairs={{0,28},{4,0},{8,4},{12,8},{16,12},{20,16},{24,20},{28,24},{1,29},{... | collective-permute-start | bytes 811016 | tf_op jit(solution)/shard_map/ppermute | solution.py:39
  159.0 18.0 %copy-start.8 = (bf16[264,512]{1,0:T(8,128)(2,1)}, bf16[264,512]{1,0:T(8,128)(2,1)S(1)}, u32[]{:S(2)}) copy-start(bf16[264,512]{1,0:T(8,128)(2,1)S(1)} %collective-permute-done.25.refs_2_) | copy-start | bytes 811012
  159.0 10.3 %collective-permute-start.26 = (bf16[264,512]{1,0:T(8,128)(2,1)S(1)}, bf16[264,512]{1,0:T(8,128)(2,1)S(1)}, u32[]{:S(2)}, u32[]{:S(2)}) collective-permute-start(bf16[264,512]{1,0:T(8,128)(2,1)S(1)} %collective-permute-done.25.refs_2_), channel_id=1, source_target_pairs={{0,4},{4,8},{8,12},{12,16},{16,20},{20,24},{24,28},{28,0},{1,5},{5... | collective-permute-start | bytes 811016 | tf_op jit(solution)/shard_map/ppermute | solution.py:42
  165.6 16.0 %copy-start.12 = (bf16[264,512]{1,0:T(8,128)(2,1)}, bf16[264,512]{1,0:T(8,128)(2,1)S(1)}, u32[]{:S(2)}) copy-start(bf16[264,512]{1,0:T(8,128)(2,1)S(1)} %collective-permute-done.19.refs_0_) | copy-start | bytes 811012
  165.6 7.7 %collective-permute-start.20 = (bf16[264,512]{1,0:T(8,128)(2,1)S(1)}, bf16[264,512]{1,0:T(8,128)(2,1)S(1)}, u32[]{:S(2)}, u32[]{:S(2)}) collective-permute-start(bf16[264,512]{1,0:T(8,128)(2,1)S(1)} %collective-permute-done.19.refs_0_), channel_id=1, source_target_pairs={{0,28},{4,0},{8,4},{12,8},{16,12},{20,16},{24,20},{28,24},{1,29},{... | collective-permute-start | bytes 811016 | tf_op jit(solution)/shard_map/ppermute | solution.py:39
  169.3 12.3 %copy-start.13 = (bf16[264,512]{1,0:T(8,128)(2,1)}, bf16[264,512]{1,0:T(8,128)(2,1)S(1)}, u32[]{:S(2)}) copy-start(bf16[264,512]{1,0:T(8,128)(2,1)S(1)} %collective-permute-done.26.refs_1_) | copy-start | bytes 811012
  169.3 12.3 %collective-permute-start.27 = (bf16[264,512]{1,0:T(8,128)(2,1)S(1)}, bf16[264,512]{1,0:T(8,128)(2,1)S(1)}, u32[]{:S(2)}, u32[]{:S(2)}) collective-permute-start(bf16[264,512]{1,0:T(8,128)(2,1)S(1)} %collective-permute-done.26.refs_1_), channel_id=1, source_target_pairs={{0,4},{4,8},{8,12},{12,16},{16,20},{20,24},{24,28},{28,0},{1,5},{5... | collective-permute-start | bytes 811016 | tf_op jit(solution)/shard_map/ppermute | solution.py:42
  173.3 8.3 %copy-start.14 = (bf16[264,512]{1,0:T(8,128)(2,1)}, bf16[264,512]{1,0:T(8,128)(2,1)S(1)}, u32[]{:S(2)}) copy-start(bf16[264,512]{1,0:T(8,128)(2,1)S(1)} %collective-permute-done.20.refs_2_) | copy-start | bytes 811012
  173.3 15.7 %collective-permute-start.21 = (bf16[264,512]{1,0:T(8,128)(2,1)S(1)}, bf16[264,512]{1,0:T(8,128)(2,1)S(1)}, u32[]{:S(2)}, u32[]{:S(2)}) collective-permute-start(bf16[264,512]{1,0:T(8,128)(2,1)S(1)} %collective-permute-done.20.refs_2_), channel_id=1, source_target_pairs={{0,28},{4,0},{8,4},{12,8},{16,12},{20,16},{24,20},{28,24},{1,29},{... | collective-permute-start | bytes 811016 | tf_op jit(solution)/shard_map/ppermute | solution.py:39
  181.6 0.7 copy-start.15
  189.0 0.7 copy-start.9
  193.5 8.2 %collective-permute-start.28 = (bf16[256,512]{1,0:T(8,128)(2,1)}, bf16[256,512]{1,0:T(8,128)(2,1)S(1)}, u32[]{:S(2)}, u32[]{:S(2)}) collective-permute-start(bf16[256,512]{1,0:T(8,128)(2,1)} %hidden.1.hidden_ref), channel_id=1, source_target_pairs={{0,2},{2,0},{1,3},{3,1},{4,6},{6,4},{5,7},{7,5},{8,10},{10,8},{9,1... | collective-permute-start | bytes 786440 | tf_op jit(solution)/shard_map/ppermute | solution.py:453
  201.6 0.7 copy-start.16
  208.4 7.3 %collective-permute-start.29 = (bf16[256,256]{1,0:T(8,128)(2,1)}, bf16[256,256]{1,0:T(8,128)(2,1)S(1)}, u32[]{:S(2)}, u32[]{:S(2)}) collective-permute-start(bf16[256,256]{1,0:T(8,128)(2,1)} %get-tuple-element.30), channel_id=1, source_target_pairs={{0,4},{4,8},{8,12},{12,16},{16,20},{20,24},{24,28},{28,0},{1,5},{5... | collective-permute-start | bytes 393224 | tf_op jit(solution)/shard_map/ppermute | solution.py:59
  208.4 8.2 %collective-permute-start.33 = (bf16[256,256]{1,0:T(8,128)(2,1)}, bf16[256,256]{1,0:T(8,128)(2,1)S(1)}, u32[]{:S(2)}, u32[]{:S(2)}) collective-permute-start(bf16[256,256]{1,0:T(8,128)(2,1)} %get-tuple-element.32), channel_id=1, source_target_pairs={{0,28},{4,0},{8,4},{12,8},{16,12},{20,16},{24,20},{28,24},{1,29},{... | collective-permute-start | bytes 393224 | tf_op jit(solution)/shard_map/ppermute | solution.py:61
  216.6 6.3 %collective-permute-start.30 = (bf16[256,256]{1,0:T(8,128)(2,1)S(1)}, bf16[256,256]{1,0:T(8,128)(2,1)S(1)}, u32[]{:S(2)}, u32[]{:S(2)}) collective-permute-start(bf16[256,256]{1,0:T(8,128)(2,1)S(1)} %fusion.17), channel_id=1, source_target_pairs={{0,4},{4,8},{8,12},{12,16},{16,20},{20,24},{24,28},{28,0},{1,5},{5... | collective-permute-start | bytes 393224 | tf_op jit(solution)/shard_map/ppermute | solution.py:59
  223.9 6.3 %collective-permute-start.31 = (bf16[256,256]{1,0:T(8,128)(2,1)S(1)}, bf16[256,256]{1,0:T(8,128)(2,1)S(1)}, u32[]{:S(2)}, u32[]{:S(2)}) collective-permute-start(bf16[256,256]{1,0:T(8,128)(2,1)S(1)} %get-tuple-element.43), channel_id=1, source_target_pairs={{0,4},{4,8},{8,12},{12,16},{16,20},{20,24},{24,28},{28,0},{1,5},{5... | collective-permute-start | bytes 393224 | tf_op jit(solution)/shard_map/ppermute | solution.py:59
  224.0 6.2 %collective-permute-start.34 = (bf16[256,256]{1,0:T(8,128)(2,1)S(1)}, bf16[256,256]{1,0:T(8,128)(2,1)S(1)}, u32[]{:S(2)}, u32[]{:S(2)}) collective-permute-start(bf16[256,256]{1,0:T(8,128)(2,1)S(1)} %get-tuple-element.44), channel_id=1, source_target_pairs={{0,28},{4,0},{8,4},{12,8},{16,12},{20,16},{24,20},{28,24},{1,29},{... | collective-permute-start | bytes 393224 | tf_op jit(solution)/shard_map/ppermute | solution.py:61
  231.2 6.3 %collective-permute-start.32 = (bf16[256,256]{1,0:T(8,128)(2,1)S(1)}, bf16[256,256]{1,0:T(8,128)(2,1)S(1)}, u32[]{:S(2)}, u32[]{:S(2)}) collective-permute-start(bf16[256,256]{1,0:T(8,128)(2,1)S(1)} %get-tuple-element.41), channel_id=1, source_target_pairs={{0,4},{4,8},{8,12},{12,16},{16,20},{20,24},{24,28},{28,0},{1,5},{5... | collective-permute-start | bytes 393224 | tf_op jit(solution)/shard_map/ppermute | solution.py:59
  231.3 6.2 %collective-permute-start.35 = (bf16[256,256]{1,0:T(8,128)(2,1)S(1)}, bf16[256,256]{1,0:T(8,128)(2,1)S(1)}, u32[]{:S(2)}, u32[]{:S(2)}) collective-permute-start(bf16[256,256]{1,0:T(8,128)(2,1)S(1)} %get-tuple-element.42), channel_id=1, source_target_pairs={{0,28},{4,0},{8,4},{12,8},{16,12},{20,16},{24,20},{28,24},{1,29},{... | collective-permute-start | bytes 393224 | tf_op jit(solution)/shard_map/ppermute | solution.py:61
Sparse Core Ops, SparseCore 0:
  20.4 32.1 all-gather.3
  100.8 43.0 all-gather.5

commit v2 on v1

--- a/solution.py
+++ b/solution.py
@@ -111,9 +111,9 @@
     ring_at, half = lax.axis_index("ma_0"), lax.axis_index("row")
     blocks = refs[:RING]
     own = refs[RING : RING + 3]
-    other_ref, own_out_ref, other_out_ref, bias_ref = refs[RING + 3 : RING + 7]
-    out_refs = refs[RING + 7 : RING + 10]
-    x_ref, w_ref, o_ref, acc_ref, attended_ref, both_ref = refs[RING + 10 : RING + 16]
+    other_ref, *out_weight_refs, bias_ref = refs[RING + 3 : RING + 8]
+    first_ref, second_ref, attended_ref = refs[RING + 8 : RING + 11]
+    x_ref, w_ref, o_ref, acc_ref, both_ref = refs[RING + 11 : RING + 16]
     x_sem, own_sem, other_sem, o_sem = refs[RING + 16 :]
     length = acc_ref.shape[0]
     inner = attended_ref.shape[1]
@@ -138,10 +138,7 @@
         )
         for k in range(parts)
     ]
-    o_copies = [
-        pltpu.make_async_copy(ref, o_ref.at[k], o_sem.at[k])
-        for k, ref in enumerate((own_out_ref, other_out_ref))
-    ]
+    o_copies = out_weight_copies(out_weight_refs, o_ref, o_sem)
     for copy in x_copies + own_copies + other_copies + o_copies:
         copy.start()
     for copy in x_copies:
@@ -198,21 +195,47 @@
     for copy in o_copies:
         copy.wait()
 
-    def out_block(owner):
-        slot = lax.rem(ring_at + owner + half * parts, RING)
-        which = slot // parts
-        column = pl.multiple_of((slot - which * parts) * wide, wide)
-        product = dot(attended_ref[...], o_ref[which, :, pl.ds(column, wide)])
-        return product.astype(jnp.bfloat16)
-
-    store_blocks(out_block, out_refs)
-
-
-def store_blocks(block, out_refs):
-    first_ref, second_ref, rest_ref = out_refs
-    first_ref[...] = block(SEND[0])
-    second_ref[...] = block(SEND[1])
-
+    first_ref[...] = out_block(SEND[0], attended_ref, o_ref)
+    second_ref[...] = out_block(SEND[1], attended_ref, o_ref)
+
+
+def out_weight_copies(refs, o_ref, o_sem):
+    width = refs[1].shape[1]
+    core = lax.rem(lax.axis_index("ba"), 2)
+    targets = [
+        o_ref.at[0],
+        o_ref.at[1, :, pl.ds(pl.multiple_of(core * width, width), width)],
+        o_ref.at[1, :, pl.ds(pl.multiple_of((1 - core) * width, width), width)],
+    ]
+    return [
+        pltpu.make_async_copy(ref, target, o_sem.at[k])
+        for k, (ref, target) in enumerate(zip(refs, targets))
+    ]
+
+
+def out_block(owner, attended_ref, o_ref):
+    ring_at, half = lax.axis_index("ma_0"), lax.axis_index("row")
+    parts = RING // 2
+    wide = o_ref.shape[2] // parts
+    slot = lax.rem(ring_at + owner + half * parts, RING)
+    which = slot // parts
+    column = pl.multiple_of((slot - which * parts) * wide, wide)
+    product = dot(attended_ref[...], o_ref[which, :, pl.ds(column, wide)])
+    return product.astype(jnp.bfloat16)
+
+
+def out_rest_kernel(*refs):
+    out_weight_refs = refs[1:4]
+    attended_ref, rest_ref, o_ref, o_sem = refs[0], *refs[4:]
+    copies = out_weight_copies(out_weight_refs, o_ref, o_sem)
+    for copy in copies:
+        copy.start()
+    for copy in copies:
+        copy.wait()
+    store_rest(lambda owner: out_block(owner, attended_ref, o_ref), rest_ref)
+
+
+def store_rest(block, rest_ref):
     def store(k, unused):
         rest_ref[k] = block(jnp.where(k < 4, k, k + 2))
         return unused
@@ -220,37 +243,43 @@
     lax.fori_loop(0, RING - 2, store, 0)
 
 
-def block_shapes(length, width):
-    one = jax.ShapeDtypeStruct((length, width), jnp.bfloat16)
-    return [one, one, jax.ShapeDtypeStruct((RING - 2, length, width), jnp.bfloat16)]
+def one_block(length, width):
+    return jax.ShapeDtypeStruct((length, width), jnp.bfloat16)
+
+
+def rest_blocks(length, width):
+    return jax.ShapeDtypeStruct((RING - 2, length, width), jnp.bfloat16)
 
 
 ANY = pl.BlockSpec(memory_space=pl.ANY)
 IN_VMEM = pl.BlockSpec(memory_space=pltpu.VMEM)
 
 
-def attention(held, bias, own, other, own_out, other_out):
+def attention(held, bias, own, other, out_weights):
     length = bias.shape[1]
     inner = own[0].shape[1]
     rows, wide = held[0].shape
     parts = RING // 2
-    return pl.pallas_call(
+    out_scratch = [
+        pltpu.VMEM((2, *out_weights[0].shape), jnp.bfloat16),
+        pltpu.SemaphoreType.DMA((3,)),
+    ]
+    first, second, attended = pl.pallas_call(
         functools.partial(attention_kernel, float(wide * RING)),
-        in_specs=[ANY] * (RING + 6) + [IN_VMEM],
+        in_specs=[ANY] * (RING + 7) + [IN_VMEM],
         out_specs=[IN_VMEM] * 3,
         scratch_shapes=[
             pltpu.VMEM((RING, rows, wide), jnp.bfloat16),
             pltpu.VMEM((RING * wide, 3 * inner), jnp.bfloat16),
-            pltpu.VMEM((2, *own_out.shape), jnp.bfloat16),
+            out_scratch[0],
             pltpu.VMEM((length, 3 * inner), jnp.float32),
-            pltpu.VMEM((length, inner), jnp.bfloat16),
             pltpu.VMEM((length, 2 * inner // bias.shape[0]), jnp.bfloat16),
             pltpu.SemaphoreType.DMA((RING,)),
             pltpu.SemaphoreType.DMA((3,)),
             pltpu.SemaphoreType.DMA((parts,)),
-            pltpu.SemaphoreType.DMA((2,)),
+            out_scratch[1],
         ],
-        out_shape=block_shapes(length, wide),
+        out_shape=[one_block(length, wide)] * 2 + [one_block(length, inner)],
         cost_estimate=pl.CostEstimate(
             flops=2 * length * wide * RING * 4 * inner, bytes_accessed=10**7, transcendentals=0
         ),
@@ -259,14 +288,28 @@
         *[held[k] for k in range(RING)],
         *own,
         other,
-        own_out,
-        other_out,
+        *out_weights,
         bias,
     )
+    rest = pl.pallas_call(
+        out_rest_kernel,
+        in_specs=[IN_VMEM] + [ANY] * 3,
+        out_specs=IN_VMEM,
+        scratch_shapes=out_scratch,
+        out_shape=rest_blocks(length, wide),
+        cost_estimate=pl.CostEstimate(
+            flops=2 * length * inner * wide * (RING - 2),
+            bytes_accessed=4 * 10**6,
+            transcendentals=0,
+        ),
+        name="out_rest",
+    )(attended, *out_weights)
+    return first, second, rest
 
 
 FIRST = (0, 1, 7)
-SECOND = (2, 6, 3, 5)
+SECOND = (2, 6)
+THIRD = (3, 5)
 LAST = (4,)
 
 
@@ -347,61 +390,49 @@
         ).astype(jnp.bfloat16)
 
 
-def down_copies(first_refs, d_ref, d_sem):
+def down_copies(owners, down_ref, other_ref, d_ref, d_sem):
+    ring_at, pair_at = lax.axis_index("ma_0"), lax.axis_index("ma_1")
+    part = d_ref.shape[2]
+    size = down_ref.shape[0]
     copies = []
-    ring_at = lax.axis_index("ma_0")
-    for j in range(RING):
-        slot = lax.rem(ring_at + j, RING)
-        for n, source in enumerate(first_refs(slot)):
-            rows = source.shape[0]
+    for j, owner in enumerate(owners):
+        slot = lax.rem(ring_at + owner, RING)
+        column = pl.multiple_of((slot * 2 + pair_at) * part, part)
+        sources = [down_ref.at[:, pl.ds(column, part)]]
+        sources += [other_ref.at[slot, pl.ds(n * size, size), :] for n in (4, 6, 5)]
+        for n, source in enumerate(sources):
             copies.append(
-                pltpu.make_async_copy(source, d_ref.at[j, pl.ds(n * rows, rows), :], d_sem.at[j, n])
+                pltpu.make_async_copy(source, d_ref.at[j, pl.ds(n * size, size), :], d_sem.at[j, n])
             )
     return copies
 
 
-def own_down_kernel(hidden_ref, down_ref, other_ref, out_ref, d_ref, d_sem):
-    size = d_ref.shape[1] // 2
-    part = d_ref.shape[2]
-    pair_at = lax.axis_index("ma_1")
-
-    def sources(slot):
-        column = pl.multiple_of((slot * 2 + pair_at) * part, part)
-        return down_ref.at[:, pl.ds(column, part)], other_ref.at[slot, pl.ds(4 * size, size), :]
-
-    copies = down_copies(sources, d_ref, d_sem)
+def down_kernel(owners, mine_ref, theirs_ref, down_ref, other_ref, *refs):
+    *out_refs, h_ref, d_ref, h_sem, d_sem = refs
+    copies = [
+        pltpu.make_async_copy(ref, h_ref.at[k], h_sem.at[k])
+        for k, ref in enumerate((mine_ref, theirs_ref))
+    ] + down_copies(owners, down_ref, other_ref, d_ref, d_sem)
     for copy in copies:
         copy.start()
     for copy in copies:
         copy.wait()
-
-    def block(j, unused):
-        out_ref[j] = dot(hidden_ref[...], d_ref[j])
+    rows = h_ref.shape[2]
+
+    def block(j):
+        product = dot(h_ref[0], d_ref[j, :rows, :]) + dot(h_ref[1], d_ref[j, rows:, :])
+        return product.astype(jnp.bfloat16)
+
+    if len(out_refs) > 1:
+        for j, out_ref in enumerate(out_refs):
+            out_ref[...] = block(j)
+        return
+
+    def store(j, unused):
+        out_refs[0][j] = block(j)
         return unused
 
-    lax.fori_loop(0, RING, block, 0)
-
-
-def pair_down_kernel(hidden_ref, other_ref, own_ref, *refs):
-    out_refs, (d_ref, own_in_ref, d_sem, own_sem) = refs[:3], refs[3:]
-    size = d_ref.shape[1] // 2
-    own_copy = pltpu.make_async_copy(own_ref, own_in_ref, own_sem)
-    own_copy.start()
-
-    def sources(slot):
-        return [other_ref.at[slot, pl.ds((5 + n) * size, size), :] for n in range(2)]
-
-    copies = down_copies(sources, d_ref, d_sem)
-    for copy in copies:
-        copy.start()
-    own_copy.wait()
-    for copy in copies:
-        copy.wait()
-
-    def block(owner):
-        return (own_in_ref[owner] + dot(hidden_ref[...], d_ref[owner])).astype(jnp.bfloat16)
-
-    store_blocks(block, out_refs)
+    lax.fori_loop(0, len(owners), store, 0)
 
 
 def feed_forward(held, gate, up, down, other):
@@ -441,6 +472,7 @@
 
     before = gate_sums(FIRST, ())
     before = gate_sums(SECOND, before)
+    before = gate_sums(THIRD, before)
     mine = pl.pallas_call(
         functools.partial(hidden_kernel, float(wide * RING)),
         in_specs=[ANY] * (len(LAST) + 3) + [IN_VMEM] * 2,
@@ -451,33 +483,25 @@
         name="hidden",
     )(*[held[k] for k in LAST], gate, up, other, *before)
     theirs = lax.ppermute(mine, "ma_1", SWAP)
-    weights = [
-        pltpu.VMEM((RING, 2 * hidden, part), jnp.bfloat16),
-        pltpu.SemaphoreType.DMA((RING, 2)),
-    ]
-    own = pl.pallas_call(
-        own_down_kernel,
-        in_specs=[IN_VMEM, ANY, ANY],
-        out_specs=IN_VMEM,
-        scratch_shapes=weights,
-        out_shape=jax.ShapeDtypeStruct((RING, length, part), jnp.float32),
-        cost_estimate=cost(2),
-        name="own_down",
-    )(mine, down, other)
-    return pl.pallas_call(
-        pair_down_kernel,
-        in_specs=[IN_VMEM, ANY, ANY],
-        out_specs=[IN_VMEM] * 3,
-        scratch_shapes=[
-            weights[0],
-            pltpu.VMEM((RING, length, part), jnp.float32),
-            weights[1],
-            pltpu.SemaphoreType.DMA,
-        ],
-        out_shape=block_shapes(length, part),
-        cost_estimate=cost(2),
-        name="pair_down",
-    )(theirs, other, own)
+
+    def down_blocks(owners, shapes):
+        return pl.pallas_call(
+            functools.partial(down_kernel, owners),
+            in_specs=[ANY] * 4,
+            out_specs=[IN_VMEM] * len(shapes),
+            scratch_shapes=[
+                pltpu.VMEM((2, length, 2 * hidden), jnp.bfloat16),
+                pltpu.VMEM((len(owners), 4 * hidden, part), jnp.bfloat16),
+                pltpu.SemaphoreType.DMA((2,)),
+                pltpu.SemaphoreType.DMA((len(owners), 4)),
+            ],
+            out_shape=shapes,
+            cost_estimate=cost(1),
+        )(mine, theirs, down, other)
+
+    first, second = down_blocks(SEND[:2], [one_block(length, part)] * 2)
+    (rest,) = down_blocks(SEND[2:], [rest_blocks(length, part)])
+    return first, second, rest
 
 
 def spread(values, gain):
@@ -523,8 +547,6 @@
     ]
     first_share = lax.ppermute(jnp.concatenate(share, axis=1), "row", SWAP)
     other_first = lax.all_gather(first_share, "ba", axis=0, tiled=True)
-    other_out = lax.ppermute(tied(attention_output_matrix, theirs), "row", SWAP)
-
     gate_depth = gate_weight.shape[0] // copies
     gate_share = [
         lax.dynamic_slice_in_dim(w, copy_at * gate_depth, gate_depth, 0)
@@ -537,30 +559,32 @@
         at = copy_at * down_width + pair * part
         return lax.dynamic_slice_in_dim(down_projection_weight, at, part, 1)
 
-    row_share = jnp.concatenate([*gate_share, down_share(pair_at)], axis=0)
-    pair_share = down_share(1 - pair_at)
-
     wide = pair_order(mine, theirs, 1)
     wide_tokens = wide[:length]
     wide_attn_gain = wide[length]
     wide_ffn_gain = wide[length + 1]
 
     held = spread(wide_tokens, wide_attn_gain)
-    row_share = lax.ppermute(tied(row_share, held[1]), "row", SWAP)
-    pair_share = tied(pair_share, held[2])
-    cross = [(0, 3), (3, 0), (1, 2), (2, 1)]
-    cross_share = lax.ppermute(pair_share, ("ma_1", "row"), cross)
+    core_width = attention_output_matrix.shape[1] // 2
+    core_out = lax.dynamic_slice_in_dim(
+        attention_output_matrix, jnp.mod(copy_at, 2) * core_width, core_width, 1
+    )
+    core_out = lax.ppermute(tied(core_out, held[1]), "row", SWAP)
+    cores = [(k, k ^ 1) for k in range(copies)]
+    other_core_out = lax.ppermute(core_out, "ba", cores)
+    pair_share = tied(down_share(1 - pair_at), held[1])
     pair_share = lax.ppermute(pair_share, "ma_1", SWAP)
+    row_share = jnp.concatenate([*gate_share, down_share(pair_at), pair_share], axis=0)
+    row_share = lax.ppermute(tied(row_share, held[2]), "row", SWAP)
     out_blocks = attention(
         held,
         position_bias(bucket_bias_matrix, length),
         (query_weight, key_weight, value_projection_matrix),
         other_first,
-        attention_output_matrix,
-        other_out,
-    )
-    second_share = jnp.concatenate([row_share, pair_share, cross_share], axis=0)
-    second_share = tied(second_share, out_blocks[0])
+        (attention_output_matrix, core_out, other_core_out),
+    )
+    row_share = tied(row_share, out_blocks[0])
+    second_share = jnp.concatenate([row_share, pair_share], axis=0)
     other_second = lax.all_gather(second_share, "ba", axis=0, tiled=False)
     summed = ring_sum(*out_blocks).astype(jnp.bfloat16)
     partner = lax.ppermute(summed, "ma_1", SWAP)
@@ -571,7 +595,7 @@
 
     held = spread(residual, wide_ffn_gain)
     summed = ring_sum(
-        *feed_forward(held, gate_weight, up_weight, down_projection_weight, other_second)
+        *feed_forward(held, gate_weight, up_weight, down_projection_weight, other_second),
     )
     encoded = own_residual.astype(jnp.float32) + summed
     return encoded.astype(jnp.bfloat16).reshape(sequences, length, part)

time: 246 us -> 232 us (0.943)
  waiting for transfers between devices: 105 us -> 93.9 us
  starting transfers between devices: 65.8 us -> 61.5 us
    ppermute x1, waiting for transfers between devices: 22.8 us -> 7.56 us  [layer(): pair_share = lax.ppermute(pair_share, 'ma_1', SWAP)]
    ppermute x8, waiting for transfers between devices: 41.8 us -> 31.6 us  [ring_sum(): got_up = lax.ppermute(up, 'ma_0', UP)]
    ppermute x6, waiting for transfers between devices: 1.2 us -> 7.39 us  [ring_gather(): below = lax.ppermute(below, 'ma_0', UP)]
    ppermute x1, waiting for transfers between devices: 2.15 us -> 8.07 us  [feed_forward(): theirs = lax.ppermute(mine, 'ma_1', SWAP)]
    ppermute x3, starting transfers between devices: 5.78 us -> 1.76 us  [the longest x1 1.58 us: layer(): core_out = lax.ppermute(tied(core_out, held[1]), 'row', SWAP)]
    pallas_call x2 -> x3, Pallas kernels: 11.2 us -> 14.3 us  [gate_sums(): pl.pallas_call(functools.partial(gate_kernel, owners, bool(before)), in_s...]
    pallas_call x2 -> x3, Pallas kernels: 11.9 us -> 12.8 us  [the longest x2 7.79 us: down_blocks(): pl.pallas_call(functools.partial(down_kernel, owners), in_specs=[ANY] * 4...]
  transfers between devices with their start and end apart: 38 -> 38, of which waited for: 19 -> 18; matrix products, arithmetic and copies ran while one was open for 4% -> 3% of each run, Pallas kernels for 8% -> 16%
where the time goes in v2:
time: 232 us
  waiting for transfers between devices  93.9 us (40%)
  starting transfers between devices  61.5 us (27%)
  Pallas kernels  44.1 us (19%)
  between operations  14 us (6%)
  local copies, waits for them, and re-layouts  9.25 us (4%)
  other arithmetic  8.96 us (4%)
    ppermute x8, waiting for transfers between devices, ring_sum(): got_up = lax.ppermute(up, 'ma_0', UP)  31.6 us
    ppermute x8, starting transfers between devices, ring_gather(): above = lax.ppermute(above, 'ma_0', DOWN)  30.6 us
    ppermute x6, starting transfers between devices, ring_sum(): got_down = lax.ppermute(down, 'ma_0', DOWN)  19.9 us
    ppermute x8, waiting for transfers between devices, ring_gather(): above = lax.ppermute(above, 'ma_0', DOWN)  18.8 us
    pallas_call x3, Pallas kernels, gate_sums(): pl.pallas_call(functools.partial(gate_kernel, owners, bool(before)), in_s...  14.3 us
    pallas_call x1, Pallas kernels, attention(): pl.pallas_call(functools.partial(attention_kernel, float(wide * RING)), i...  11.1 us
    ppermute x1, waiting for transfers between devices, layer(): first_share = lax.ppermute(jnp.concatenate(share, axis=1), 'row', SWAP)  9.28 us
    ppermute x1, waiting for transfers between devices, feed_forward(): theirs = lax.ppermute(mine, 'ma_1', SWAP)  8.07 us
  transfers between devices with their start and end apart: 38, of which 18 were waited for; matrix products, arithmetic and copies ran while one was open for 3% of the time, Pallas kernels for 16%

profile of v2, /device:TPU:2, one launch (start us, length us, event | category | flops | bytes accessed | tf_op | source)
XLA Modules:
  0.0 231.7 jit_solution(1317057113526863749)
XLA Ops:
  6.5 0.9 constant_dynamic-slice_fusion.7
  7.5 1.0 constant_dynamic-slice_fusion.5
  8.5 1.7 collective-permute-start.8
  10.2 9.3 %collective-permute-done.8 = bf16[256,768]{1,0:T(8,128)(2,1)S(1)} collective-permute-done((bf16[256,768]{1,0:T(8,128)(2,1)S(1)}, bf16[256,768]{1,0:T(8,128)(2,1)S(1)}, u32[]{:S(2)}, u32[]{:S(2)}) %collective-permute-start.8) | collective-permute-done | bytes 393248 | tf_op jit(solution)/shard_map/ppermute | solution.py:548
  19.5 0.7 copy-done.8
  20.4 3.3 %collective-permute-start = (bf16[264,256]{1,0:T(8,128)(2,1)S(1)}, bf16[264,256]{1,0:T(8,128)(2,1)S(1)}, u32[]{:S(2)}, u32[]{:S(2)}) collective-permute-start(bf16[264,256]{1,0:T(8,128)(2,1)S(1)} %pad_maximum_fusion.5), channel_id=1, source_target_pairs={{0,2},{2,0},{1,3},{3,1},{4,6},{6,4},{5,7},{7,5},{8,10},{10,8},{9,1... | collective-permute-start | bytes 405512 | tf_op jit(solution)/shard_map/ppermute | solution.py:540
  23.7 3.3 %collective-permute-done = bf16[264,256]{1,0:T(8,128)(2,1)S(1)} collective-permute-done((bf16[264,256]{1,0:T(8,128)(2,1)S(1)}, bf16[264,256]{1,0:T(8,128)(2,1)S(1)}, u32[]{:S(2)}, u32[]{:S(2)}) %collective-permute-start) | collective-permute-done | bytes 135200 | tf_op jit(solution)/shard_map/ppermute | solution.py:540
  27.4 5.9 %collective-permute-start.1 = (bf16[264,512]{1,0:T(8,128)(2,1)S(1)}, bf16[264,512]{1,0:T(8,128)(2,1)S(1)}, u32[]{:S(2)}, u32[]{:S(2)}) collective-permute-start(bf16[264,512]{1,0:T(8,128)(2,1)S(1)} %pad_maximum_fusion.3.refs_0_), channel_id=1, source_target_pairs={{0,28},{4,0},{8,4},{12,8},{16,12},{20,16},{24,20},{28,24},{1,29},{... | collective-permute-start | bytes 811016 | tf_op jit(solution)/shard_map/ppermute | solution.py:39
  33.3 0.9 constant_dynamic-slice_fusion.4
  34.1 3.1 %collective-permute-done.1.refs_1_ = bf16[264,512]{1,0:T(8,128)(2,1)S(1)} collective-permute-done((bf16[264,512]{1,0:T(8,128)(2,1)S(1)}, bf16[264,512]{1,0:T(8,128)(2,1)S(1)}, u32[]{:S(2)}, u32[]{:S(2)}) %collective-permute-start.1) | collective-permute-done | bytes 270368 | tf_op jit(solution)/shard_map/ppermute | solution.py:39
  37.3 1.6 collective-permute-start.9
  38.8 1.0 constant_dynamic-slice_fusion.1
  39.8 3.0 %collective-permute-start.23 = (bf16[256,256]{1,0:T(8,128)(2,1)S(1)}, bf16[256,256]{1,0:T(8,128)(2,1)S(1)}, u32[]{:S(2)}, u32[]{:S(2)}) collective-permute-start(bf16[256,256]{1,0:T(8,128)(2,1)S(1)} %get-tuple-element.24), channel_id=1, source_target_pairs={{0,2},{2,0},{1,3},{3,1},{4,6},{6,4},{5,7},{7,5},{8,10},{10,8},{9,1... | collective-permute-start | bytes 393224 | tf_op jit(solution)/shard_map/ppermute | solution.py:576
  42.8 3.7 %collective-permute-start.2 = (bf16[264,512]{1,0:T(8,128)(2,1)S(1)}, bf16[264,512]{1,0:T(8,128)(2,1)S(1)}, u32[]{:S(2)}, u32[]{:S(2)}) collective-permute-start(bf16[264,512]{1,0:T(8,128)(2,1)S(1)} %collective-permute-done.1.refs_1_), channel_id=1, source_target_pairs={{0,28},{4,0},{8,4},{12,8},{16,12},{20,16},{24,20},{28,24},{1,29},{... | collective-permute-start | bytes 811016 | tf_op jit(solution)/shard_map/ppermute | solution.py:39
  46.5 1.1 constant_dynamic-slice_fusion.2
  47.7 7.6 %collective-permute-done.23 = bf16[256,256]{1,0:T(8,128)(2,1)S(1)} collective-permute-done((bf16[256,256]{1,0:T(8,128)(2,1)S(1)}, bf16[256,256]{1,0:T(8,128)(2,1)S(1)}, u32[]{:S(2)}, u32[]{:S(2)}) %collective-permute-start.23) | collective-permute-done | bytes 131104 | tf_op jit(solution)/shard_map/ppermute | solution.py:576
  55.5 1.4 collective-permute-done.5.refs_7_
  56.9 3.2 %collective-permute-start.3 = (bf16[264,512]{1,0:T(8,128)(2,1)S(1)}, bf16[264,512]{1,0:T(8,128)(2,1)}, u32[]{:S(2)}, u32[]{:S(2)}) collective-permute-start(bf16[264,512]{1,0:T(8,128)(2,1)S(1)} %collective-permute-done.2.refs_2_), channel_id=1, source_target_pairs={{0,28},{4,0},{8,4},{12,8},{16,12},{20,16},{24,20},{28,24},{1,29},{... | collective-permute-start | bytes 811016 | tf_op jit(solution)/shard_map/ppermute | solution.py:39
  60.2 4.4 %collective-permute-done.6.refs_6_ = bf16[264,512]{1,0:T(8,128)(2,1)S(1)} collective-permute-done((bf16[264,512]{1,0:T(8,128)(2,1)S(1)}, bf16[264,512]{1,0:T(8,128)(2,1)S(1)}, u32[]{:S(2)}, u32[]{:S(2)}) %collective-permute-start.6) | collective-permute-done | bytes 270368 | tf_op jit(solution)/shard_map/ppermute | solution.py:42
  64.6 3.4 %collective-permute-start.4 = (bf16[264,512]{1,0:T(8,128)(2,1)}, bf16[264,512]{1,0:T(8,128)(2,1)}, u32[]{:S(2)}, u32[]{:S(2)}) collective-permute-start(bf16[264,512]{1,0:T(8,128)(2,1)} %collective-permute-done.3.refs_3_), channel_id=1, source_target_pairs={{0,28},{4,0},{8,4},{12,8},{16,12},{20,16},{24,20},{28,24},{1,29},{... | collective-permute-start | bytes 811016 | tf_op jit(solution)/shard_map/ppermute | solution.py:39
  68.0 0.6 broadcast_in_dim.40.bucket_ref
  68.6 2.1 position_bias.1.refs_15_
  70.8 1.6 collective-permute-done.7.refs_5_
  72.4 0.8 copy-done.3
  73.2 11.1 %attention.1 = (bf16[256,512]{1,0:T(8,128)(2,1)}, bf16[256,512]{1,0:T(8,128)(2,1)}, bf16[256,256]{1,0:T(8,128)(2,1)}) custom-call(bf16[264,512]{1,0:T(8,128)(2,1)} %copy-done.5, bf16[264,512]{1,0:T(8,128)(2,1)} %copy-done.16, bf16[264,512]{1,0:T(8,128)(2,1)} %copy-done.17, bf16[264,512]{1,0:T(8,128)(2,1)} %collective-permute-done.3.refs_3_, ...), custom_call_target="tpu_custom_call" | custom-call | flops 2147483648 | bytes 10000000 | tf_op jit(solution)/shard_map/attention/pallas_call | solution.py:267
  84.3 1.0 pad_maximum_fusion
  85.3 0.3 collective-permute-start.11
  85.6 3.7 %collective-permute-start.15 = (bf16[256,512]{1,0:T(8,128)(2,1)S(1)}, bf16[256,512]{1,0:T(8,128)(2,1)S(1)}, u32[]{:S(2)}, u32[]{:S(2)}) collective-permute-start(bf16[256,512]{1,0:T(8,128)(2,1)S(1)} %copy-done.20), channel_id=1, source_target_pairs={{0,28},{4,0},{8,4},{12,8},{16,12},{20,16},{24,20},{28,24},{1,29},{... | collective-permute-start | bytes 786440 | tf_op jit(solution)/shard_map/ppermute | solution.py:61
  89.3 5.0 %out_rest.1 = bf16[6,256,512]{2,1,0:T(8,128)(2,1)} custom-call(bf16[256,256]{1,0:T(8,128)(2,1)} %get-tuple-element.22.refs_0_, bf16[256,2048]{1,0:T(8,128)(2,1)} %refs_1_.2, bf16[256,1024]{1,0:T(8,128)(2,1)} %copy-done.2, bf16[256,1024]{1,0:T(8,128)(2,1)} %copy-done.3), custom_call_target="tpu_custom_call" | custom-call | flops 402653184 | bytes 4000000 | tf_op jit(solution)/shard_map/out_rest/pallas_call | solution.py:294
  94.4 1.2 fusion.10
  95.6 9.2 %collective-permute-done.12 = bf16[256,512]{1,0:T(8,128)(2,1)S(1)} collective-permute-done((bf16[256,512]{1,0:T(8,128)(2,1)S(1)}, bf16[256,512]{1,0:T(8,128)(2,1)S(1)}, u32[]{:S(2)}, u32[]{:S(2)}) %collective-permute-start.12) | collective-permute-done | bytes 262176 | tf_op jit(solution)/shard_map/ppermute | solution.py:59
  104.9 1.2 fusion.9
  106.2 3.2 %collective-permute-start.16 = (bf16[256,512]{1,0:T(8,128)(2,1)S(1)}, bf16[256,512]{1,0:T(8,128)(2,1)S(1)}, u32[]{:S(2)}, u32[]{:S(2)}) collective-permute-start(bf16[256,512]{1,0:T(8,128)(2,1)S(1)} %get-tuple-element.42), channel_id=1, source_target_pairs={{0,28},{4,0},{8,4},{12,8},{16,12},{20,16},{24,20},{28,24},{1,29},{... | collective-permute-start | bytes 786440 | tf_op jit(solution)/shard_map/ppermute | solution.py:61
  109.4 6.1 %collective-permute-done.13 = bf16[256,512]{1,0:T(8,128)(2,1)S(1)} collective-permute-done((bf16[256,512]{1,0:T(8,128)(2,1)S(1)}, bf16[256,512]{1,0:T(8,128)(2,1)S(1)}, u32[]{:S(2)}, u32[]{:S(2)}) %collective-permute-start.13) | collective-permute-done | bytes 262176 | tf_op jit(solution)/shard_map/ppermute | solution.py:59
  115.7 3.2 %collective-permute-start.17 = (bf16[256,512]{1,0:T(8,128)(2,1)S(1)}, bf16[256,512]{1,0:T(8,128)(2,1)S(1)}, u32[]{:S(2)}, u32[]{:S(2)}) collective-permute-start(bf16[256,512]{1,0:T(8,128)(2,1)S(1)} %get-tuple-element.40), channel_id=1, source_target_pairs={{0,28},{4,0},{8,4},{12,8},{16,12},{20,16},{24,20},{28,24},{1,29},{... | collective-permute-start | bytes 786440 | tf_op jit(solution)/shard_map/ppermute | solution.py:61
  118.9 4.3 %collective-permute-done.14 = bf16[256,512]{1,0:T(8,128)(2,1)S(1)} collective-permute-done((bf16[256,512]{1,0:T(8,128)(2,1)S(1)}, bf16[256,512]{1,0:T(8,128)(2,1)S(1)}, u32[]{:S(2)}, u32[]{:S(2)}) %collective-permute-start.14) | collective-permute-done | bytes 262176 | tf_op jit(solution)/shard_map/ppermute | solution.py:59
  123.6 7.8 %collective-permute-done.18 = bf16[256,512]{1,0:T(8,128)(2,1)S(1)} collective-permute-done((bf16[256,512]{1,0:T(8,128)(2,1)S(1)}, bf16[256,512]{1,0:T(8,128)(2,1)S(1)}, u32[]{:S(2)}, u32[]{:S(2)}) %collective-permute-start.18) | collective-permute-done | bytes 262176 | tf_op jit(solution)/shard_map/ppermute | solution.py:590
  131.7 3.3 %collective-permute-start.19 = (bf16[264,512]{1,0:T(8,128)(2,1)S(1)}, bf16[264,512]{1,0:T(8,128)(2,1)S(1)}, u32[]{:S(2)}, u32[]{:S(2)}) collective-permute-start(bf16[264,512]{1,0:T(8,128)(2,1)S(1)} %pad_maximum_fusion.4.refs_0_), channel_id=1, source_target_pairs={{0,28},{4,0},{8,4},{12,8},{16,12},{20,16},{24,20},{28,24},{1,29},{... | collective-permute-start | bytes 811016 | tf_op jit(solution)/shard_map/ppermute | solution.py:39
  135.0 5.3 %collective-permute-done.19.refs_1_ = bf16[264,512]{1,0:T(8,128)(2,1)S(1)} collective-permute-done((bf16[264,512]{1,0:T(8,128)(2,1)S(1)}, bf16[264,512]{1,0:T(8,128)(2,1)S(1)}, u32[]{:S(2)}, u32[]{:S(2)}) %collective-permute-start.19) | collective-permute-done | bytes 270368 | tf_op jit(solution)/shard_map/ppermute | solution.py:39
  140.3 3.7 %collective-permute-start.20 = (bf16[264,512]{1,0:T(8,128)(2,1)S(1)}, bf16[264,512]{1,0:T(8,128)(2,1)S(1)}, u32[]{:S(2)}, u32[]{:S(2)}) collective-permute-start(bf16[264,512]{1,0:T(8,128)(2,1)S(1)} %collective-permute-done.19.refs_1_), channel_id=1, source_target_pairs={{0,28},{4,0},{8,4},{12,8},{16,12},{20,16},{24,20},{28,24},{1,29},{... | collective-permute-start | bytes 811016 | tf_op jit(solution)/shard_map/ppermute | solution.py:39
  144.0 6.4 %collective-permute-done.20.refs_0_ = bf16[264,512]{1,0:T(8,128)(2,1)S(1)} collective-permute-done((bf16[264,512]{1,0:T(8,128)(2,1)S(1)}, bf16[264,512]{1,0:T(8,128)(2,1)S(1)}, u32[]{:S(2)}, u32[]{:S(2)}) %collective-permute-start.20) | collective-permute-done | bytes 270368 | tf_op jit(solution)/shard_map/ppermute | solution.py:39
  150.4 3.7 %collective-permute-start.21 = (bf16[264,512]{1,0:T(8,128)(2,1)S(1)}, bf16[264,512]{1,0:T(8,128)(2,1)S(1)}, u32[]{:S(2)}, u32[]{:S(2)}) collective-permute-start(bf16[264,512]{1,0:T(8,128)(2,1)S(1)} %collective-permute-done.20.refs_0_), channel_id=1, source_target_pairs={{0,28},{4,0},{8,4},{12,8},{16,12},{20,16},{24,20},{28,24},{1,29},{... | collective-permute-start | bytes 811016 | tf_op jit(solution)/shard_map/ppermute | solution.py:39
  154.1 4.0 %collective-permute-done.21.refs_0_ = bf16[264,512]{1,0:T(8,128)(2,1)S(1)} collective-permute-done((bf16[264,512]{1,0:T(8,128)(2,1)S(1)}, bf16[264,512]{1,0:T(8,128)(2,1)S(1)}, u32[]{:S(2)}, u32[]{:S(2)}) %collective-permute-start.21) | collective-permute-done | bytes 270368 | tf_op jit(solution)/shard_map/ppermute | solution.py:39
  158.1 3.7 %collective-permute-start.22 = (bf16[264,512]{1,0:T(8,128)(2,1)S(1)}, bf16[264,512]{1,0:T(8,128)(2,1)S(1)}, u32[]{:S(2)}, u32[]{:S(2)}) collective-permute-start(bf16[264,512]{1,0:T(8,128)(2,1)S(1)} %collective-permute-done.21.refs_0_), channel_id=1, source_target_pairs={{0,28},{4,0},{8,4},{12,8},{16,12},{20,16},{24,20},{28,24},{1,29},{... | collective-permute-start | bytes 811016 | tf_op jit(solution)/shard_map/ppermute | solution.py:39
  161.8 4.5 %shard_map.109 = (f32[256,1024]{1,0:T(8,128)}, f32[8,256]{1,0:T(8,128)}) custom-call(bf16[264,512]{1,0:T(8,128)(2,1)} %copy-done.4, bf16[264,512]{1,0:T(8,128)(2,1)} %copy-done.9, bf16[264,512]{1,0:T(8,128)(2,1)} %copy-done.10, bf16[4096,256]{1,0:T(8,128)(2,1)} %refs_1_.3, bf16[4096,256]{1,0:T(8,128)(2,1)} %refs_2_.5, bf16[8,1792,256]{2,1,0:T(8,128)(2,1)} %bitcast.67), custom_call_target="tpu_custom_call" | custom-call | flops 805306368 | bytes 4000000 | tf_op jit(solution)/shard_map/pallas_call | solution.py:464
  166.3 4.9 %shard_map.110 = (f32[256,1024]{1,0:T(8,128)}, f32[8,256]{1,0:T(8,128)}) custom-call(bf16[264,512]{1,0:T(8,128)(2,1)} %copy-done.11, bf16[264,512]{1,0:T(8,128)(2,1)} %copy-done.13, bf16[4096,256]{1,0:T(8,128)(2,1)} %refs_1_.3, bf16[4096,256]{1,0:T(8,128)(2,1)} %refs_2_.5, bf16[8,1792,256]{2,1,0:T(8,128)(2,1)} %bitcast.68, ...), custom_call_target="tpu_custom_call" | custom-call | flops 536870912 | bytes 3000000 | tf_op jit(solution)/shard_map/pallas_call | solution.py:464
  171.2 0.7 copy-done.15
  171.9 4.9 %shard_map.111 = (f32[256,1024]{1,0:T(8,128)}, f32[8,256]{1,0:T(8,128)}) custom-call(bf16[264,512]{1,0:T(8,128)(2,1)} %copy-done.12, bf16[264,512]{1,0:T(8,128)(2,1)} %copy-done.15, bf16[4096,256]{1,0:T(8,128)(2,1)} %refs_1_.3, bf16[4096,256]{1,0:T(8,128)(2,1)} %refs_2_.5, bf16[8,1792,256]{2,1,0:T(8,128)(2,1)} %bitcast.69, ...), custom_call_target="tpu_custom_call" | custom-call | flops 536870912 | bytes 3000000 | tf_op jit(solution)/shard_map/pallas_call | solution.py:464
  176.9 0.7 copy-done.14
  177.6 3.8 %hidden.1.mine_ref = bf16[256,512]{1,0:T(8,128)(2,1)} custom-call(bf16[264,512]{1,0:T(8,128)(2,1)} %copy-done.14, bf16[4096,256]{1,0:T(8,128)(2,1)} %refs_1_.3, bf16[4096,256]{1,0:T(8,128)(2,1)} %refs_2_.5, bf16[8,1792,256]{2,1,0:T(8,128)(2,1)} %bitcast.70, f32[256,1024]{1,0:T(8,128)} %get-tuple-element.31.refs_4_, f32[8,256]{1,0:T(8,128)} %get-tuple-element.32.refs_5_), custom_call_target="tpu_custom_call" | custom-call | flops 268435456 | bytes 2000000 | tf_op jit(solution)/shard_map/hidden/pallas_call | solution.py:476
  181.5 8.1 %collective-permute-done.28.theirs_ref = bf16[256,512]{1,0:T(8,128)(2,1)S(1)} collective-permute-done((bf16[256,512]{1,0:T(8,128)(2,1)}, bf16[256,512]{1,0:T(8,128)(2,1)S(1)}, u32[]{:S(2)}, u32[]{:S(2)}) %collective-permute-start.28) | collective-permute-done | bytes 262176 | tf_op jit(solution)/shard_map/ppermute | solution.py:485
  189.6 0.7 copy-done.6
  190.3 2.7 %shard_map.112 = (bf16[256,256]{1,0:T(8,128)(2,1)}, bf16[256,256]{1,0:T(8,128)(2,1)}) custom-call(bf16[256,512]{1,0:T(8,128)(2,1)} %hidden.1.mine_ref, bf16[256,512]{1,0:T(8,128)(2,1)} %copy-done.6, bf16[256,4096]{1,0:T(8,128)(2,1)} %down_ref.3, bf16[8,1792,256]{2,1,0:T(8,128)(2,1)} %bitcast.71), custom_call_target="tpu_custom_call" | custom-call | flops 268435456 | bytes 2000000 | tf_op jit(solution)/shard_map/pallas_call | solution.py:488
  193.0 3.2 %collective-permute-start.33 = (bf16[256,256]{1,0:T(8,128)(2,1)}, bf16[256,256]{1,0:T(8,128)(2,1)S(1)}, u32[]{:S(2)}, u32[]{:S(2)}) collective-permute-start(bf16[256,256]{1,0:T(8,128)(2,1)} %get-tuple-element.34), channel_id=1, source_target_pairs={{0,28},{4,0},{8,4},{12,8},{16,12},{20,16},{24,20},{28,24},{1,29},{... | collective-permute-start | bytes 393224 | tf_op jit(solution)/shard_map/ppermute | solution.py:61
  196.2 5.1 %shard_map.113 = bf16[6,256,256]{2,1,0:T(8,128)(2,1)} custom-call(bf16[256,512]{1,0:T(8,128)(2,1)} %hidden.1.mine_ref, bf16[256,512]{1,0:T(8,128)(2,1)} %copy-done.6, bf16[256,4096]{1,0:T(8,128)(2,1)} %down_ref.3, bf16[8,1792,256]{2,1,0:T(8,128)(2,1)} %bitcast.72), custom_call_target="tpu_custom_call" | custom-call | flops 268435456 | bytes 2000000 | tf_op jit(solution)/shard_map/pallas_call | solution.py:488
  201.4 0.9 fusion.17
  202.4 6.2 %collective-permute-done.30 = bf16[256,256]{1,0:T(8,128)(2,1)S(1)} collective-permute-done((bf16[256,256]{1,0:T(8,128)(2,1)S(1)}, bf16[256,256]{1,0:T(8,128)(2,1)S(1)}, u32[]{:S(2)}, u32[]{:S(2)}) %collective-permute-start.30) | collective-permute-done | bytes 131104 | tf_op jit(solution)/shard_map/ppermute | solution.py:59
  208.6 1.0 fusion.16
  209.7 3.2 %collective-permute-start.34 = (bf16[256,256]{1,0:T(8,128)(2,1)S(1)}, bf16[256,256]{1,0:T(8,128)(2,1)S(1)}, u32[]{:S(2)}, u32[]{:S(2)}) collective-permute-start(bf16[256,256]{1,0:T(8,128)(2,1)S(1)} %get-tuple-element.46), channel_id=1, source_target_pairs={{0,28},{4,0},{8,4},{12,8},{16,12},{20,16},{24,20},{28,24},{1,29},{... | collective-permute-start | bytes 393224 | tf_op jit(solution)/shard_map/ppermute | solution.py:61
  212.9 2.9 %collective-permute-done.31 = bf16[256,256]{1,0:T(8,128)(2,1)S(1)} collective-permute-done((bf16[256,256]{1,0:T(8,128)(2,1)S(1)}, bf16[256,256]{1,0:T(8,128)(2,1)S(1)}, u32[]{:S(2)}, u32[]{:S(2)}) %collective-permute-start.31) | collective-permute-done | bytes 131104 | tf_op jit(solution)/shard_map/ppermute | solution.py:59
  215.9 1.0 fusion.15
  217.0 3.3 %collective-permute-start.35 = (bf16[256,256]{1,0:T(8,128)(2,1)S(1)}, bf16[256,256]{1,0:T(8,128)(2,1)S(1)}, u32[]{:S(2)}, u32[]{:S(2)}) collective-permute-start(bf16[256,256]{1,0:T(8,128)(2,1)S(1)} %get-tuple-element.44), channel_id=1, source_target_pairs={{0,28},{4,0},{8,4},{12,8},{16,12},{20,16},{24,20},{28,24},{1,29},{... | collective-permute-start | bytes 393224 | tf_op jit(solution)/shard_map/ppermute | solution.py:61
  220.3 2.9 %collective-permute-done.32 = bf16[256,256]{1,0:T(8,128)(2,1)S(1)} collective-permute-done((bf16[256,256]{1,0:T(8,128)(2,1)S(1)}, bf16[256,256]{1,0:T(8,128)(2,1)S(1)}, u32[]{:S(2)}, u32[]{:S(2)}) %collective-permute-start.32) | collective-permute-done | bytes 131104 | tf_op jit(solution)/shard_map/ppermute | solution.py:59
  223.2 1.7 fusion.18
  (104 shorter events, 2.3 us)
Async XLA Ops:
  6.5 13.8 %copy-start.22 = (bf16[256]{0:T(256)(128)(2,1)S(1)}, bf16[256]{0:T(256)(128)(2,1)}, u32[]{:S(2)}) copy-start(bf16[256]{0:T(256)(128)(2,1)} %param.12) | copy-start | bytes 1540
  6.5 13.8 %copy-start.23 = (bf16[256]{0:T(256)(128)(2,1)S(1)}, bf16[256]{0:T(256)(128)(2,1)}, u32[]{:S(2)}) copy-start(bf16[256]{0:T(256)(128)(2,1)} %param.18) | copy-start | bytes 1540
  6.5 13.8 %copy-start.7 = (bf16[1,256,256]{2,1,0:T(8,128)(2,1)S(1)}, bf16[1,256,256]{2,1,0:T(8,128)(2,1)}, u32[]{:S(2)}) copy-start(bf16[1,256,256]{2,1,0:T(8,128)(2,1)} %param.11) | copy-start | bytes 393220
  6.5 65.9 %all-gather.4.cloned.1.call-start = ((), (), s32[]{:S(2)}) async-start(), calls=%async_computation | async-start | bytes 3538944 | tf_op jit(solution)/shard_map/all_gather | solution.py:549
  8.5 24.8 %copy-start = (bf16[256,2048]{1,0:T(8,128)(2,1)S(1)}, bf16[256,2048]{1,0:T(8,128)(2,1)}, u32[]{:S(2)}) copy-start(bf16[256,2048]{1,0:T(8,128)(2,1)} %refs_1_.2) | copy-start | bytes 3145732
  8.5 10.9 %collective-permute-start.8 = (bf16[256,768]{1,0:T(8,128)(2,1)S(1)}, bf16[256,768]{1,0:T(8,128)(2,1)S(1)}, u32[]{:S(2)}, u32[]{:S(2)}) collective-permute-start(bf16[256,768]{1,0:T(8,128)(2,1)S(1)} %pad_maximum_fusion.2), channel_id=1, source_target_pairs={{0,1},{1,0},{2,3},{3,2},{4,5},{5,4},{6,7},{7,6},{8,9},{9,8},{10,11... | collective-permute-start | bytes 1179656 | tf_op jit(solution)/shard_map/ppermute | solution.py:548
  19.5 0.8 copy-start.8
  20.3 141.5 %all-gather.6.cloned.1.call-start = ((), (), s32[]{:S(2)}) async-start(), calls=%async_computation.1 | async-start | bytes 8257536 | tf_op jit(solution)/shard_map/all_gather | solution.py:588
  20.4 6.6 %collective-permute-start = (bf16[264,256]{1,0:T(8,128)(2,1)S(1)}, bf16[264,256]{1,0:T(8,128)(2,1)S(1)}, u32[]{:S(2)}, u32[]{:S(2)}) collective-permute-start(bf16[264,256]{1,0:T(8,128)(2,1)S(1)} %pad_maximum_fusion.5), channel_id=1, source_target_pairs={{0,2},{2,0},{1,3},{3,1},{4,6},{6,4},{5,7},{7,5},{8,10},{10,8},{9,1... | collective-permute-start | bytes 405512 | tf_op jit(solution)/shard_map/ppermute | solution.py:540
  27.3 28.0 %copy-start.5 = (bf16[264,512]{1,0:T(8,128)(2,1)}, bf16[264,512]{1,0:T(8,128)(2,1)S(1)}, u32[]{:S(2)}) copy-start(bf16[264,512]{1,0:T(8,128)(2,1)S(1)} %pad_maximum_fusion.3.refs_0_) | copy-start | bytes 811012
  27.4 9.9 %collective-permute-start.1 = (bf16[264,512]{1,0:T(8,128)(2,1)S(1)}, bf16[264,512]{1,0:T(8,128)(2,1)S(1)}, u32[]{:S(2)}, u32[]{:S(2)}) collective-permute-start(bf16[264,512]{1,0:T(8,128)(2,1)S(1)} %pad_maximum_fusion.3.refs_0_), channel_id=1, source_target_pairs={{0,28},{4,0},{8,4},{12,8},{16,12},{20,16},{24,20},{28,24},{1,29},{... | collective-permute-start | bytes 811016 | tf_op jit(solution)/shard_map/ppermute | solution.py:39
  37.3 18.1 %copy-start.16 = (bf16[264,512]{1,0:T(8,128)(2,1)}, bf16[264,512]{1,0:T(8,128)(2,1)S(1)}, u32[]{:S(2)}) copy-start(bf16[264,512]{1,0:T(8,128)(2,1)S(1)} %collective-permute-done.1.refs_1_) | copy-start | bytes 811012
  37.3 22.9 %collective-permute-start.9 = (bf16[256,1024]{1,0:T(8,128)(2,1)}, bf16[256,1024]{1,0:T(8,128)(2,1)S(1)}, u32[]{:S(2)}, u32[]{:S(2)}) collective-permute-start(bf16[256,1024]{1,0:T(8,128)(2,1)} %constant_dynamic-slice_fusion.4), channel_id=1, source_target_pairs={{0,1},{1,0},{2,3},{3,2},{4,5},{5,4},{6,7},{7,6},{8,9},{9,8},{10,11... | collective-permute-start | bytes 1572872 | tf_op jit(solution)/shard_map/ppermute | solution.py:572
  39.8 15.4 %collective-permute-start.23 = (bf16[256,256]{1,0:T(8,128)(2,1)S(1)}, bf16[256,256]{1,0:T(8,128)(2,1)S(1)}, u32[]{:S(2)}, u32[]{:S(2)}) collective-permute-start(bf16[256,256]{1,0:T(8,128)(2,1)S(1)} %get-tuple-element.24), channel_id=1, source_target_pairs={{0,2},{2,0},{1,3},{3,1},{4,6},{6,4},{5,7},{7,5},{8,10},{10,8},{9,1... | collective-permute-start | bytes 393224 | tf_op jit(solution)/shard_map/ppermute | solution.py:576
  42.8 12.5 %collective-permute-start.2 = (bf16[264,512]{1,0:T(8,128)(2,1)S(1)}, bf16[264,512]{1,0:T(8,128)(2,1)S(1)}, u32[]{:S(2)}, u32[]{:S(2)}) collective-permute-start(bf16[264,512]{1,0:T(8,128)(2,1)S(1)} %collective-permute-done.1.refs_1_), channel_id=1, source_target_pairs={{0,28},{4,0},{8,4},{12,8},{16,12},{20,16},{24,20},{28,24},{1,29},{... | collective-permute-start | bytes 811016 | tf_op jit(solution)/shard_map/ppermute | solution.py:39
  47.6 9.3 %collective-permute-start.5 = (bf16[264,512]{1,0:T(8,128)(2,1)S(1)}, bf16[264,512]{1,0:T(8,128)(2,1)S(1)}, u32[]{:S(2)}, u32[]{:S(2)}) collective-permute-start(bf16[264,512]{1,0:T(8,128)(2,1)S(1)} %pad_maximum_fusion.3.refs_0_), channel_id=1, source_target_pairs={{0,4},{4,8},{8,12},{12,16},{16,20},{20,24},{24,28},{28,0},{1,5},{5... | collective-permute-start | bytes 811016 | tf_op jit(solution)/shard_map/ppermute | solution.py:42
  55.4 4.8 %copy-start.17 = (bf16[264,512]{1,0:T(8,128)(2,1)}, bf16[264,512]{1,0:T(8,128)(2,1)S(1)}, u32[]{:S(2)}) copy-start(bf16[264,512]{1,0:T(8,128)(2,1)S(1)} %collective-permute-done.2.refs_2_) | copy-start | bytes 811012
  55.4 28.9 %collective-permute-start.24 = (bf16[1536,256]{1,0:T(8,128)(2,1)S(1)}, bf16[1536,256]{1,0:T(8,128)(2,1)S(1)}, u32[]{:S(2)}, u32[]{:S(2)}) collective-permute-start(bf16[1536,256]{1,0:T(8,128)(2,1)S(1)} %pad_maximum_fusion.1), channel_id=1, source_target_pairs={{0,1},{1,0},{2,3},{3,2},{4,5},{5,4},{6,7},{7,6},{8,9},{9,8},{10,11... | collective-permute-start | bytes 2359304 | tf_op jit(solution)/shard_map/ppermute | solution.py:578
  56.9 7.7 %copy-start.18 = (bf16[264,512]{1,0:T(8,128)(2,1)}, bf16[264,512]{1,0:T(8,128)(2,1)S(1)}, u32[]{:S(2)}) copy-start(bf16[264,512]{1,0:T(8,128)(2,1)S(1)} %collective-permute-done.5.refs_7_) | copy-start | bytes 811012
  56.9 7.7 %collective-permute-start.6 = (bf16[264,512]{1,0:T(8,128)(2,1)S(1)}, bf16[264,512]{1,0:T(8,128)(2,1)S(1)}, u32[]{:S(2)}, u32[]{:S(2)}) collective-permute-start(bf16[264,512]{1,0:T(8,128)(2,1)S(1)} %collective-permute-done.5.refs_7_), channel_id=1, source_target_pairs={{0,4},{4,8},{8,12},{12,16},{16,20},{20,24},{24,28},{28,0},{1,5},{5... | collective-permute-start | bytes 811016 | tf_op jit(solution)/shard_map/ppermute | solution.py:42
  56.9 7.7 %collective-permute-start.3 = (bf16[264,512]{1,0:T(8,128)(2,1)S(1)}, bf16[264,512]{1,0:T(8,128)(2,1)}, u32[]{:S(2)}, u32[]{:S(2)}) collective-permute-start(bf16[264,512]{1,0:T(8,128)(2,1)S(1)} %collective-permute-done.2.refs_2_), channel_id=1, source_target_pairs={{0,28},{4,0},{8,4},{12,8},{16,12},{20,16},{24,20},{28,24},{1,29},{... | collective-permute-start | bytes 811016 | tf_op jit(solution)/shard_map/ppermute | solution.py:39
  60.1 12.3 %copy-start.2 = (bf16[256,1024]{1,0:T(8,128)(2,1)}, bf16[256,1024]{1,0:T(8,128)(2,1)S(1)}, u32[]{:S(2)}) copy-start(bf16[256,1024]{1,0:T(8,128)(2,1)S(1)} %collective-permute-done.9.refs_13_.refs_2_) | copy-start | bytes 1572868
  60.1 12.2 %collective-permute-start.10 = (bf16[256,1024]{1,0:T(8,128)(2,1)S(1)}, bf16[256,1024]{1,0:T(8,128)(2,1)S(1)}, u32[]{:S(2)}, u32[]{:S(2)}) collective-permute-start(bf16[256,1024]{1,0:T(8,128)(2,1)S(1)} %collective-permute-done.9.refs_13_.refs_2_), channel_id=1, source_target_pairs={{0,32},{32,0},{64,96},{96,64},{128,160},{160,128},{192,224},{224,1... | collective-permute-start | bytes 1572872 | tf_op jit(solution)/shard_map/ppermute | solution.py:574
  64.6 7.8 %copy-start.19 = (bf16[264,512]{1,0:T(8,128)(2,1)}, bf16[264,512]{1,0:T(8,128)(2,1)S(1)}, u32[]{:S(2)}) copy-start(bf16[264,512]{1,0:T(8,128)(2,1)S(1)} %collective-permute-done.6.refs_6_) | copy-start | bytes 811012
  64.6 7.8 %collective-permute-start.7 = (bf16[264,512]{1,0:T(8,128)(2,1)S(1)}, bf16[264,512]{1,0:T(8,128)(2,1)}, u32[]{:S(2)}, u32[]{:S(2)}) collective-permute-start(bf16[264,512]{1,0:T(8,128)(2,1)S(1)} %collective-permute-done.6.refs_6_), channel_id=1, source_target_pairs={{0,4},{4,8},{8,12},{12,16},{16,20},{20,24},{24,28},{28,0},{1,5},{5... | collective-permute-start | bytes 811016 | tf_op jit(solution)/shard_map/ppermute | solution.py:42
  64.6 7.8 %collective-permute-start.4 = (bf16[264,512]{1,0:T(8,128)(2,1)}, bf16[264,512]{1,0:T(8,128)(2,1)}, u32[]{:S(2)}, u32[]{:S(2)}) collective-permute-start(bf16[264,512]{1,0:T(8,128)(2,1)} %collective-permute-done.3.refs_3_), channel_id=1, source_target_pairs={{0,28},{4,0},{8,4},{12,8},{16,12},{20,16},{24,20},{28,24},{1,29},{... | collective-permute-start | bytes 811016 | tf_op jit(solution)/shard_map/ppermute | solution.py:39
  72.4 0.8 copy-start.3
  84.3 1.0 copy-start.21
  84.3 1.3 copy-start.20
  85.3 9.0 %collective-permute-start.11 = (bf16[256,512]{1,0:T(8,128)(2,1)S(1)}, bf16[256,512]{1,0:T(8,128)(2,1)S(1)}, u32[]{:S(2)}, u32[]{:S(2)}) collective-permute-start(bf16[256,512]{1,0:T(8,128)(2,1)S(1)} %copy-done.21), channel_id=1, source_target_pairs={{0,4},{4,8},{8,12},{12,16},{16,20},{20,24},{24,28},{28,0},{1,5},{5... | collective-permute-start | bytes 786440 | tf_op jit(solution)/shard_map/ppermute | solution.py:59
  85.6 10.0 %collective-permute-start.15 = (bf16[256,512]{1,0:T(8,128)(2,1)S(1)}, bf16[256,512]{1,0:T(8,128)(2,1)S(1)}, u32[]{:S(2)}, u32[]{:S(2)}) collective-permute-start(bf16[256,512]{1,0:T(8,128)(2,1)S(1)} %copy-done.20), channel_id=1, source_target_pairs={{0,28},{4,0},{8,4},{12,8},{16,12},{20,16},{24,20},{28,24},{1,29},{... | collective-permute-start | bytes 786440 | tf_op jit(solution)/shard_map/ppermute | solution.py:61
  94.4 21.1 %copy-start.1 = (bf16[6,256,512]{2,1,0:T(8,128)(2,1)S(1)}, bf16[6,256,512]{2,1,0:T(8,128)(2,1)}, u32[]{:S(2)}) copy-start(bf16[6,256,512]{2,1,0:T(8,128)(2,1)} %out_rest.1) | copy-start | bytes 4718596
  95.5 9.3 %collective-permute-start.12 = (bf16[256,512]{1,0:T(8,128)(2,1)S(1)}, bf16[256,512]{1,0:T(8,128)(2,1)S(1)}, u32[]{:S(2)}, u32[]{:S(2)}) collective-permute-start(bf16[256,512]{1,0:T(8,128)(2,1)S(1)} %fusion.10), channel_id=1, source_target_pairs={{0,4},{4,8},{8,12},{12,16},{16,20},{20,24},{24,28},{28,0},{1,5},{5... | collective-permute-start | bytes 786440 | tf_op jit(solution)/shard_map/ppermute | solution.py:59
  106.1 9.4 %collective-permute-start.13 = (bf16[256,512]{1,0:T(8,128)(2,1)S(1)}, bf16[256,512]{1,0:T(8,128)(2,1)S(1)}, u32[]{:S(2)}, u32[]{:S(2)}) collective-permute-start(bf16[256,512]{1,0:T(8,128)(2,1)S(1)} %get-tuple-element.41), channel_id=1, source_target_pairs={{0,4},{4,8},{8,12},{12,16},{16,20},{20,24},{24,28},{28,0},{1,5},{5... | collective-permute-start | bytes 786440 | tf_op jit(solution)/shard_map/ppermute | solution.py:59
  106.2 9.3 %collective-permute-start.16 = (bf16[256,512]{1,0:T(8,128)(2,1)S(1)}, bf16[256,512]{1,0:T(8,128)(2,1)S(1)}, u32[]{:S(2)}, u32[]{:S(2)}) collective-permute-start(bf16[256,512]{1,0:T(8,128)(2,1)S(1)} %get-tuple-element.42), channel_id=1, source_target_pairs={{0,28},{4,0},{8,4},{12,8},{16,12},{20,16},{24,20},{28,24},{1,29},{... | collective-permute-start | bytes 786440 | tf_op jit(solution)/shard_map/ppermute | solution.py:61
  115.6 7.7 %collective-permute-start.14 = (bf16[256,512]{1,0:T(8,128)(2,1)S(1)}, bf16[256,512]{1,0:T(8,128)(2,1)S(1)}, u32[]{:S(2)}, u32[]{:S(2)}) collective-permute-start(bf16[256,512]{1,0:T(8,128)(2,1)S(1)} %get-tuple-element.39), channel_id=1, source_target_pairs={{0,4},{4,8},{8,12},{12,16},{16,20},{20,24},{24,28},{28,0},{1,5},{5... | collective-permute-start | bytes 786440 | tf_op jit(solution)/shard_map/ppermute | solution.py:59
  115.7 7.6 %collective-permute-start.17 = (bf16[256,512]{1,0:T(8,128)(2,1)S(1)}, bf16[256,512]{1,0:T(8,128)(2,1)S(1)}, u32[]{:S(2)}, u32[]{:S(2)}) collective-permute-start(bf16[256,512]{1,0:T(8,128)(2,1)S(1)} %get-tuple-element.40), channel_id=1, source_target_pairs={{0,28},{4,0},{8,4},{12,8},{16,12},{20,16},{24,20},{28,24},{1,29},{... | collective-permute-start | bytes 786440 | tf_op jit(solution)/shard_map/ppermute | solution.py:61
  123.4 8.0 %collective-permute-start.18 = (bf16[256,512]{1,0:T(8,128)(2,1)S(1)}, bf16[256,512]{1,0:T(8,128)(2,1)S(1)}, u32[]{:S(2)}, u32[]{:S(2)}) collective-permute-start(bf16[256,512]{1,0:T(8,128)(2,1)S(1)} %fusion.5), channel_id=1, source_target_pairs={{0,2},{2,0},{1,3},{3,1},{4,6},{6,4},{5,7},{7,5},{8,10},{10,8},{9,1... | collective-permute-start | bytes 786440 | tf_op jit(solution)/shard_map/ppermute | solution.py:590
  131.7 30.1 %copy-start.4 = (bf16[264,512]{1,0:T(8,128)(2,1)}, bf16[264,512]{1,0:T(8,128)(2,1)S(1)}, u32[]{:S(2)}) copy-start(bf16[264,512]{1,0:T(8,128)(2,1)S(1)} %pad_maximum_fusion.4.refs_0_) | copy-start | bytes 811012
  131.7 8.6 %collective-permute-start.19 = (bf16[264,512]{1,0:T(8,128)(2,1)S(1)}, bf16[264,512]{1,0:T(8,128)(2,1)S(1)}, u32[]{:S(2)}, u32[]{:S(2)}) collective-permute-start(bf16[264,512]{1,0:T(8,128)(2,1)S(1)} %pad_maximum_fusion.4.refs_0_), channel_id=1, source_target_pairs={{0,28},{4,0},{8,4},{12,8},{16,12},{20,16},{24,20},{28,24},{1,29},{... | collective-permute-start | bytes 811016 | tf_op jit(solution)/shard_map/ppermute | solution.py:39
  135.0 9.0 %collective-permute-start.25 = (bf16[264,512]{1,0:T(8,128)(2,1)S(1)}, bf16[264,512]{1,0:T(8,128)(2,1)S(1)}, u32[]{:S(2)}, u32[]{:S(2)}) collective-permute-start(bf16[264,512]{1,0:T(8,128)(2,1)S(1)} %pad_maximum_fusion.4.refs_0_), channel_id=1, source_target_pairs={{0,4},{4,8},{8,12},{12,16},{16,20},{20,24},{24,28},{28,0},{1,5},{5... | collective-permute-start | bytes 811016 | tf_op jit(solution)/shard_map/ppermute | solution.py:42
  140.3 21.5 %copy-start.9 = (bf16[264,512]{1,0:T(8,128)(2,1)}, bf16[264,512]{1,0:T(8,128)(2,1)S(1)}, u32[]{:S(2)}) copy-start(bf16[264,512]{1,0:T(8,128)(2,1)S(1)} %collective-permute-done.19.refs_1_) | copy-start | bytes 811012
  140.3 10.1 %collective-permute-start.20 = (bf16[264,512]{1,0:T(8,128)(2,1)S(1)}, bf16[264,512]{1,0:T(8,128)(2,1)S(1)}, u32[]{:S(2)}, u32[]{:S(2)}) collective-permute-start(bf16[264,512]{1,0:T(8,128)(2,1)S(1)} %collective-permute-done.19.refs_1_), channel_id=1, source_target_pairs={{0,28},{4,0},{8,4},{12,8},{16,12},{20,16},{24,20},{28,24},{1,29},{... | collective-permute-start | bytes 811016 | tf_op jit(solution)/shard_map/ppermute | solution.py:39
  144.0 17.8 %copy-start.10 = (bf16[264,512]{1,0:T(8,128)(2,1)}, bf16[264,512]{1,0:T(8,128)(2,1)S(1)}, u32[]{:S(2)}) copy-start(bf16[264,512]{1,0:T(8,128)(2,1)S(1)} %collective-permute-done.25.refs_2_) | copy-start | bytes 811012
  144.0 10.1 %collective-permute-start.26 = (bf16[264,512]{1,0:T(8,128)(2,1)S(1)}, bf16[264,512]{1,0:T(8,128)(2,1)S(1)}, u32[]{:S(2)}, u32[]{:S(2)}) collective-permute-start(bf16[264,512]{1,0:T(8,128)(2,1)S(1)} %collective-permute-done.25.refs_2_), channel_id=1, source_target_pairs={{0,4},{4,8},{8,12},{12,16},{16,20},{20,24},{24,28},{28,0},{1,5},{5... | collective-permute-start | bytes 811016 | tf_op jit(solution)/shard_map/ppermute | solution.py:42
  150.4 15.9 %copy-start.11 = (bf16[264,512]{1,0:T(8,128)(2,1)}, bf16[264,512]{1,0:T(8,128)(2,1)S(1)}, u32[]{:S(2)}) copy-start(bf16[264,512]{1,0:T(8,128)(2,1)S(1)} %collective-permute-done.20.refs_0_) | copy-start | bytes 811012
  150.4 7.7 %collective-permute-start.21 = (bf16[264,512]{1,0:T(8,128)(2,1)S(1)}, bf16[264,512]{1,0:T(8,128)(2,1)S(1)}, u32[]{:S(2)}, u32[]{:S(2)}) collective-permute-start(bf16[264,512]{1,0:T(8,128)(2,1)S(1)} %collective-permute-done.20.refs_0_), channel_id=1, source_target_pairs={{0,28},{4,0},{8,4},{12,8},{16,12},{20,16},{24,20},{28,24},{1,29},{... | collective-permute-start | bytes 811016 | tf_op jit(solution)/shard_map/ppermute | solution.py:39
  154.1 12.2 %copy-start.13 = (bf16[264,512]{1,0:T(8,128)(2,1)}, bf16[264,512]{1,0:T(8,128)(2,1)S(1)}, u32[]{:S(2)}) copy-start(bf16[264,512]{1,0:T(8,128)(2,1)S(1)} %collective-permute-done.26.refs_1_) | copy-start | bytes 811012
  154.1 17.1 %collective-permute-start.27 = (bf16[264,512]{1,0:T(8,128)(2,1)S(1)}, bf16[264,512]{1,0:T(8,128)(2,1)S(1)}, u32[]{:S(2)}, u32[]{:S(2)}) collective-permute-start(bf16[264,512]{1,0:T(8,128)(2,1)S(1)} %collective-permute-done.26.refs_1_), channel_id=1, source_target_pairs={{0,4},{4,8},{8,12},{12,16},{16,20},{20,24},{24,28},{28,0},{1,5},{5... | collective-permute-start | bytes 811016 | tf_op jit(solution)/shard_map/ppermute | solution.py:42
  158.1 8.3 %copy-start.12 = (bf16[264,512]{1,0:T(8,128)(2,1)}, bf16[264,512]{1,0:T(8,128)(2,1)S(1)}, u32[]{:S(2)}) copy-start(bf16[264,512]{1,0:T(8,128)(2,1)S(1)} %collective-permute-done.21.refs_0_) | copy-start | bytes 811012
  158.1 18.8 %collective-permute-start.22 = (bf16[264,512]{1,0:T(8,128)(2,1)S(1)}, bf16[264,512]{1,0:T(8,128)(2,1)S(1)}, u32[]{:S(2)}, u32[]{:S(2)}) collective-permute-start(bf16[264,512]{1,0:T(8,128)(2,1)S(1)} %collective-permute-done.21.refs_0_), channel_id=1, source_target_pairs={{0,28},{4,0},{8,4},{12,8},{16,12},{20,16},{24,20},{28,24},{1,29},{... | collective-permute-start | bytes 811016 | tf_op jit(solution)/shard_map/ppermute | solution.py:39
  171.2 0.7 copy-start.15
  176.9 0.7 copy-start.14
  181.4 8.2 %collective-permute-start.28 = (bf16[256,512]{1,0:T(8,128)(2,1)}, bf16[256,512]{1,0:T(8,128)(2,1)S(1)}, u32[]{:S(2)}, u32[]{:S(2)}) collective-permute-start(bf16[256,512]{1,0:T(8,128)(2,1)} %hidden.1.mine_ref), channel_id=1, source_target_pairs={{0,2},{2,0},{1,3},{3,1},{4,6},{6,4},{5,7},{7,5},{8,10},{10,8},{9,1... | collective-permute-start | bytes 786440 | tf_op jit(solution)/shard_map/ppermute | solution.py:485
  189.6 0.7 copy-start.6
  192.9 8.5 %collective-permute-start.29 = (bf16[256,256]{1,0:T(8,128)(2,1)}, bf16[256,256]{1,0:T(8,128)(2,1)S(1)}, u32[]{:S(2)}, u32[]{:S(2)}) collective-permute-start(bf16[256,256]{1,0:T(8,128)(2,1)} %get-tuple-element.33), channel_id=1, source_target_pairs={{0,4},{4,8},{8,12},{12,16},{16,20},{20,24},{24,28},{28,0},{1,5},{5... | collective-permute-start | bytes 393224 | tf_op jit(solution)/shard_map/ppermute | solution.py:59
  193.0 9.4 %collective-permute-start.33 = (bf16[256,256]{1,0:T(8,128)(2,1)}, bf16[256,256]{1,0:T(8,128)(2,1)S(1)}, u32[]{:S(2)}, u32[]{:S(2)}) collective-permute-start(bf16[256,256]{1,0:T(8,128)(2,1)} %get-tuple-element.34), channel_id=1, source_target_pairs={{0,28},{4,0},{8,4},{12,8},{16,12},{20,16},{24,20},{28,24},{1,29},{... | collective-permute-start | bytes 393224 | tf_op jit(solution)/shard_map/ppermute | solution.py:61
  202.3 6.3 %collective-permute-start.30 = (bf16[256,256]{1,0:T(8,128)(2,1)S(1)}, bf16[256,256]{1,0:T(8,128)(2,1)S(1)}, u32[]{:S(2)}, u32[]{:S(2)}) collective-permute-start(bf16[256,256]{1,0:T(8,128)(2,1)S(1)} %fusion.17), channel_id=1, source_target_pairs={{0,4},{4,8},{8,12},{12,16},{16,20},{20,24},{24,28},{28,0},{1,5},{5... | collective-permute-start | bytes 393224 | tf_op jit(solution)/shard_map/ppermute | solution.py:59
  209.6 6.3 %collective-permute-start.31 = (bf16[256,256]{1,0:T(8,128)(2,1)S(1)}, bf16[256,256]{1,0:T(8,128)(2,1)S(1)}, u32[]{:S(2)}, u32[]{:S(2)}) collective-permute-start(bf16[256,256]{1,0:T(8,128)(2,1)S(1)} %get-tuple-element.45), channel_id=1, source_target_pairs={{0,4},{4,8},{8,12},{12,16},{16,20},{20,24},{24,28},{28,0},{1,5},{5... | collective-permute-start | bytes 393224 | tf_op jit(solution)/shard_map/ppermute | solution.py:59
  209.7 6.2 %collective-permute-start.34 = (bf16[256,256]{1,0:T(8,128)(2,1)S(1)}, bf16[256,256]{1,0:T(8,128)(2,1)S(1)}, u32[]{:S(2)}, u32[]{:S(2)}) collective-permute-start(bf16[256,256]{1,0:T(8,128)(2,1)S(1)} %get-tuple-element.46), channel_id=1, source_target_pairs={{0,28},{4,0},{8,4},{12,8},{16,12},{20,16},{24,20},{28,24},{1,29},{... | collective-permute-start | bytes 393224 | tf_op jit(solution)/shard_map/ppermute | solution.py:61
  216.9 6.3 %collective-permute-start.32 = (bf16[256,256]{1,0:T(8,128)(2,1)S(1)}, bf16[256,256]{1,0:T(8,128)(2,1)S(1)}, u32[]{:S(2)}, u32[]{:S(2)}) collective-permute-start(bf16[256,256]{1,0:T(8,128)(2,1)S(1)} %get-tuple-element.43), channel_id=1, source_target_pairs={{0,4},{4,8},{8,12},{12,16},{16,20},{20,24},{24,28},{28,0},{1,5},{5... | collective-permute-start | bytes 393224 | tf_op jit(solution)/shard_map/ppermute | solution.py:59
  217.0 6.2 %collective-permute-start.35 = (bf16[256,256]{1,0:T(8,128)(2,1)S(1)}, bf16[256,256]{1,0:T(8,128)(2,1)S(1)}, u32[]{:S(2)}, u32[]{:S(2)}) collective-permute-start(bf16[256,256]{1,0:T(8,128)(2,1)S(1)} %get-tuple-element.44), channel_id=1, source_target_pairs={{0,28},{4,0},{8,4},{12,8},{16,12},{20,16},{24,20},{28,24},{1,29},{... | collective-permute-start | bytes 393224 | tf_op jit(solution)/shard_map/ppermute | solution.py:61
Sparse Core Ops, SparseCore 0:
  20.4 32.1 all-gather.3
  85.5 44.8 all-gather.5

commit v3 on v2

--- a/solution.py
+++ b/solution.py
@@ -113,8 +113,9 @@
     own = refs[RING : RING + 3]
     other_ref, *out_weight_refs, bias_ref = refs[RING + 3 : RING + 8]
     first_ref, second_ref, attended_ref = refs[RING + 8 : RING + 11]
-    x_ref, w_ref, o_ref, acc_ref, both_ref = refs[RING + 11 : RING + 16]
-    x_sem, own_sem, other_sem, o_sem = refs[RING + 16 :]
+    x_ref, w_ref, o_ref, acc_ref, both_ref, table_ref = refs[RING + 11 : RING + 17]
+    x_sem, own_sem, other_sem, o_sem, table_sem = refs[RING + 17 :]
+    table_copy = pltpu.make_async_copy(bias_ref, table_ref, table_sem)
     length = acc_ref.shape[0]
     inner = attended_ref.shape[1]
     wide = x_ref.shape[2]
@@ -139,7 +140,7 @@
         for k in range(parts)
     ]
     o_copies = out_weight_copies(out_weight_refs, o_ref, o_sem)
-    for copy in x_copies + own_copies + other_copies + o_copies:
+    for copy in x_copies + own_copies + other_copies + [table_copy] + o_copies:
         copy.start()
     for copy in x_copies:
         copy.wait()
@@ -165,6 +166,8 @@
     heads = bias_ref.shape[0]
     size = inner // heads
     pair = 2 * size
+
+    table_copy.wait()
 
     def two_heads(n, unused):
         query, key, value = (
@@ -182,7 +185,7 @@
                     (((1,), (1,)), ((), ())),
                     preferred_element_type=jnp.float32,
                 )
-                + bias_ref[2 * n + h]
+                + table_ref[2 * n + h]
             )
             exponent = jnp.exp(scores - jnp.max(scores, axis=-1, keepdims=True))
             weights = exponent / jnp.sum(exponent, axis=-1, keepdims=True)
@@ -226,8 +229,9 @@
 
 def out_rest_kernel(*refs):
     out_weight_refs = refs[1:4]
-    attended_ref, rest_ref, o_ref, o_sem = refs[0], *refs[4:]
-    copies = out_weight_copies(out_weight_refs, o_ref, o_sem)
+    rest_ref, o_ref, o_sem, attended_ref, attended_sem = refs[4:]
+    copies = [pltpu.make_async_copy(refs[0], attended_ref, attended_sem)]
+    copies += out_weight_copies(out_weight_refs, o_ref, o_sem)
     for copy in copies:
         copy.start()
     for copy in copies:
@@ -266,7 +270,7 @@
     ]
     first, second, attended = pl.pallas_call(
         functools.partial(attention_kernel, float(wide * RING)),
-        in_specs=[ANY] * (RING + 7) + [IN_VMEM],
+        in_specs=[ANY] * (RING + 8),
         out_specs=[IN_VMEM] * 3,
         scratch_shapes=[
             pltpu.VMEM((RING, rows, wide), jnp.bfloat16),
@@ -274,10 +278,12 @@
             out_scratch[0],
             pltpu.VMEM((length, 3 * inner), jnp.float32),
             pltpu.VMEM((length, 2 * inner // bias.shape[0]), jnp.bfloat16),
+            pltpu.VMEM(bias.shape, jnp.float32),
             pltpu.SemaphoreType.DMA((RING,)),
             pltpu.SemaphoreType.DMA((3,)),
             pltpu.SemaphoreType.DMA((parts,)),
             out_scratch[1],
+            pltpu.SemaphoreType.DMA,
         ],
         out_shape=[one_block(length, wide)] * 2 + [one_block(length, inner)],
         cost_estimate=pl.CostEstimate(
@@ -293,9 +299,10 @@
     )
     rest = pl.pallas_call(
         out_rest_kernel,
-        in_specs=[IN_VMEM] + [ANY] * 3,
+        in_specs=[ANY] * 4,
         out_specs=IN_VMEM,
-        scratch_shapes=out_scratch,
+        scratch_shapes=out_scratch
+        + [pltpu.VMEM((length, inner), jnp.bfloat16), pltpu.SemaphoreType.DMA],
         out_shape=rest_blocks(length, wide),
         cost_estimate=pl.CostEstimate(
             flops=2 * length * inner * wide * (RING - 2),
@@ -343,15 +350,15 @@
     refs = refs[count + 3 :]
     if more:
         acc_in_ref, squares_in_ref, refs = refs[0], refs[1], refs[2:]
-    acc_ref, squares_ref, x_ref, w_ref, x_sem, w_sem = refs
+    acc_ref, squares_ref, x_ref, w_ref, x_sem, w_sem, sum_sem = refs
     length = acc_ref.shape[0]
     copies = gate_copies(owners, blocks, gate_ref, up_ref, other_ref, x_ref, w_ref, x_sem, w_sem)
+    if more:
+        copies.append(pltpu.make_async_copy(squares_in_ref, squares_ref, sum_sem.at[0]))
+        copies.append(pltpu.make_async_copy(acc_in_ref, acc_ref, sum_sem.at[1]))
     for copy in copies:
         copy.start()
-    if more:
-        acc_ref[...] = acc_in_ref[...]
-        squares_ref[...] = squares_in_ref[...]
-    else:
+    if not more:
         acc_ref[...] = jnp.zeros_like(acc_ref)
         squares_ref[...] = jnp.zeros_like(squares_ref)
     for copy in copies:
@@ -369,22 +376,24 @@
     count = len(LAST)
     blocks = refs[:count]
     gate_ref, up_ref, other_ref, acc_in_ref, squares_in_ref = refs[count : count + 5]
-    hidden_ref, x_ref, w_ref, x_sem, w_sem = refs[count + 5 :]
+    hidden_ref, x_ref, w_ref, x_sem, w_sem, sum_sem, acc_ref, squares_ref = refs[count + 5 :]
     size = gate_ref.shape[1]
     length = hidden_ref.shape[0]
     copies = gate_copies(LAST, blocks, gate_ref, up_ref, other_ref, x_ref, w_ref, x_sem, w_sem)
+    copies.append(pltpu.make_async_copy(squares_in_ref, squares_ref, sum_sem.at[0]))
+    copies.append(pltpu.make_async_copy(acc_in_ref, acc_ref, sum_sem.at[1]))
     for copy in copies:
         copy.start()
     for copy in copies:
         copy.wait()
     rows = x_ref[0, :length, :]
-    squares = squares_in_ref[0:1, :] + x_ref[0, length : length + 1, :length].astype(jnp.float32)
+    squares = squares_ref[0:1, :] + x_ref[0, length : length + 1, :length].astype(jnp.float32)
     scale = as_column(lax.rsqrt(squares / width + epsilon))
     for k in range(2):
         sums = []
         for n in (2 * k, 2 * k + 1):
             at = slice(n * size, (n + 1) * size)
-            sums.append((acc_in_ref[:, at] + dot(rows, w_ref[0, :, at])) * scale)
+            sums.append((acc_ref[:, at] + dot(rows, w_ref[0, :, at])) * scale)
         hidden_ref[:, k * size : (k + 1) * size] = (
             jax.nn.gelu(sums[0], approximate=True) * sums[1]
         ).astype(jnp.bfloat16)
@@ -451,6 +460,7 @@
             pltpu.VMEM((count, wide, 4 * hidden), jnp.bfloat16),
             pltpu.SemaphoreType.DMA((count,)),
             pltpu.SemaphoreType.DMA((count, 4)),
+            pltpu.SemaphoreType.DMA((2,)),
         ]
 
     def cost(count, extra=0):
@@ -463,7 +473,7 @@
     def gate_sums(owners, before):
         return pl.pallas_call(
             functools.partial(gate_kernel, owners, bool(before)),
-            in_specs=[ANY] * (len(owners) + 3) + [IN_VMEM] * len(before),
+            in_specs=[ANY] * (len(owners) + 3 + len(before)),
             out_specs=[IN_VMEM] * 2,
             scratch_shapes=scratch(len(owners)),
             out_shape=sums,
@@ -475,9 +485,9 @@
     before = gate_sums(THIRD, before)
     mine = pl.pallas_call(
         functools.partial(hidden_kernel, float(wide * RING)),
-        in_specs=[ANY] * (len(LAST) + 3) + [IN_VMEM] * 2,
+        in_specs=[ANY] * (len(LAST) + 5),
         out_specs=IN_VMEM,
-        scratch_shapes=scratch(len(LAST)),
+        scratch_shapes=scratch(len(LAST)) + [pltpu.VMEM(s.shape, s.dtype) for s in sums],
         out_shape=jax.ShapeDtypeStruct((length, 2 * hidden), jnp.bfloat16),
         cost_estimate=cost(1),
         name="hidden",
@@ -574,8 +584,10 @@
     other_core_out = lax.ppermute(core_out, "ba", cores)
     pair_share = tied(down_share(1 - pair_at), held[1])
     pair_share = lax.ppermute(pair_share, "ma_1", SWAP)
-    row_share = jnp.concatenate([*gate_share, down_share(pair_at), pair_share], axis=0)
-    row_share = lax.ppermute(tied(row_share, held[2]), "row", SWAP)
+    pair_share = tied(pair_share, held[3])
+    same_share = down_share(pair_at)
+    row_share = jnp.concatenate([*gate_share, same_share, pair_share], axis=0)
+    row_share = lax.ppermute(row_share, "row", SWAP)
     out_blocks = attention(
         held,
         position_bias(bucket_bias_matrix, length),

time: 232 us -> 243 us (1.047)
  the two profiles are of different devices: /device:TPU:2 before, /device:TPU:8 now
where the time goes in v3:
time: 243 us; the launch traced here: 242 us
  waiting for transfers between devices  108 us (44%)
  starting transfers between devices  62 us (26%)
  Pallas kernels  39.6 us (16%)
  between operations  13.9 us (6%)
  local copies, waits for them, and re-layouts  9.91 us (4%)
  other arithmetic  8.82 us (4%)
    ppermute x8, waiting for transfers between devices, ring_sum(): got_up = lax.ppermute(up, 'ma_0', UP)  31.8 us
    ppermute x8, starting transfers between devices, ring_gather(): above = lax.ppermute(above, 'ma_0', DOWN)  31 us
    ppermute x8, waiting for transfers between devices, ring_gather(): above = lax.ppermute(above, 'ma_0', DOWN)  24.5 us
    ppermute x6, starting transfers between devices, ring_sum(): got_down = lax.ppermute(down, 'ma_0', DOWN)  19.8 us
    pallas_call x3, Pallas kernels, gate_sums(): pl.pallas_call(functools.partial(gate_kernel, owners, bool(before)), in_s...  12.6 us
    ppermute x6, waiting for transfers between devices, ring_gather(): below = lax.ppermute(below, 'ma_0', UP)  11.6 us
    ppermute x1, waiting for transfers between devices, layer(): pair_share = lax.ppermute(pair_share, 'ma_1', SWAP)  11.1 us
    pallas_call x1, Pallas kernels, attention(): pl.pallas_call(functools.partial(attention_kernel, float(wide * RING)), i...  9.87 us
  transfers between devices with their start and end apart: 38, of which 20 were waited for; matrix products, arithmetic and copies ran while one was open for 3% of the time, Pallas kernels for 14%

profile of v3, /device:TPU:8, one launch (start us, length us, event | category | flops | bytes accessed | tf_op | source)
XLA Modules:
  0.0 242.1 jit_solution(1781795855510766999)
XLA Ops:
  6.5 0.9 constant_dynamic-slice_fusion.7
  7.5 1.0 constant_dynamic-slice_fusion.5
  8.5 2.2 collective-permute-start.8
  10.8 8.7 %collective-permute-done.8 = bf16[256,768]{1,0:T(8,128)(2,1)S(1)} collective-permute-done((bf16[256,768]{1,0:T(8,128)(2,1)S(1)}, bf16[256,768]{1,0:T(8,128)(2,1)S(1)}, u32[]{:S(2)}, u32[]{:S(2)}) %collective-permute-start.8) | collective-permute-done | bytes 393248 | tf_op jit(solution)/shard_map/ppermute | solution.py:558
  19.5 0.7 copy-done.8
  20.4 2.4 collective-permute-start
  22.8 4.2 %collective-permute-done = bf16[264,256]{1,0:T(8,128)(2,1)S(1)} collective-permute-done((bf16[264,256]{1,0:T(8,128)(2,1)S(1)}, bf16[264,256]{1,0:T(8,128)(2,1)S(1)}, u32[]{:S(2)}, u32[]{:S(2)}) %collective-permute-start) | collective-permute-done | bytes 135200 | tf_op jit(solution)/shard_map/ppermute | solution.py:550
  27.4 5.9 %collective-permute-start.1 = (bf16[264,512]{1,0:T(8,128)(2,1)S(1)}, bf16[264,512]{1,0:T(8,128)(2,1)S(1)}, u32[]{:S(2)}, u32[]{:S(2)}) collective-permute-start(bf16[264,512]{1,0:T(8,128)(2,1)S(1)} %pad_maximum_fusion.3.refs_0_), channel_id=1, source_target_pairs={{0,28},{4,0},{8,4},{12,8},{16,12},{20,16},{24,20},{28,24},{1,29},{... | collective-permute-start | bytes 811016 | tf_op jit(solution)/shard_map/ppermute | solution.py:39
  33.3 4.0 %collective-permute-done.1.refs_1_ = bf16[264,512]{1,0:T(8,128)(2,1)S(1)} collective-permute-done((bf16[264,512]{1,0:T(8,128)(2,1)S(1)}, bf16[264,512]{1,0:T(8,128)(2,1)S(1)}, u32[]{:S(2)}, u32[]{:S(2)}) %collective-permute-start.1) | collective-permute-done | bytes 270368 | tf_op jit(solution)/shard_map/ppermute | solution.py:39
  37.3 3.7 %collective-permute-start.2 = (bf16[264,512]{1,0:T(8,128)(2,1)S(1)}, bf16[264,512]{1,0:T(8,128)(2,1)S(1)}, u32[]{:S(2)}, u32[]{:S(2)}) collective-permute-start(bf16[264,512]{1,0:T(8,128)(2,1)S(1)} %collective-permute-done.1.refs_1_), channel_id=1, source_target_pairs={{0,28},{4,0},{8,4},{12,8},{16,12},{20,16},{24,20},{28,24},{1,29},{... | collective-permute-start | bytes 811016 | tf_op jit(solution)/shard_map/ppermute | solution.py:39
  41.0 4.2 %collective-permute-done.2.refs_2_ = bf16[264,512]{1,0:T(8,128)(2,1)S(1)} collective-permute-done((bf16[264,512]{1,0:T(8,128)(2,1)S(1)}, bf16[264,512]{1,0:T(8,128)(2,1)S(1)}, u32[]{:S(2)}, u32[]{:S(2)}) %collective-permute-start.2) | collective-permute-done | bytes 270368 | tf_op jit(solution)/shard_map/ppermute | solution.py:39
  45.2 3.7 %collective-permute-start.3 = (bf16[264,512]{1,0:T(8,128)(2,1)S(1)}, bf16[264,512]{1,0:T(8,128)(2,1)}, u32[]{:S(2)}, u32[]{:S(2)}) collective-permute-start(bf16[264,512]{1,0:T(8,128)(2,1)S(1)} %collective-permute-done.2.refs_2_), channel_id=1, source_target_pairs={{0,28},{4,0},{8,4},{12,8},{16,12},{20,16},{24,20},{28,24},{1,29},{... | collective-permute-start | bytes 811016 | tf_op jit(solution)/shard_map/ppermute | solution.py:39
  48.9 0.9 constant_dynamic-slice_fusion.4
  50.2 1.0 constant_dynamic-slice_fusion.1
  51.2 2.7 %collective-permute-start.23 = (bf16[256,256]{1,0:T(8,128)(2,1)S(1)}, bf16[256,256]{1,0:T(8,128)(2,1)S(1)}, u32[]{:S(2)}, u32[]{:S(2)}) collective-permute-start(bf16[256,256]{1,0:T(8,128)(2,1)S(1)} %get-tuple-element.24), channel_id=1, source_target_pairs={{0,2},{2,0},{1,3},{3,1},{4,6},{6,4},{5,7},{7,5},{8,10},{10,8},{9,1... | collective-permute-start | bytes 393224 | tf_op jit(solution)/shard_map/ppermute | solution.py:586
  53.9 1.1 constant_dynamic-slice_fusion.2
  55.0 11.1 %collective-permute-done.23 = bf16[256,256]{1,0:T(8,128)(2,1)S(1)} collective-permute-done((bf16[256,256]{1,0:T(8,128)(2,1)S(1)}, bf16[256,256]{1,0:T(8,128)(2,1)S(1)}, u32[]{:S(2)}, u32[]{:S(2)}) %collective-permute-start.23) | collective-permute-done | bytes 131104 | tf_op jit(solution)/shard_map/ppermute | solution.py:586
  66.2 2.2 collective-permute-start.24
  68.4 0.7 copy-done.18
  69.1 9.6 %collective-permute-done.6.refs_6_ = bf16[264,512]{1,0:T(8,128)(2,1)S(1)} collective-permute-done((bf16[264,512]{1,0:T(8,128)(2,1)S(1)}, bf16[264,512]{1,0:T(8,128)(2,1)S(1)}, u32[]{:S(2)}, u32[]{:S(2)}) %collective-permute-start.6) | collective-permute-done | bytes 270368 | tf_op jit(solution)/shard_map/ppermute | solution.py:42
  78.7 3.2 %collective-permute-start.4 = (bf16[264,512]{1,0:T(8,128)(2,1)}, bf16[264,512]{1,0:T(8,128)(2,1)}, u32[]{:S(2)}, u32[]{:S(2)}) collective-permute-start(bf16[264,512]{1,0:T(8,128)(2,1)} %collective-permute-done.3.refs_3_), channel_id=1, source_target_pairs={{0,28},{4,0},{8,4},{12,8},{16,12},{20,16},{24,20},{28,24},{1,29},{... | collective-permute-start | bytes 811016 | tf_op jit(solution)/shard_map/ppermute | solution.py:39
  82.6 2.1 position_bias.1.refs_15_
  84.7 1.8 collective-permute-done.7.refs_5_
  86.5 0.8 copy-done.3
  87.3 9.9 %attention.1 = (bf16[256,512]{1,0:T(8,128)(2,1)}, bf16[256,512]{1,0:T(8,128)(2,1)}, bf16[256,256]{1,0:T(8,128)(2,1)}) custom-call(bf16[264,512]{1,0:T(8,128)(2,1)} %copy-done.5, bf16[264,512]{1,0:T(8,128)(2,1)} %copy-done.16, bf16[264,512]{1,0:T(8,128)(2,1)} %copy-done.17, bf16[264,512]{1,0:T(8,128)(2,1)} %collective-permute-done.3.refs_3_, ...), custom_call_target="tpu_custom_call" | custom-call | flops 2147483648 | bytes 10000000 | tf_op jit(solution)/shard_map/attention/pallas_call | solution.py:271
  97.2 1.0 pad_maximum_fusion
  98.5 3.5 %collective-permute-start.15 = (bf16[256,512]{1,0:T(8,128)(2,1)S(1)}, bf16[256,512]{1,0:T(8,128)(2,1)S(1)}, u32[]{:S(2)}, u32[]{:S(2)}) collective-permute-start(bf16[256,512]{1,0:T(8,128)(2,1)S(1)} %copy-done.20), channel_id=1, source_target_pairs={{0,28},{4,0},{8,4},{12,8},{16,12},{20,16},{24,20},{28,24},{1,29},{... | collective-permute-start | bytes 786440 | tf_op jit(solution)/shard_map/ppermute | solution.py:61
  102.0 4.2 %out_rest.1 = bf16[6,256,512]{2,1,0:T(8,128)(2,1)} custom-call(bf16[256,256]{1,0:T(8,128)(2,1)} %get-tuple-element.22.refs_0_, bf16[256,2048]{1,0:T(8,128)(2,1)} %refs_1_.2, bf16[256,1024]{1,0:T(8,128)(2,1)} %copy-done.2, bf16[256,1024]{1,0:T(8,128)(2,1)} %copy-done.3), custom_call_target="tpu_custom_call" | custom-call | flops 402653184 | bytes 4000000 | tf_op jit(solution)/shard_map/out_rest/pallas_call | solution.py:300
  106.2 2.2 collective-permute-done.11
  108.4 1.0 fusion.10
  109.6 9.0 %collective-permute-done.12 = bf16[256,512]{1,0:T(8,128)(2,1)S(1)} collective-permute-done((bf16[256,512]{1,0:T(8,128)(2,1)S(1)}, bf16[256,512]{1,0:T(8,128)(2,1)S(1)}, u32[]{:S(2)}, u32[]{:S(2)}) %collective-permute-start.12) | collective-permute-done | bytes 262176 | tf_op jit(solution)/shard_map/ppermute | solution.py:59
  118.6 1.2 fusion.9
  119.9 3.2 %collective-permute-start.16 = (bf16[256,512]{1,0:T(8,128)(2,1)S(1)}, bf16[256,512]{1,0:T(8,128)(2,1)S(1)}, u32[]{:S(2)}, u32[]{:S(2)}) collective-permute-start(bf16[256,512]{1,0:T(8,128)(2,1)S(1)} %get-tuple-element.42), channel_id=1, source_target_pairs={{0,28},{4,0},{8,4},{12,8},{16,12},{20,16},{24,20},{28,24},{1,29},{... | collective-permute-start | bytes 786440 | tf_op jit(solution)/shard_map/ppermute | solution.py:61
  123.1 4.3 %collective-permute-done.13 = bf16[256,512]{1,0:T(8,128)(2,1)S(1)} collective-permute-done((bf16[256,512]{1,0:T(8,128)(2,1)S(1)}, bf16[256,512]{1,0:T(8,128)(2,1)S(1)}, u32[]{:S(2)}, u32[]{:S(2)}) %collective-permute-start.13) | collective-permute-done | bytes 262176 | tf_op jit(solution)/shard_map/ppermute | solution.py:59
  127.7 3.3 %collective-permute-start.17 = (bf16[256,512]{1,0:T(8,128)(2,1)S(1)}, bf16[256,512]{1,0:T(8,128)(2,1)S(1)}, u32[]{:S(2)}, u32[]{:S(2)}) collective-permute-start(bf16[256,512]{1,0:T(8,128)(2,1)S(1)} %get-tuple-element.40), channel_id=1, source_target_pairs={{0,28},{4,0},{8,4},{12,8},{16,12},{20,16},{24,20},{28,24},{1,29},{... | collective-permute-start | bytes 786440 | tf_op jit(solution)/shard_map/ppermute | solution.py:61
  131.0 4.3 %collective-permute-done.14 = bf16[256,512]{1,0:T(8,128)(2,1)S(1)} collective-permute-done((bf16[256,512]{1,0:T(8,128)(2,1)S(1)}, bf16[256,512]{1,0:T(8,128)(2,1)S(1)}, u32[]{:S(2)}, u32[]{:S(2)}) %collective-permute-start.14) | collective-permute-done | bytes 262176 | tf_op jit(solution)/shard_map/ppermute | solution.py:59
  135.5 7.9 %collective-permute-done.18 = bf16[256,512]{1,0:T(8,128)(2,1)S(1)} collective-permute-done((bf16[256,512]{1,0:T(8,128)(2,1)S(1)}, bf16[256,512]{1,0:T(8,128)(2,1)S(1)}, u32[]{:S(2)}, u32[]{:S(2)}) %collective-permute-start.18) | collective-permute-done | bytes 262176 | tf_op jit(solution)/shard_map/ppermute | solution.py:602
  143.7 3.4 %collective-permute-start.19 = (bf16[264,512]{1,0:T(8,128)(2,1)S(1)}, bf16[264,512]{1,0:T(8,128)(2,1)S(1)}, u32[]{:S(2)}, u32[]{:S(2)}) collective-permute-start(bf16[264,512]{1,0:T(8,128)(2,1)S(1)} %pad_maximum_fusion.4.refs_0_), channel_id=1, source_target_pairs={{0,28},{4,0},{8,4},{12,8},{16,12},{20,16},{24,20},{28,24},{1,29},{... | collective-permute-start | bytes 811016 | tf_op jit(solution)/shard_map/ppermute | solution.py:39
  147.1 6.2 %collective-permute-done.19.refs_1_ = bf16[264,512]{1,0:T(8,128)(2,1)S(1)} collective-permute-done((bf16[264,512]{1,0:T(8,128)(2,1)S(1)}, bf16[264,512]{1,0:T(8,128)(2,1)S(1)}, u32[]{:S(2)}, u32[]{:S(2)}) %collective-permute-start.19) | collective-permute-done | bytes 270368 | tf_op jit(solution)/shard_map/ppermute | solution.py:39
  153.3 3.7 %collective-permute-start.20 = (bf16[264,512]{1,0:T(8,128)(2,1)S(1)}, bf16[264,512]{1,0:T(8,128)(2,1)S(1)}, u32[]{:S(2)}, u32[]{:S(2)}) collective-permute-start(bf16[264,512]{1,0:T(8,128)(2,1)S(1)} %collective-permute-done.19.refs_1_), channel_id=1, source_target_pairs={{0,28},{4,0},{8,4},{12,8},{16,12},{20,16},{24,20},{28,24},{1,29},{... | collective-permute-start | bytes 811016 | tf_op jit(solution)/shard_map/ppermute | solution.py:39
  157.3 6.1 %collective-permute-done.20.refs_0_ = bf16[264,512]{1,0:T(8,128)(2,1)S(1)} collective-permute-done((bf16[264,512]{1,0:T(8,128)(2,1)S(1)}, bf16[264,512]{1,0:T(8,128)(2,1)S(1)}, u32[]{:S(2)}, u32[]{:S(2)}) %collective-permute-start.20) | collective-permute-done | bytes 270368 | tf_op jit(solution)/shard_map/ppermute | solution.py:39
  163.4 3.7 %collective-permute-start.21 = (bf16[264,512]{1,0:T(8,128)(2,1)S(1)}, bf16[264,512]{1,0:T(8,128)(2,1)S(1)}, u32[]{:S(2)}, u32[]{:S(2)}) collective-permute-start(bf16[264,512]{1,0:T(8,128)(2,1)S(1)} %collective-permute-done.20.refs_0_), channel_id=1, source_target_pairs={{0,28},{4,0},{8,4},{12,8},{16,12},{20,16},{24,20},{28,24},{1,29},{... | collective-permute-start | bytes 811016 | tf_op jit(solution)/shard_map/ppermute | solution.py:39
  167.1 4.0 %collective-permute-done.21.refs_0_ = bf16[264,512]{1,0:T(8,128)(2,1)S(1)} collective-permute-done((bf16[264,512]{1,0:T(8,128)(2,1)S(1)}, bf16[264,512]{1,0:T(8,128)(2,1)S(1)}, u32[]{:S(2)}, u32[]{:S(2)}) %collective-permute-start.21) | collective-permute-done | bytes 270368 | tf_op jit(solution)/shard_map/ppermute | solution.py:39
  171.0 3.7 %collective-permute-start.22 = (bf16[264,512]{1,0:T(8,128)(2,1)S(1)}, bf16[264,512]{1,0:T(8,128)(2,1)S(1)}, u32[]{:S(2)}, u32[]{:S(2)}) collective-permute-start(bf16[264,512]{1,0:T(8,128)(2,1)S(1)} %collective-permute-done.21.refs_0_), channel_id=1, source_target_pairs={{0,28},{4,0},{8,4},{12,8},{16,12},{20,16},{24,20},{28,24},{1,29},{... | collective-permute-start | bytes 811016 | tf_op jit(solution)/shard_map/ppermute | solution.py:39
  174.7 4.5 %shard_map.109 = (f32[256,1024]{1,0:T(8,128)}, f32[8,256]{1,0:T(8,128)}) custom-call(bf16[264,512]{1,0:T(8,128)(2,1)} %copy-done.4, bf16[264,512]{1,0:T(8,128)(2,1)} %copy-done.9, bf16[264,512]{1,0:T(8,128)(2,1)} %copy-done.10, bf16[4096,256]{1,0:T(8,128)(2,1)} %refs_1_.3, bf16[4096,256]{1,0:T(8,128)(2,1)} %refs_2_.5, bf16[8,1792,256]{2,1,0:T(8,128)(2,1)} %bitcast.67), custom_call_target="tpu_custom_call" | custom-call | flops 805306368 | bytes 4000000 | tf_op jit(solution)/shard_map/pallas_call | solution.py:474
  179.3 4.0 %shard_map.110 = (f32[256,1024]{1,0:T(8,128)}, f32[8,256]{1,0:T(8,128)}) custom-call(bf16[264,512]{1,0:T(8,128)(2,1)} %copy-done.11, bf16[264,512]{1,0:T(8,128)(2,1)} %copy-done.13, bf16[4096,256]{1,0:T(8,128)(2,1)} %refs_1_.3, bf16[4096,256]{1,0:T(8,128)(2,1)} %refs_2_.5, bf16[8,1792,256]{2,1,0:T(8,128)(2,1)} %bitcast.68, ...), custom_call_target="tpu_custom_call" | custom-call | flops 536870912 | bytes 3000000 | tf_op jit(solution)/shard_map/pallas_call | solution.py:474
  183.4 0.7 copy-done.15
  184.1 4.1 %shard_map.111 = (f32[256,1024]{1,0:T(8,128)}, f32[8,256]{1,0:T(8,128)}) custom-call(bf16[264,512]{1,0:T(8,128)(2,1)} %copy-done.12, bf16[264,512]{1,0:T(8,128)(2,1)} %copy-done.15, bf16[4096,256]{1,0:T(8,128)(2,1)} %refs_1_.3, bf16[4096,256]{1,0:T(8,128)(2,1)} %refs_2_.5, bf16[8,1792,256]{2,1,0:T(8,128)(2,1)} %bitcast.69, ...), custom_call_target="tpu_custom_call" | custom-call | flops 536870912 | bytes 3000000 | tf_op jit(solution)/shard_map/pallas_call | solution.py:474
  188.2 0.7 copy-done.14
  188.9 2.9 %hidden.1.mine_ref = bf16[256,512]{1,0:T(8,128)(2,1)} custom-call(bf16[264,512]{1,0:T(8,128)(2,1)} %copy-done.14, bf16[4096,256]{1,0:T(8,128)(2,1)} %refs_1_.3, bf16[4096,256]{1,0:T(8,128)(2,1)} %refs_2_.5, bf16[8,1792,256]{2,1,0:T(8,128)(2,1)} %bitcast.70, f32[256,1024]{1,0:T(8,128)} %get-tuple-element.31.refs_4_, f32[8,256]{1,0:T(8,128)} %get-tuple-element.32.refs_5_), custom_call_target="tpu_custom_call" | custom-call | flops 268435456 | bytes 2000000 | tf_op jit(solution)/shard_map/hidden/pallas_call | solution.py:486
  191.9 8.1 %collective-permute-done.28.theirs_ref = bf16[256,512]{1,0:T(8,128)(2,1)S(1)} collective-permute-done((bf16[256,512]{1,0:T(8,128)(2,1)}, bf16[256,512]{1,0:T(8,128)(2,1)S(1)}, u32[]{:S(2)}, u32[]{:S(2)}) %collective-permute-start.28) | collective-permute-done | bytes 262176 | tf_op jit(solution)/shard_map/ppermute | solution.py:495
  200.0 0.7 copy-done.6
  200.7 2.7 %shard_map.112 = (bf16[256,256]{1,0:T(8,128)(2,1)}, bf16[256,256]{1,0:T(8,128)(2,1)}) custom-call(bf16[256,512]{1,0:T(8,128)(2,1)} %hidden.1.mine_ref, bf16[256,512]{1,0:T(8,128)(2,1)} %copy-done.6, bf16[256,4096]{1,0:T(8,128)(2,1)} %down_ref.3, bf16[8,1792,256]{2,1,0:T(8,128)(2,1)} %bitcast.71), custom_call_target="tpu_custom_call" | custom-call | flops 268435456 | bytes 2000000 | tf_op jit(solution)/shard_map/pallas_call | solution.py:498
  203.5 3.2 %collective-permute-start.33 = (bf16[256,256]{1,0:T(8,128)(2,1)}, bf16[256,256]{1,0:T(8,128)(2,1)S(1)}, u32[]{:S(2)}, u32[]{:S(2)}) collective-permute-start(bf16[256,256]{1,0:T(8,128)(2,1)} %get-tuple-element.34), channel_id=1, source_target_pairs={{0,28},{4,0},{8,4},{12,8},{16,12},{20,16},{24,20},{28,24},{1,29},{... | collective-permute-start | bytes 393224 | tf_op jit(solution)/shard_map/ppermute | solution.py:61
  206.7 5.1 %shard_map.113 = bf16[6,256,256]{2,1,0:T(8,128)(2,1)} custom-call(bf16[256,512]{1,0:T(8,128)(2,1)} %hidden.1.mine_ref, bf16[256,512]{1,0:T(8,128)(2,1)} %copy-done.6, bf16[256,4096]{1,0:T(8,128)(2,1)} %down_ref.3, bf16[8,1792,256]{2,1,0:T(8,128)(2,1)} %bitcast.72), custom_call_target="tpu_custom_call" | custom-call | flops 268435456 | bytes 2000000 | tf_op jit(solution)/shard_map/pallas_call | solution.py:498
  211.9 0.9 fusion.17
  212.9 6.2 %collective-permute-done.30 = bf16[256,256]{1,0:T(8,128)(2,1)S(1)} collective-permute-done((bf16[256,256]{1,0:T(8,128)(2,1)S(1)}, bf16[256,256]{1,0:T(8,128)(2,1)S(1)}, u32[]{:S(2)}, u32[]{:S(2)}) %collective-permute-start.30) | collective-permute-done | bytes 131104 | tf_op jit(solution)/shard_map/ppermute | solution.py:59
  219.0 1.0 fusion.16
  220.2 3.2 %collective-permute-start.34 = (bf16[256,256]{1,0:T(8,128)(2,1)S(1)}, bf16[256,256]{1,0:T(8,128)(2,1)S(1)}, u32[]{:S(2)}, u32[]{:S(2)}) collective-permute-start(bf16[256,256]{1,0:T(8,128)(2,1)S(1)} %get-tuple-element.46), channel_id=1, source_target_pairs={{0,28},{4,0},{8,4},{12,8},{16,12},{20,16},{24,20},{28,24},{1,29},{... | collective-permute-start | bytes 393224 | tf_op jit(solution)/shard_map/ppermute | solution.py:61
  223.4 2.9 %collective-permute-done.31 = bf16[256,256]{1,0:T(8,128)(2,1)S(1)} collective-permute-done((bf16[256,256]{1,0:T(8,128)(2,1)S(1)}, bf16[256,256]{1,0:T(8,128)(2,1)S(1)}, u32[]{:S(2)}, u32[]{:S(2)}) %collective-permute-start.31) | collective-permute-done | bytes 131104 | tf_op jit(solution)/shard_map/ppermute | solution.py:59
  226.4 1.0 fusion.15
  227.5 3.3 %collective-permute-start.35 = (bf16[256,256]{1,0:T(8,128)(2,1)S(1)}, bf16[256,256]{1,0:T(8,128)(2,1)S(1)}, u32[]{:S(2)}, u32[]{:S(2)}) collective-permute-start(bf16[256,256]{1,0:T(8,128)(2,1)S(1)} %get-tuple-element.44), channel_id=1, source_target_pairs={{0,28},{4,0},{8,4},{12,8},{16,12},{20,16},{24,20},{28,24},{1,29},{... | collective-permute-start | bytes 393224 | tf_op jit(solution)/shard_map/ppermute | solution.py:61
  230.8 2.9 %collective-permute-done.32 = bf16[256,256]{1,0:T(8,128)(2,1)S(1)} collective-permute-done((bf16[256,256]{1,0:T(8,128)(2,1)S(1)}, bf16[256,256]{1,0:T(8,128)(2,1)S(1)}, u32[]{:S(2)}, u32[]{:S(2)}) %collective-permute-start.32) | collective-permute-done | bytes 131104 | tf_op jit(solution)/shard_map/ppermute | solution.py:59
  233.7 1.7 fusion.18
  (104 shorter events, 3.7 us)
Async XLA Ops:
  6.5 13.8 %copy-start.22 = (bf16[256]{0:T(256)(128)(2,1)S(1)}, bf16[256]{0:T(256)(128)(2,1)}, u32[]{:S(2)}) copy-start(bf16[256]{0:T(256)(128)(2,1)} %param.12) | copy-start | bytes 1540
  6.5 13.8 %copy-start.23 = (bf16[256]{0:T(256)(128)(2,1)S(1)}, bf16[256]{0:T(256)(128)(2,1)}, u32[]{:S(2)}) copy-start(bf16[256]{0:T(256)(128)(2,1)} %param.18) | copy-start | bytes 1540
  6.5 13.8 %copy-start.7 = (bf16[1,256,256]{2,1,0:T(8,128)(2,1)S(1)}, bf16[1,256,256]{2,1,0:T(8,128)(2,1)}, u32[]{:S(2)}) copy-start(bf16[1,256,256]{2,1,0:T(8,128)(2,1)} %param.11) | copy-start | bytes 393220
  6.5 80.0 %all-gather.4.cloned.1.call-start = ((), (), s32[]{:S(2)}) async-start(), calls=%async_computation | async-start | bytes 3538944 | tf_op jit(solution)/shard_map/all_gather | solution.py:559
  8.5 40.4 %copy-start = (bf16[256,2048]{1,0:T(8,128)(2,1)S(1)}, bf16[256,2048]{1,0:T(8,128)(2,1)}, u32[]{:S(2)}) copy-start(bf16[256,2048]{1,0:T(8,128)(2,1)} %refs_1_.2) | copy-start | bytes 3145732
  8.5 10.9 %collective-permute-start.8 = (bf16[256,768]{1,0:T(8,128)(2,1)S(1)}, bf16[256,768]{1,0:T(8,128)(2,1)S(1)}, u32[]{:S(2)}, u32[]{:S(2)}) collective-permute-start(bf16[256,768]{1,0:T(8,128)(2,1)S(1)} %pad_maximum_fusion.2), channel_id=1, source_target_pairs={{0,1},{1,0},{2,3},{3,2},{4,5},{5,4},{6,7},{7,6},{8,9},{9,8},{10,11... | collective-permute-start | bytes 1179656 | tf_op jit(solution)/shard_map/ppermute | solution.py:558
  19.5 0.8 copy-start.8
  20.3 154.5 %all-gather.6.cloned.1.call-start = ((), (), s32[]{:S(2)}) async-start(), calls=%async_computation.1 | async-start | bytes 8257536 | tf_op jit(solution)/shard_map/all_gather | solution.py:600
  20.4 6.6 %collective-permute-start = (bf16[264,256]{1,0:T(8,128)(2,1)S(1)}, bf16[264,256]{1,0:T(8,128)(2,1)S(1)}, u32[]{:S(2)}, u32[]{:S(2)}) collective-permute-start(bf16[264,256]{1,0:T(8,128)(2,1)S(1)} %pad_maximum_fusion.5), channel_id=1, source_target_pairs={{0,2},{2,0},{1,3},{3,1},{4,6},{6,4},{5,7},{7,5},{8,10},{10,8},{9,1... | collective-permute-start | bytes 405512 | tf_op jit(solution)/shard_map/ppermute | solution.py:550
  27.3 38.8 %copy-start.5 = (bf16[264,512]{1,0:T(8,128)(2,1)}, bf16[264,512]{1,0:T(8,128)(2,1)S(1)}, u32[]{:S(2)}) copy-start(bf16[264,512]{1,0:T(8,128)(2,1)S(1)} %pad_maximum_fusion.3.refs_0_) | copy-start | bytes 811012
  27.4 9.9 %collective-permute-start.1 = (bf16[264,512]{1,0:T(8,128)(2,1)S(1)}, bf16[264,512]{1,0:T(8,128)(2,1)S(1)}, u32[]{:S(2)}, u32[]{:S(2)}) collective-permute-start(bf16[264,512]{1,0:T(8,128)(2,1)S(1)} %pad_maximum_fusion.3.refs_0_), channel_id=1, source_target_pairs={{0,28},{4,0},{8,4},{12,8},{16,12},{20,16},{24,20},{28,24},{1,29},{... | collective-permute-start | bytes 811016 | tf_op jit(solution)/shard_map/ppermute | solution.py:39
  37.3 12.5 %copy-start.16 = (bf16[264,512]{1,0:T(8,128)(2,1)}, bf16[264,512]{1,0:T(8,128)(2,1)S(1)}, u32[]{:S(2)}) copy-start(bf16[264,512]{1,0:T(8,128)(2,1)S(1)} %collective-permute-done.1.refs_1_) | copy-start | bytes 811012
  37.3 7.9 %collective-permute-start.2 = (bf16[264,512]{1,0:T(8,128)(2,1)S(1)}, bf16[264,512]{1,0:T(8,128)(2,1)S(1)}, u32[]{:S(2)}, u32[]{:S(2)}) collective-permute-start(bf16[264,512]{1,0:T(8,128)(2,1)S(1)} %collective-permute-done.1.refs_1_), channel_id=1, source_target_pairs={{0,28},{4,0},{8,4},{12,8},{16,12},{20,16},{24,20},{28,24},{1,29},{... | collective-permute-start | bytes 811016 | tf_op jit(solution)/shard_map/ppermute | solution.py:39
  45.2 20.9 %copy-start.17 = (bf16[264,512]{1,0:T(8,128)(2,1)}, bf16[264,512]{1,0:T(8,128)(2,1)S(1)}, u32[]{:S(2)}) copy-start(bf16[264,512]{1,0:T(8,128)(2,1)S(1)} %collective-permute-done.2.refs_2_) | copy-start | bytes 811012
  45.2 20.9 %collective-permute-start.3 = (bf16[264,512]{1,0:T(8,128)(2,1)S(1)}, bf16[264,512]{1,0:T(8,128)(2,1)}, u32[]{:S(2)}, u32[]{:S(2)}) collective-permute-start(bf16[264,512]{1,0:T(8,128)(2,1)S(1)} %collective-permute-done.2.refs_2_), channel_id=1, source_target_pairs={{0,28},{4,0},{8,4},{12,8},{16,12},{20,16},{24,20},{28,24},{1,29},{... | collective-permute-start | bytes 811016 | tf_op jit(solution)/shard_map/ppermute | solution.py:39
  49.7 18.7 %collective-permute-start.9 = (bf16[256,1024]{1,0:T(8,128)(2,1)}, bf16[256,1024]{1,0:T(8,128)(2,1)S(1)}, u32[]{:S(2)}, u32[]{:S(2)}) collective-permute-start(bf16[256,1024]{1,0:T(8,128)(2,1)} %constant_dynamic-slice_fusion.4), channel_id=1, source_target_pairs={{0,1},{1,0},{2,3},{3,2},{4,5},{5,4},{6,7},{7,6},{8,9},{9,8},{10,11... | collective-permute-start | bytes 1572872 | tf_op jit(solution)/shard_map/ppermute | solution.py:582
  51.2 14.9 %collective-permute-start.23 = (bf16[256,256]{1,0:T(8,128)(2,1)S(1)}, bf16[256,256]{1,0:T(8,128)(2,1)S(1)}, u32[]{:S(2)}, u32[]{:S(2)}) collective-permute-start(bf16[256,256]{1,0:T(8,128)(2,1)S(1)} %get-tuple-element.24), channel_id=1, source_target_pairs={{0,2},{2,0},{1,3},{3,1},{4,6},{6,4},{5,7},{7,5},{8,10},{10,8},{9,1... | collective-permute-start | bytes 393224 | tf_op jit(solution)/shard_map/ppermute | solution.py:586
  54.9 13.5 %collective-permute-start.5 = (bf16[264,512]{1,0:T(8,128)(2,1)S(1)}, bf16[264,512]{1,0:T(8,128)(2,1)S(1)}, u32[]{:S(2)}, u32[]{:S(2)}) collective-permute-start(bf16[264,512]{1,0:T(8,128)(2,1)S(1)} %pad_maximum_fusion.3.refs_0_), channel_id=1, source_target_pairs={{0,4},{4,8},{8,12},{12,16},{16,20},{20,24},{24,28},{28,0},{1,5},{5... | collective-permute-start | bytes 811016 | tf_op jit(solution)/shard_map/ppermute | solution.py:42
  66.2 31.0 %collective-permute-start.24 = (bf16[1536,256]{1,0:T(8,128)(2,1)S(1)}, bf16[1536,256]{1,0:T(8,128)(2,1)S(1)}, u32[]{:S(2)}, u32[]{:S(2)}) collective-permute-start(bf16[1536,256]{1,0:T(8,128)(2,1)S(1)} %pad_maximum_fusion.1), channel_id=1, source_target_pairs={{0,1},{1,0},{2,3},{3,2},{4,5},{5,4},{6,7},{7,6},{8,9},{9,8},{10,11... | collective-permute-start | bytes 2359304 | tf_op jit(solution)/shard_map/ppermute | solution.py:590
  68.4 0.7 copy-start.18
  68.4 10.3 %collective-permute-start.6 = (bf16[264,512]{1,0:T(8,128)(2,1)S(1)}, bf16[264,512]{1,0:T(8,128)(2,1)S(1)}, u32[]{:S(2)}, u32[]{:S(2)}) collective-permute-start(bf16[264,512]{1,0:T(8,128)(2,1)S(1)} %collective-permute-done.5.refs_7_), channel_id=1, source_target_pairs={{0,4},{4,8},{8,12},{12,16},{16,20},{20,24},{24,28},{28,0},{1,5},{5... | collective-permute-start | bytes 811016 | tf_op jit(solution)/shard_map/ppermute | solution.py:42
  69.1 17.4 %copy-start.2 = (bf16[256,1024]{1,0:T(8,128)(2,1)}, bf16[256,1024]{1,0:T(8,128)(2,1)S(1)}, u32[]{:S(2)}) copy-start(bf16[256,1024]{1,0:T(8,128)(2,1)S(1)} %collective-permute-done.9.refs_13_.refs_2_) | copy-start | bytes 1572868
  69.1 17.4 %collective-permute-start.10 = (bf16[256,1024]{1,0:T(8,128)(2,1)S(1)}, bf16[256,1024]{1,0:T(8,128)(2,1)S(1)}, u32[]{:S(2)}, u32[]{:S(2)}) collective-permute-start(bf16[256,1024]{1,0:T(8,128)(2,1)S(1)} %collective-permute-done.9.refs_13_.refs_2_), channel_id=1, source_target_pairs={{0,32},{32,0},{64,96},{96,64},{128,160},{160,128},{192,224},{224,1... | collective-permute-start | bytes 1572872 | tf_op jit(solution)/shard_map/ppermute | solution.py:584
  78.7 7.8 %copy-start.19 = (bf16[264,512]{1,0:T(8,128)(2,1)}, bf16[264,512]{1,0:T(8,128)(2,1)S(1)}, u32[]{:S(2)}) copy-start(bf16[264,512]{1,0:T(8,128)(2,1)S(1)} %collective-permute-done.6.refs_6_) | copy-start | bytes 811012
  78.7 7.8 %collective-permute-start.7 = (bf16[264,512]{1,0:T(8,128)(2,1)S(1)}, bf16[264,512]{1,0:T(8,128)(2,1)}, u32[]{:S(2)}, u32[]{:S(2)}) collective-permute-start(bf16[264,512]{1,0:T(8,128)(2,1)S(1)} %collective-permute-done.6.refs_6_), channel_id=1, source_target_pairs={{0,4},{4,8},{8,12},{12,16},{16,20},{20,24},{24,28},{28,0},{1,5},{5... | collective-permute-start | bytes 811016 | tf_op jit(solution)/shard_map/ppermute | solution.py:42
  78.7 7.8 %collective-permute-start.4 = (bf16[264,512]{1,0:T(8,128)(2,1)}, bf16[264,512]{1,0:T(8,128)(2,1)}, u32[]{:S(2)}, u32[]{:S(2)}) collective-permute-start(bf16[264,512]{1,0:T(8,128)(2,1)} %collective-permute-done.3.refs_3_), channel_id=1, source_target_pairs={{0,28},{4,0},{8,4},{12,8},{16,12},{20,16},{24,20},{28,24},{1,29},{... | collective-permute-start | bytes 811016 | tf_op jit(solution)/shard_map/ppermute | solution.py:39
  86.5 0.8 copy-start.3
  97.2 1.0 copy-start.21
  97.2 1.3 copy-start.20
  98.2 10.2 %collective-permute-start.11 = (bf16[256,512]{1,0:T(8,128)(2,1)S(1)}, bf16[256,512]{1,0:T(8,128)(2,1)S(1)}, u32[]{:S(2)}, u32[]{:S(2)}) collective-permute-start(bf16[256,512]{1,0:T(8,128)(2,1)S(1)} %copy-done.21), channel_id=1, source_target_pairs={{0,4},{4,8},{8,12},{12,16},{16,20},{20,24},{24,28},{28,0},{1,5},{5... | collective-permute-start | bytes 786440 | tf_op jit(solution)/shard_map/ppermute | solution.py:59
  98.5 11.1 %collective-permute-start.15 = (bf16[256,512]{1,0:T(8,128)(2,1)S(1)}, bf16[256,512]{1,0:T(8,128)(2,1)S(1)}, u32[]{:S(2)}, u32[]{:S(2)}) collective-permute-start(bf16[256,512]{1,0:T(8,128)(2,1)S(1)} %copy-done.20), channel_id=1, source_target_pairs={{0,28},{4,0},{8,4},{12,8},{16,12},{20,16},{24,20},{28,24},{1,29},{... | collective-permute-start | bytes 786440 | tf_op jit(solution)/shard_map/ppermute | solution.py:61
  106.2 21.2 %copy-start.1 = (bf16[6,256,512]{2,1,0:T(8,128)(2,1)S(1)}, bf16[6,256,512]{2,1,0:T(8,128)(2,1)}, u32[]{:S(2)}) copy-start(bf16[6,256,512]{2,1,0:T(8,128)(2,1)} %out_rest.1) | copy-start | bytes 4718596
  109.5 9.1 %collective-permute-start.12 = (bf16[256,512]{1,0:T(8,128)(2,1)S(1)}, bf16[256,512]{1,0:T(8,128)(2,1)S(1)}, u32[]{:S(2)}, u32[]{:S(2)}) collective-permute-start(bf16[256,512]{1,0:T(8,128)(2,1)S(1)} %fusion.10), channel_id=1, source_target_pairs={{0,4},{4,8},{8,12},{12,16},{16,20},{20,24},{24,28},{28,0},{1,5},{5... | collective-permute-start | bytes 786440 | tf_op jit(solution)/shard_map/ppermute | solution.py:59
  119.8 7.7 %collective-permute-start.13 = (bf16[256,512]{1,0:T(8,128)(2,1)S(1)}, bf16[256,512]{1,0:T(8,128)(2,1)S(1)}, u32[]{:S(2)}, u32[]{:S(2)}) collective-permute-start(bf16[256,512]{1,0:T(8,128)(2,1)S(1)} %get-tuple-element.41), channel_id=1, source_target_pairs={{0,4},{4,8},{8,12},{12,16},{16,20},{20,24},{24,28},{28,0},{1,5},{5... | collective-permute-start | bytes 786440 | tf_op jit(solution)/shard_map/ppermute | solution.py:59
  119.9 7.6 %collective-permute-start.16 = (bf16[256,512]{1,0:T(8,128)(2,1)S(1)}, bf16[256,512]{1,0:T(8,128)(2,1)S(1)}, u32[]{:S(2)}, u32[]{:S(2)}) collective-permute-start(bf16[256,512]{1,0:T(8,128)(2,1)S(1)} %get-tuple-element.42), channel_id=1, source_target_pairs={{0,28},{4,0},{8,4},{12,8},{16,12},{20,16},{24,20},{28,24},{1,29},{... | collective-permute-start | bytes 786440 | tf_op jit(solution)/shard_map/ppermute | solution.py:61
  127.6 7.7 %collective-permute-start.14 = (bf16[256,512]{1,0:T(8,128)(2,1)S(1)}, bf16[256,512]{1,0:T(8,128)(2,1)S(1)}, u32[]{:S(2)}, u32[]{:S(2)}) collective-permute-start(bf16[256,512]{1,0:T(8,128)(2,1)S(1)} %get-tuple-element.39), channel_id=1, source_target_pairs={{0,4},{4,8},{8,12},{12,16},{16,20},{20,24},{24,28},{28,0},{1,5},{5... | collective-permute-start | bytes 786440 | tf_op jit(solution)/shard_map/ppermute | solution.py:59
  127.7 7.6 %collective-permute-start.17 = (bf16[256,512]{1,0:T(8,128)(2,1)S(1)}, bf16[256,512]{1,0:T(8,128)(2,1)S(1)}, u32[]{:S(2)}, u32[]{:S(2)}) collective-permute-start(bf16[256,512]{1,0:T(8,128)(2,1)S(1)} %get-tuple-element.40), channel_id=1, source_target_pairs={{0,28},{4,0},{8,4},{12,8},{16,12},{20,16},{24,20},{28,24},{1,29},{... | collective-permute-start | bytes 786440 | tf_op jit(solution)/shard_map/ppermute | solution.py:61
  135.4 8.0 %collective-permute-start.18 = (bf16[256,512]{1,0:T(8,128)(2,1)S(1)}, bf16[256,512]{1,0:T(8,128)(2,1)S(1)}, u32[]{:S(2)}, u32[]{:S(2)}) collective-permute-start(bf16[256,512]{1,0:T(8,128)(2,1)S(1)} %fusion.5), channel_id=1, source_target_pairs={{0,2},{2,0},{1,3},{3,1},{4,6},{6,4},{5,7},{7,5},{8,10},{10,8},{9,1... | collective-permute-start | bytes 786440 | tf_op jit(solution)/shard_map/ppermute | solution.py:602
  143.7 31.1 %copy-start.4 = (bf16[264,512]{1,0:T(8,128)(2,1)}, bf16[264,512]{1,0:T(8,128)(2,1)S(1)}, u32[]{:S(2)}) copy-start(bf16[264,512]{1,0:T(8,128)(2,1)S(1)} %pad_maximum_fusion.4.refs_0_) | copy-start | bytes 811012
  143.7 9.6 %collective-permute-start.19 = (bf16[264,512]{1,0:T(8,128)(2,1)S(1)}, bf16[264,512]{1,0:T(8,128)(2,1)S(1)}, u32[]{:S(2)}, u32[]{:S(2)}) collective-permute-start(bf16[264,512]{1,0:T(8,128)(2,1)S(1)} %pad_maximum_fusion.4.refs_0_), channel_id=1, source_target_pairs={{0,28},{4,0},{8,4},{12,8},{16,12},{20,16},{24,20},{28,24},{1,29},{... | collective-permute-start | bytes 811016 | tf_op jit(solution)/shard_map/ppermute | solution.py:39
  147.1 10.2 %collective-permute-start.25 = (bf16[264,512]{1,0:T(8,128)(2,1)S(1)}, bf16[264,512]{1,0:T(8,128)(2,1)S(1)}, u32[]{:S(2)}, u32[]{:S(2)}) collective-permute-start(bf16[264,512]{1,0:T(8,128)(2,1)S(1)} %pad_maximum_fusion.4.refs_0_), channel_id=1, source_target_pairs={{0,4},{4,8},{8,12},{12,16},{16,20},{20,24},{24,28},{28,0},{1,5},{5... | collective-permute-start | bytes 811016 | tf_op jit(solution)/shard_map/ppermute | solution.py:42
  153.3 21.4 %copy-start.9 = (bf16[264,512]{1,0:T(8,128)(2,1)}, bf16[264,512]{1,0:T(8,128)(2,1)S(1)}, u32[]{:S(2)}) copy-start(bf16[264,512]{1,0:T(8,128)(2,1)S(1)} %collective-permute-done.19.refs_1_) | copy-start | bytes 811012
  153.3 10.1 %collective-permute-start.20 = (bf16[264,512]{1,0:T(8,128)(2,1)S(1)}, bf16[264,512]{1,0:T(8,128)(2,1)S(1)}, u32[]{:S(2)}, u32[]{:S(2)}) collective-permute-start(bf16[264,512]{1,0:T(8,128)(2,1)S(1)} %collective-permute-done.19.refs_1_), channel_id=1, source_target_pairs={{0,28},{4,0},{8,4},{12,8},{16,12},{20,16},{24,20},{28,24},{1,29},{... | collective-permute-start | bytes 811016 | tf_op jit(solution)/shard_map/ppermute | solution.py:39
  157.3 17.5 %copy-start.10 = (bf16[264,512]{1,0:T(8,128)(2,1)}, bf16[264,512]{1,0:T(8,128)(2,1)S(1)}, u32[]{:S(2)}) copy-start(bf16[264,512]{1,0:T(8,128)(2,1)S(1)} %collective-permute-done.25.refs_2_) | copy-start | bytes 811012
  157.3 9.8 %collective-permute-start.26 = (bf16[264,512]{1,0:T(8,128)(2,1)S(1)}, bf16[264,512]{1,0:T(8,128)(2,1)S(1)}, u32[]{:S(2)}, u32[]{:S(2)}) collective-permute-start(bf16[264,512]{1,0:T(8,128)(2,1)S(1)} %collective-permute-done.25.refs_2_), channel_id=1, source_target_pairs={{0,4},{4,8},{8,12},{12,16},{16,20},{20,24},{24,28},{28,0},{1,5},{5... | collective-permute-start | bytes 811016 | tf_op jit(solution)/shard_map/ppermute | solution.py:42
  163.4 15.9 %copy-start.11 = (bf16[264,512]{1,0:T(8,128)(2,1)}, bf16[264,512]{1,0:T(8,128)(2,1)S(1)}, u32[]{:S(2)}) copy-start(bf16[264,512]{1,0:T(8,128)(2,1)S(1)} %collective-permute-done.20.refs_0_) | copy-start | bytes 811012
  163.4 7.7 %collective-permute-start.21 = (bf16[264,512]{1,0:T(8,128)(2,1)S(1)}, bf16[264,512]{1,0:T(8,128)(2,1)S(1)}, u32[]{:S(2)}, u32[]{:S(2)}) collective-permute-start(bf16[264,512]{1,0:T(8,128)(2,1)S(1)} %collective-permute-done.20.refs_0_), channel_id=1, source_target_pairs={{0,28},{4,0},{8,4},{12,8},{16,12},{20,16},{24,20},{28,24},{1,29},{... | collective-permute-start | bytes 811016 | tf_op jit(solution)/shard_map/ppermute | solution.py:39
  167.1 12.2 %copy-start.13 = (bf16[264,512]{1,0:T(8,128)(2,1)}, bf16[264,512]{1,0:T(8,128)(2,1)S(1)}, u32[]{:S(2)}) copy-start(bf16[264,512]{1,0:T(8,128)(2,1)S(1)} %collective-permute-done.26.refs_1_) | copy-start | bytes 811012
  167.1 16.3 %collective-permute-start.27 = (bf16[264,512]{1,0:T(8,128)(2,1)S(1)}, bf16[264,512]{1,0:T(8,128)(2,1)S(1)}, u32[]{:S(2)}, u32[]{:S(2)}) collective-permute-start(bf16[264,512]{1,0:T(8,128)(2,1)S(1)} %collective-permute-done.26.refs_1_), channel_id=1, source_target_pairs={{0,4},{4,8},{8,12},{12,16},{16,20},{20,24},{24,28},{28,0},{1,5},{5... | collective-permute-start | bytes 811016 | tf_op jit(solution)/shard_map/ppermute | solution.py:42
  171.0 8.3 %copy-start.12 = (bf16[264,512]{1,0:T(8,128)(2,1)}, bf16[264,512]{1,0:T(8,128)(2,1)S(1)}, u32[]{:S(2)}) copy-start(bf16[264,512]{1,0:T(8,128)(2,1)S(1)} %collective-permute-done.21.refs_0_) | copy-start | bytes 811012
  171.0 17.1 %collective-permute-start.22 = (bf16[264,512]{1,0:T(8,128)(2,1)S(1)}, bf16[264,512]{1,0:T(8,128)(2,1)S(1)}, u32[]{:S(2)}, u32[]{:S(2)}) collective-permute-start(bf16[264,512]{1,0:T(8,128)(2,1)S(1)} %collective-permute-done.21.refs_0_), channel_id=1, source_target_pairs={{0,28},{4,0},{8,4},{12,8},{16,12},{20,16},{24,20},{28,24},{1,29},{... | collective-permute-start | bytes 811016 | tf_op jit(solution)/shard_map/ppermute | solution.py:39
  183.4 0.7 copy-start.15
  188.2 0.7 copy-start.14
  191.8 8.2 %collective-permute-start.28 = (bf16[256,512]{1,0:T(8,128)(2,1)}, bf16[256,512]{1,0:T(8,128)(2,1)S(1)}, u32[]{:S(2)}, u32[]{:S(2)}) collective-permute-start(bf16[256,512]{1,0:T(8,128)(2,1)} %hidden.1.mine_ref), channel_id=1, source_target_pairs={{0,2},{2,0},{1,3},{3,1},{4,6},{6,4},{5,7},{7,5},{8,10},{10,8},{9,1... | collective-permute-start | bytes 786440 | tf_op jit(solution)/shard_map/ppermute | solution.py:495
  200.0 0.7 copy-start.6
  203.4 8.5 %collective-permute-start.29 = (bf16[256,256]{1,0:T(8,128)(2,1)}, bf16[256,256]{1,0:T(8,128)(2,1)S(1)}, u32[]{:S(2)}, u32[]{:S(2)}) collective-permute-start(bf16[256,256]{1,0:T(8,128)(2,1)} %get-tuple-element.33), channel_id=1, source_target_pairs={{0,4},{4,8},{8,12},{12,16},{16,20},{20,24},{24,28},{28,0},{1,5},{5... | collective-permute-start | bytes 393224 | tf_op jit(solution)/shard_map/ppermute | solution.py:59
  203.5 9.4 %collective-permute-start.33 = (bf16[256,256]{1,0:T(8,128)(2,1)}, bf16[256,256]{1,0:T(8,128)(2,1)S(1)}, u32[]{:S(2)}, u32[]{:S(2)}) collective-permute-start(bf16[256,256]{1,0:T(8,128)(2,1)} %get-tuple-element.34), channel_id=1, source_target_pairs={{0,28},{4,0},{8,4},{12,8},{16,12},{20,16},{24,20},{28,24},{1,29},{... | collective-permute-start | bytes 393224 | tf_op jit(solution)/shard_map/ppermute | solution.py:61
  212.8 6.3 %collective-permute-start.30 = (bf16[256,256]{1,0:T(8,128)(2,1)S(1)}, bf16[256,256]{1,0:T(8,128)(2,1)S(1)}, u32[]{:S(2)}, u32[]{:S(2)}) collective-permute-start(bf16[256,256]{1,0:T(8,128)(2,1)S(1)} %fusion.17), channel_id=1, source_target_pairs={{0,4},{4,8},{8,12},{12,16},{16,20},{20,24},{24,28},{28,0},{1,5},{5... | collective-permute-start | bytes 393224 | tf_op jit(solution)/shard_map/ppermute | solution.py:59
  220.1 6.3 %collective-permute-start.31 = (bf16[256,256]{1,0:T(8,128)(2,1)S(1)}, bf16[256,256]{1,0:T(8,128)(2,1)S(1)}, u32[]{:S(2)}, u32[]{:S(2)}) collective-permute-start(bf16[256,256]{1,0:T(8,128)(2,1)S(1)} %get-tuple-element.45), channel_id=1, source_target_pairs={{0,4},{4,8},{8,12},{12,16},{16,20},{20,24},{24,28},{28,0},{1,5},{5... | collective-permute-start | bytes 393224 | tf_op jit(solution)/shard_map/ppermute | solution.py:59
  220.2 6.2 %collective-permute-start.34 = (bf16[256,256]{1,0:T(8,128)(2,1)S(1)}, bf16[256,256]{1,0:T(8,128)(2,1)S(1)}, u32[]{:S(2)}, u32[]{:S(2)}) collective-permute-start(bf16[256,256]{1,0:T(8,128)(2,1)S(1)} %get-tuple-element.46), channel_id=1, source_target_pairs={{0,28},{4,0},{8,4},{12,8},{16,12},{20,16},{24,20},{28,24},{1,29},{... | collective-permute-start | bytes 393224 | tf_op jit(solution)/shard_map/ppermute | solution.py:61
  227.4 6.3 %collective-permute-start.32 = (bf16[256,256]{1,0:T(8,128)(2,1)S(1)}, bf16[256,256]{1,0:T(8,128)(2,1)S(1)}, u32[]{:S(2)}, u32[]{:S(2)}) collective-permute-start(bf16[256,256]{1,0:T(8,128)(2,1)S(1)} %get-tuple-element.43), channel_id=1, source_target_pairs={{0,4},{4,8},{8,12},{12,16},{16,20},{20,24},{24,28},{28,0},{1,5},{5... | collective-permute-start | bytes 393224 | tf_op jit(solution)/shard_map/ppermute | solution.py:59
  227.5 6.2 %collective-permute-start.35 = (bf16[256,256]{1,0:T(8,128)(2,1)S(1)}, bf16[256,256]{1,0:T(8,128)(2,1)S(1)}, u32[]{:S(2)}, u32[]{:S(2)}) collective-permute-start(bf16[256,256]{1,0:T(8,128)(2,1)S(1)} %get-tuple-element.44), channel_id=1, source_target_pairs={{0,28},{4,0},{8,4},{12,8},{16,12},{20,16},{24,20},{28,24},{1,29},{... | collective-permute-start | bytes 393224 | tf_op jit(solution)/shard_map/ppermute | solution.py:61
Sparse Core Ops, SparseCore 0:
  20.4 33.0 all-gather.3
  98.3 45.6 all-gather.5

commit v4 on v3

--- a/solution.py
+++ b/solution.py
@@ -289,6 +289,7 @@
         cost_estimate=pl.CostEstimate(
             flops=2 * length * wide * RING * 4 * inner, bytes_accessed=10**7, transcendentals=0
         ),
+        compiler_params=pltpu.CompilerParams(vmem_limit_bytes=50 * 2**20),
         name="attention",
     )(
         *[held[k] for k in range(RING)],
@@ -309,6 +310,7 @@
             bytes_accessed=4 * 10**6,
             transcendentals=0,
         ),
+        compiler_params=pltpu.CompilerParams(vmem_limit_bytes=52 * 2**20),
         name="out_rest",
     )(attended, *out_weights)
     return first, second, rest
@@ -477,6 +479,7 @@
             out_specs=[IN_VMEM] * 2,
             scratch_shapes=scratch(len(owners)),
             out_shape=sums,
+            compiler_params=pltpu.CompilerParams(vmem_limit_bytes=50 * 2**20),
             cost_estimate=cost(len(owners)),
         )(*[held[k] for k in owners], gate, up, other, *before)
 
@@ -489,6 +492,7 @@
         out_specs=IN_VMEM,
         scratch_shapes=scratch(len(LAST)) + [pltpu.VMEM(s.shape, s.dtype) for s in sums],
         out_shape=jax.ShapeDtypeStruct((length, 2 * hidden), jnp.bfloat16),
+        compiler_params=pltpu.CompilerParams(vmem_limit_bytes=52 * 2**20),
         cost_estimate=cost(1),
         name="hidden",
     )(*[held[k] for k in LAST], gate, up, other, *before)
@@ -506,6 +510,7 @@
                 pltpu.SemaphoreType.DMA((len(owners), 4)),
             ],
             out_shape=shapes,
+            compiler_params=pltpu.CompilerParams(vmem_limit_bytes=52 * 2**20),
             cost_estimate=cost(1),
         )(mine, theirs, down, other)
 

time: 243 us -> 233 us (0.959)
  Pallas kernels: 39.6 us -> 30.1 us
    pallas_call x3, Pallas kernels: 12.6 us -> 8.41 us  [gate_sums(): pl.pallas_call(functools.partial(gate_kernel, owners, bool(before)), in_s...]
    convert_element_type x6, other arithmetic: 5.38 us -> 2.51 us  [ring_sum(): up = (got_up.astype(jnp.float32) + block(4 - step)).astype(jnp.bfloat16)]
    unnamed x48 -> x42, local copies, waits for them, and re-layouts: 4.42 us -> 5.79 us
  transfers between devices with their start and end apart: 38 -> 38, of which waited for: 20 -> 19; matrix products, arithmetic and copies ran while one was open for 3% -> 4% of each run, Pallas kernels for 14% -> 11%
where the time goes in v4:
time: 233 us
  waiting for transfers between devices  107 us (46%)
  starting transfers between devices  61.6 us (26%)
  Pallas kernels  30.1 us (13%)
  between operations  13.9 us (6%)
  local copies, waits for them, and re-layouts  12.3 us (5%)
  other arithmetic  7.83 us (3%)
    ppermute x8, waiting for transfers between devices, ring_sum(): got_up = lax.ppermute(up, 'ma_0', UP)  32.3 us
    ppermute x8, starting transfers between devices, ring_gather(): above = lax.ppermute(above, 'ma_0', DOWN)  31 us
    ppermute x8, waiting for transfers between devices, ring_gather(): above = lax.ppermute(above, 'ma_0', DOWN)  24.8 us
    ppermute x6, starting transfers between devices, ring_sum(): got_down = lax.ppermute(down, 'ma_0', DOWN)  19.6 us
    ppermute x6, waiting for transfers between devices, ring_gather(): below = lax.ppermute(below, 'ma_0', UP)  11.2 us
    ppermute x1, waiting for transfers between devices, layer(): pair_share = lax.ppermute(pair_share, 'ma_1', SWAP)  10.2 us
    ppermute x1, waiting for transfers between devices, layer(): first_share = lax.ppermute(jnp.concatenate(share, axis=1), 'row', SWAP)  8.7 us
    pallas_call x3, Pallas kernels, gate_sums(): pl.pallas_call(functools.partial(gate_kernel, owners, bool(before)), in_s...  8.41 us
  transfers between devices with their start and end apart: 38, of which 19 were waited for; matrix products, arithmetic and copies ran while one was open for 4% of the time, Pallas kernels for 11%

profile of v4, /device:TPU:8, one launch (start us, length us, event | category | flops | bytes accessed | tf_op | source)
XLA Modules:
  0.0 232.9 jit_solution(15968558787995707996)
XLA Ops:
  6.5 0.9 constant_dynamic-slice_fusion.7
  7.5 1.0 constant_dynamic-slice_fusion.5
  8.5 2.2 collective-permute-start.8
  10.8 8.7 %collective-permute-done.8 = bf16[256,768]{1,0:T(8,128)(2,1)S(1)} collective-permute-done((bf16[256,768]{1,0:T(8,128)(2,1)S(1)}, bf16[256,768]{1,0:T(8,128)(2,1)S(1)}, u32[]{:S(2)}, u32[]{:S(2)}) %collective-permute-start.8) | collective-permute-done | bytes 393248 | tf_op jit(solution)/shard_map/ppermute | solution.py:563
  19.5 0.8 copy-done.17
  20.4 2.4 %collective-permute-start = (bf16[264,256]{1,0:T(8,128)(2,1)S(1)}, bf16[264,256]{1,0:T(8,128)(2,1)S(1)}, u32[]{:S(2)}, u32[]{:S(2)}) collective-permute-start(bf16[264,256]{1,0:T(8,128)(2,1)S(1)} %pad_maximum_fusion.5), channel_id=1, source_target_pairs={{0,2},{2,0},{1,3},{3,1},{4,6},{6,4},{5,7},{7,5},{8,10},{10,8},{9,1... | collective-permute-start | bytes 405512 | tf_op jit(solution)/shard_map/ppermute | solution.py:555
  22.8 4.2 %collective-permute-done = bf16[264,256]{1,0:T(8,128)(2,1)S(1)} collective-permute-done((bf16[264,256]{1,0:T(8,128)(2,1)S(1)}, bf16[264,256]{1,0:T(8,128)(2,1)S(1)}, u32[]{:S(2)}, u32[]{:S(2)}) %collective-permute-start) | collective-permute-done | bytes 135200 | tf_op jit(solution)/shard_map/ppermute | solution.py:555
  27.1 0.6 slice_convert_fusion.1
  28.0 5.9 %collective-permute-start.1 = (bf16[264,512]{1,0:T(8,128)(2,1)S(1)}, bf16[264,512]{1,0:T(8,128)(2,1)S(1)}, u32[]{:S(2)}, u32[]{:S(2)}) collective-permute-start(bf16[264,512]{1,0:T(8,128)(2,1)S(1)} %pad_maximum_fusion.3.refs_0_), channel_id=1, source_target_pairs={{0,28},{4,0},{8,4},{12,8},{16,12},{20,16},{24,20},{28,24},{1,29},{... | collective-permute-start | bytes 811016 | tf_op jit(solution)/shard_map/ppermute | solution.py:39
  33.9 4.0 %collective-permute-done.1.refs_1_ = bf16[264,512]{1,0:T(8,128)(2,1)S(1)} collective-permute-done((bf16[264,512]{1,0:T(8,128)(2,1)S(1)}, bf16[264,512]{1,0:T(8,128)(2,1)S(1)}, u32[]{:S(2)}, u32[]{:S(2)}) %collective-permute-start.1) | collective-permute-done | bytes 270368 | tf_op jit(solution)/shard_map/ppermute | solution.py:39
  37.9 3.7 %collective-permute-start.2 = (bf16[264,512]{1,0:T(8,128)(2,1)S(1)}, bf16[264,512]{1,0:T(8,128)(2,1)S(1)}, u32[]{:S(2)}, u32[]{:S(2)}) collective-permute-start(bf16[264,512]{1,0:T(8,128)(2,1)S(1)} %collective-permute-done.1.refs_1_), channel_id=1, source_target_pairs={{0,28},{4,0},{8,4},{12,8},{16,12},{20,16},{24,20},{28,24},{1,29},{... | collective-permute-start | bytes 811016 | tf_op jit(solution)/shard_map/ppermute | solution.py:39
  41.6 4.2 %collective-permute-done.2.refs_2_ = bf16[264,512]{1,0:T(8,128)(2,1)S(1)} collective-permute-done((bf16[264,512]{1,0:T(8,128)(2,1)S(1)}, bf16[264,512]{1,0:T(8,128)(2,1)S(1)}, u32[]{:S(2)}, u32[]{:S(2)}) %collective-permute-start.2) | collective-permute-done | bytes 270368 | tf_op jit(solution)/shard_map/ppermute | solution.py:39
  45.8 3.7 %collective-permute-start.3 = (bf16[264,512]{1,0:T(8,128)(2,1)S(1)}, bf16[264,512]{1,0:T(8,128)(2,1)}, u32[]{:S(2)}, u32[]{:S(2)}) collective-permute-start(bf16[264,512]{1,0:T(8,128)(2,1)S(1)} %collective-permute-done.2.refs_2_), channel_id=1, source_target_pairs={{0,28},{4,0},{8,4},{12,8},{16,12},{20,16},{24,20},{28,24},{1,29},{... | collective-permute-start | bytes 811016 | tf_op jit(solution)/shard_map/ppermute | solution.py:39
  49.5 1.9 constant_dynamic-slice_fusion.4
  51.9 1.0 constant_dynamic-slice_fusion.1
  52.9 2.7 %collective-permute-start.23 = (bf16[256,256]{1,0:T(8,128)(2,1)S(1)}, bf16[256,256]{1,0:T(8,128)(2,1)S(1)}, u32[]{:S(2)}, u32[]{:S(2)}) collective-permute-start(bf16[256,256]{1,0:T(8,128)(2,1)S(1)} %get-tuple-element.24), channel_id=1, source_target_pairs={{0,2},{2,0},{1,3},{3,1},{4,6},{6,4},{5,7},{7,5},{8,10},{10,8},{9,1... | collective-permute-start | bytes 393224 | tf_op jit(solution)/shard_map/ppermute | solution.py:591
  55.5 1.0 constant_dynamic-slice_fusion.2
  56.6 10.2 %collective-permute-done.23 = bf16[256,256]{1,0:T(8,128)(2,1)S(1)} collective-permute-done((bf16[256,256]{1,0:T(8,128)(2,1)S(1)}, bf16[256,256]{1,0:T(8,128)(2,1)S(1)}, u32[]{:S(2)}, u32[]{:S(2)}) %collective-permute-start.23) | collective-permute-done | bytes 131104 | tf_op jit(solution)/shard_map/ppermute | solution.py:591
  66.8 0.9 pad_maximum_fusion.1
  67.7 2.1 collective-permute-start.24
  69.9 0.7 copy-done.5
  70.6 9.1 %collective-permute-done.6.refs_6_ = bf16[264,512]{1,0:T(8,128)(2,1)} collective-permute-done((bf16[264,512]{1,0:T(8,128)(2,1)S(1)}, bf16[264,512]{1,0:T(8,128)(2,1)}, u32[]{:S(2)}, u32[]{:S(2)}) %collective-permute-start.6) | collective-permute-done | bytes 270368 | tf_op jit(solution)/shard_map/ppermute | solution.py:42
  79.7 3.2 %collective-permute-start.4 = (bf16[264,512]{1,0:T(8,128)(2,1)}, bf16[264,512]{1,0:T(8,128)(2,1)}, u32[]{:S(2)}, u32[]{:S(2)}) collective-permute-start(bf16[264,512]{1,0:T(8,128)(2,1)} %collective-permute-done.3.refs_3_), channel_id=1, source_target_pairs={{0,28},{4,0},{8,4},{12,8},{16,12},{20,16},{24,20},{28,24},{1,29},{... | collective-permute-start | bytes 811016 | tf_op jit(solution)/shard_map/ppermute | solution.py:39
  83.6 2.1 position_bias.1.refs_15_
  85.7 2.0 collective-permute-done.7.refs_5_
  87.8 0.9 copy-done.2
  88.7 1.0 copy-done.4
  89.7 1.0 copy-done.6
  90.6 7.8 %attention.1 = (bf16[256,512]{1,0:T(8,128)(2,1)S(1)}, bf16[256,512]{1,0:T(8,128)(2,1)S(1)}, bf16[256,256]{1,0:T(8,128)(2,1)S(1)}) custom-call(bf16[264,512]{1,0:T(8,128)(2,1)S(1)} %pad_maximum_fusion.3.refs_0_, bf16[264,512]{1,0:T(8,128)(2,1)S(1)} %copy-done.2, bf16[264,512]{1,0:T(8,128)(2,1)S(1)} %copy-done.4, ...), custom_call_target="tpu_custom_call" | custom-call | flops 2147483648 | bytes 10000000 | tf_op jit(solution)/shard_map/attention/pallas_call | solution.py:271
  98.5 0.7 copy-done.7
  99.2 0.7 copy-done.9
  99.9 2.3 pad_maximum_fusion
  102.4 3.3 %collective-permute-start.15 = (bf16[256,512]{1,0:T(8,128)(2,1)S(1)}, bf16[256,512]{1,0:T(8,128)(2,1)S(1)}, u32[]{:S(2)}, u32[]{:S(2)}) collective-permute-start(bf16[256,512]{1,0:T(8,128)(2,1)S(1)} %copy-done.8), channel_id=1, source_target_pairs={{0,28},{4,0},{8,4},{12,8},{16,12},{20,16},{24,20},{28,24},{1,29},{... | collective-permute-start | bytes 786440 | tf_op jit(solution)/shard_map/ppermute | solution.py:61
  105.7 4.1 %out_rest.1 = bf16[6,256,512]{2,1,0:T(8,128)(2,1)} custom-call(bf16[256,256]{1,0:T(8,128)(2,1)S(1)} %get-tuple-element.22.refs_0_, bf16[256,2048]{1,0:T(8,128)(2,1)} %refs_1_.2, bf16[256,1024]{1,0:T(8,128)(2,1)S(1)} %collective-permute-done.9.refs_13_.refs_2_, bf16[256,1024]{1,0:T(8,128)(2,1)S(1)} %collective-permute-done.10.refs_14_.refs_3_), custom_call_target="tpu_custom_call" | custom-call | flops 402653184 | bytes 4000000 | tf_op jit(solution)/shard_map/out_rest/pallas_call | solution.py:301
  109.8 2.6 %collective-permute-done.11 = bf16[256,512]{1,0:T(8,128)(2,1)S(1)} collective-permute-done((bf16[256,512]{1,0:T(8,128)(2,1)}, bf16[256,512]{1,0:T(8,128)(2,1)S(1)}, u32[]{:S(2)}, u32[]{:S(2)}) %collective-permute-start.11) | collective-permute-done | bytes 262176 | tf_op jit(solution)/shard_map/ppermute | solution.py:59
  112.4 1.0 fusion.10
  113.6 9.1 %collective-permute-done.12 = bf16[256,512]{1,0:T(8,128)(2,1)S(1)} collective-permute-done((bf16[256,512]{1,0:T(8,128)(2,1)S(1)}, bf16[256,512]{1,0:T(8,128)(2,1)S(1)}, u32[]{:S(2)}, u32[]{:S(2)}) %collective-permute-start.12) | collective-permute-done | bytes 262176 | tf_op jit(solution)/shard_map/ppermute | solution.py:59
  122.7 1.2 fusion.9
  124.0 3.2 %collective-permute-start.16 = (bf16[256,512]{1,0:T(8,128)(2,1)S(1)}, bf16[256,512]{1,0:T(8,128)(2,1)S(1)}, u32[]{:S(2)}, u32[]{:S(2)}) collective-permute-start(bf16[256,512]{1,0:T(8,128)(2,1)S(1)} %get-tuple-element.42), channel_id=1, source_target_pairs={{0,28},{4,0},{8,4},{12,8},{16,12},{20,16},{24,20},{28,24},{1,29},{... | collective-permute-start | bytes 786440 | tf_op jit(solution)/shard_map/ppermute | solution.py:61
  127.2 4.3 %collective-permute-done.13 = bf16[256,512]{1,0:T(8,128)(2,1)S(1)} collective-permute-done((bf16[256,512]{1,0:T(8,128)(2,1)S(1)}, bf16[256,512]{1,0:T(8,128)(2,1)S(1)}, u32[]{:S(2)}, u32[]{:S(2)}) %collective-permute-start.13) | collective-permute-done | bytes 262176 | tf_op jit(solution)/shard_map/ppermute | solution.py:59
  131.8 3.3 %collective-permute-start.17 = (bf16[256,512]{1,0:T(8,128)(2,1)S(1)}, bf16[256,512]{1,0:T(8,128)(2,1)S(1)}, u32[]{:S(2)}, u32[]{:S(2)}) collective-permute-start(bf16[256,512]{1,0:T(8,128)(2,1)S(1)} %get-tuple-element.40), channel_id=1, source_target_pairs={{0,28},{4,0},{8,4},{12,8},{16,12},{20,16},{24,20},{28,24},{1,29},{... | collective-permute-start | bytes 786440 | tf_op jit(solution)/shard_map/ppermute | solution.py:61
  135.1 4.3 %collective-permute-done.14 = bf16[256,512]{1,0:T(8,128)(2,1)S(1)} collective-permute-done((bf16[256,512]{1,0:T(8,128)(2,1)S(1)}, bf16[256,512]{1,0:T(8,128)(2,1)S(1)}, u32[]{:S(2)}, u32[]{:S(2)}) %collective-permute-start.14) | collective-permute-done | bytes 262176 | tf_op jit(solution)/shard_map/ppermute | solution.py:59
  139.6 7.9 %collective-permute-done.18 = bf16[256,512]{1,0:T(8,128)(2,1)S(1)} collective-permute-done((bf16[256,512]{1,0:T(8,128)(2,1)S(1)}, bf16[256,512]{1,0:T(8,128)(2,1)S(1)}, u32[]{:S(2)}, u32[]{:S(2)}) %collective-permute-start.18) | collective-permute-done | bytes 262176 | tf_op jit(solution)/shard_map/ppermute | solution.py:607
  147.8 3.4 %collective-permute-start.19 = (bf16[264,512]{1,0:T(8,128)(2,1)S(1)}, bf16[264,512]{1,0:T(8,128)(2,1)S(1)}, u32[]{:S(2)}, u32[]{:S(2)}) collective-permute-start(bf16[264,512]{1,0:T(8,128)(2,1)S(1)} %pad_maximum_fusion.4.refs_0_), channel_id=1, source_target_pairs={{0,28},{4,0},{8,4},{12,8},{16,12},{20,16},{24,20},{28,24},{1,29},{... | collective-permute-start | bytes 811016 | tf_op jit(solution)/shard_map/ppermute | solution.py:39
  151.2 6.1 %collective-permute-done.19.refs_1_ = bf16[264,512]{1,0:T(8,128)(2,1)S(1)} collective-permute-done((bf16[264,512]{1,0:T(8,128)(2,1)S(1)}, bf16[264,512]{1,0:T(8,128)(2,1)S(1)}, u32[]{:S(2)}, u32[]{:S(2)}) %collective-permute-start.19) | collective-permute-done | bytes 270368 | tf_op jit(solution)/shard_map/ppermute | solution.py:39
  157.3 3.7 %collective-permute-start.20 = (bf16[264,512]{1,0:T(8,128)(2,1)S(1)}, bf16[264,512]{1,0:T(8,128)(2,1)S(1)}, u32[]{:S(2)}, u32[]{:S(2)}) collective-permute-start(bf16[264,512]{1,0:T(8,128)(2,1)S(1)} %collective-permute-done.19.refs_1_), channel_id=1, source_target_pairs={{0,28},{4,0},{8,4},{12,8},{16,12},{20,16},{24,20},{28,24},{1,29},{... | collective-permute-start | bytes 811016 | tf_op jit(solution)/shard_map/ppermute | solution.py:39
  161.0 6.5 %collective-permute-done.20.refs_0_ = bf16[264,512]{1,0:T(8,128)(2,1)S(1)} collective-permute-done((bf16[264,512]{1,0:T(8,128)(2,1)S(1)}, bf16[264,512]{1,0:T(8,128)(2,1)S(1)}, u32[]{:S(2)}, u32[]{:S(2)}) %collective-permute-start.20) | collective-permute-done | bytes 270368 | tf_op jit(solution)/shard_map/ppermute | solution.py:39
  167.5 3.7 %collective-permute-start.21 = (bf16[264,512]{1,0:T(8,128)(2,1)S(1)}, bf16[264,512]{1,0:T(8,128)(2,1)S(1)}, u32[]{:S(2)}, u32[]{:S(2)}) collective-permute-start(bf16[264,512]{1,0:T(8,128)(2,1)S(1)} %collective-permute-done.20.refs_0_), channel_id=1, source_target_pairs={{0,28},{4,0},{8,4},{12,8},{16,12},{20,16},{24,20},{28,24},{1,29},{... | collective-permute-start | bytes 811016 | tf_op jit(solution)/shard_map/ppermute | solution.py:39
  171.2 4.0 %collective-permute-done.21.refs_0_ = bf16[264,512]{1,0:T(8,128)(2,1)S(1)} collective-permute-done((bf16[264,512]{1,0:T(8,128)(2,1)S(1)}, bf16[264,512]{1,0:T(8,128)(2,1)S(1)}, u32[]{:S(2)}, u32[]{:S(2)}) %collective-permute-start.21) | collective-permute-done | bytes 270368 | tf_op jit(solution)/shard_map/ppermute | solution.py:39
  175.1 3.7 %collective-permute-start.22 = (bf16[264,512]{1,0:T(8,128)(2,1)S(1)}, bf16[264,512]{1,0:T(8,128)(2,1)}, u32[]{:S(2)}, u32[]{:S(2)}) collective-permute-start(bf16[264,512]{1,0:T(8,128)(2,1)S(1)} %collective-permute-done.21.refs_0_), channel_id=1, source_target_pairs={{0,28},{4,0},{8,4},{12,8},{16,12},{20,16},{24,20},{28,24},{1,29},{... | collective-permute-start | bytes 811016 | tf_op jit(solution)/shard_map/ppermute | solution.py:39
  178.8 3.2 %shard_map.109 = (f32[256,1024]{1,0:T(8,128)S(1)}, f32[8,256]{1,0:T(8,128)S(1)}) custom-call(bf16[264,512]{1,0:T(8,128)(2,1)S(1)} %pad_maximum_fusion.4.refs_0_, bf16[264,512]{1,0:T(8,128)(2,1)S(1)} %collective-permute-done.19.refs_1_, bf16[264,512]{1,0:T(8,128)(2,1)S(1)} %collective-permute-done.25.refs_2_, bf16[4096,256]{1,0:T(8,128)(2,1)S(1)} %copy-done, ...), custom_call_target="tpu_custom_call" | custom-call | flops 805306368 | bytes 4000000 | tf_op jit(solution)/shard_map/pallas_call | solution.py:476
  182.0 2.6 %shard_map.110 = (f32[256,1024]{1,0:T(8,128)S(1)}, f32[8,256]{1,0:T(8,128)S(1)}) custom-call(bf16[264,512]{1,0:T(8,128)(2,1)S(1)} %collective-permute-done.20.refs_0_, bf16[264,512]{1,0:T(8,128)(2,1)} %collective-permute-done.26.refs_1_, bf16[4096,256]{1,0:T(8,128)(2,1)} %refs_1_.3, bf16[4096,256]{1,0:T(8,128)(2,1)} %refs_2_.5, ...), custom_call_target="tpu_custom_call" | custom-call | flops 536870912 | bytes 3000000 | tf_op jit(solution)/shard_map/pallas_call | solution.py:476
  184.6 2.6 %shard_map.111 = (f32[256,1024]{1,0:T(8,128)S(1)}, f32[8,256]{1,0:T(8,128)S(1)}) custom-call(bf16[264,512]{1,0:T(8,128)(2,1)S(1)} %collective-permute-done.21.refs_0_, bf16[264,512]{1,0:T(8,128)(2,1)} %collective-permute-done.27.refs_1_, bf16[4096,256]{1,0:T(8,128)(2,1)} %refs_1_.3, bf16[4096,256]{1,0:T(8,128)(2,1)} %refs_2_.5, ...), custom_call_target="tpu_custom_call" | custom-call | flops 536870912 | bytes 3000000 | tf_op jit(solution)/shard_map/pallas_call | solution.py:476
  187.3 1.8 hidden.1.mine_ref
  189.2 7.9 %collective-permute-done.28.theirs_ref = bf16[256,512]{1,0:T(8,128)(2,1)S(1)} collective-permute-done((bf16[256,512]{1,0:T(8,128)(2,1)S(1)}, bf16[256,512]{1,0:T(8,128)(2,1)S(1)}, u32[]{:S(2)}, u32[]{:S(2)}) %collective-permute-start.28) | collective-permute-done | bytes 262176 | tf_op jit(solution)/shard_map/ppermute | solution.py:499
  197.1 1.8 shard_map.112
  199.0 3.2 %collective-permute-start.33 = (bf16[256,256]{1,0:T(8,128)(2,1)S(1)}, bf16[256,256]{1,0:T(8,128)(2,1)S(1)}, u32[]{:S(2)}, u32[]{:S(2)}) collective-permute-start(bf16[256,256]{1,0:T(8,128)(2,1)S(1)} %get-tuple-element.34), channel_id=1, source_target_pairs={{0,28},{4,0},{8,4},{12,8},{16,12},{20,16},{24,20},{28,24},{1,29},{... | collective-permute-start | bytes 393224 | tf_op jit(solution)/shard_map/ppermute | solution.py:61
  202.3 4.0 %shard_map.113 = bf16[6,256,256]{2,1,0:T(8,128)(2,1)S(1)} custom-call(bf16[256,512]{1,0:T(8,128)(2,1)S(1)} %hidden.1.mine_ref, bf16[256,512]{1,0:T(8,128)(2,1)S(1)} %collective-permute-done.28.theirs_ref, bf16[256,4096]{1,0:T(8,128)(2,1)} %down_ref.3, bf16[8,1792,256]{2,1,0:T(8,128)(2,1)} %bitcast.72), custom_call_target="tpu_custom_call" | custom-call | flops 268435456 | bytes 2000000 | tf_op jit(solution)/shard_map/pallas_call | solution.py:502
  206.5 6.2 %collective-permute-done.30 = bf16[256,256]{1,0:T(8,128)(2,1)S(1)} collective-permute-done((bf16[256,256]{1,0:T(8,128)(2,1)S(1)}, bf16[256,256]{1,0:T(8,128)(2,1)S(1)}, u32[]{:S(2)}, u32[]{:S(2)}) %collective-permute-start.30) | collective-permute-done | bytes 131104 | tf_op jit(solution)/shard_map/ppermute | solution.py:59
  212.8 3.2 %collective-permute-start.34 = (bf16[256,256]{1,0:T(8,128)(2,1)S(1)}, bf16[256,256]{1,0:T(8,128)(2,1)S(1)}, u32[]{:S(2)}, u32[]{:S(2)}) collective-permute-start(bf16[256,256]{1,0:T(8,128)(2,1)S(1)} %get-tuple-element.46), channel_id=1, source_target_pairs={{0,28},{4,0},{8,4},{12,8},{16,12},{20,16},{24,20},{28,24},{1,29},{... | collective-permute-start | bytes 393224 | tf_op jit(solution)/shard_map/ppermute | solution.py:61
  216.0 2.9 %collective-permute-done.31 = bf16[256,256]{1,0:T(8,128)(2,1)S(1)} collective-permute-done((bf16[256,256]{1,0:T(8,128)(2,1)S(1)}, bf16[256,256]{1,0:T(8,128)(2,1)S(1)}, u32[]{:S(2)}, u32[]{:S(2)}) %collective-permute-start.31) | collective-permute-done | bytes 131104 | tf_op jit(solution)/shard_map/ppermute | solution.py:59
  219.1 3.3 %collective-permute-start.35 = (bf16[256,256]{1,0:T(8,128)(2,1)S(1)}, bf16[256,256]{1,0:T(8,128)(2,1)S(1)}, u32[]{:S(2)}, u32[]{:S(2)}) collective-permute-start(bf16[256,256]{1,0:T(8,128)(2,1)S(1)} %get-tuple-element.44), channel_id=1, source_target_pairs={{0,28},{4,0},{8,4},{12,8},{16,12},{20,16},{24,20},{28,24},{1,29},{... | collective-permute-start | bytes 393224 | tf_op jit(solution)/shard_map/ppermute | solution.py:61
  222.4 2.9 %collective-permute-done.32 = bf16[256,256]{1,0:T(8,128)(2,1)S(1)} collective-permute-done((bf16[256,256]{1,0:T(8,128)(2,1)S(1)}, bf16[256,256]{1,0:T(8,128)(2,1)S(1)}, u32[]{:S(2)}, u32[]{:S(2)}) %collective-permute-start.32) | collective-permute-done | bytes 131104 | tf_op jit(solution)/shard_map/ppermute | solution.py:59
  225.3 0.7 fusion.18
  (98 shorter events, 3.5 us)
Async XLA Ops:
  6.5 13.8 %copy-start.19 = (bf16[256]{0:T(256)(128)(2,1)S(1)}, bf16[256]{0:T(256)(128)(2,1)}, u32[]{:S(2)}) copy-start(bf16[256]{0:T(256)(128)(2,1)} %param.12) | copy-start | bytes 1540
  6.5 13.8 %copy-start.20 = (bf16[256]{0:T(256)(128)(2,1)S(1)}, bf16[256]{0:T(256)(128)(2,1)}, u32[]{:S(2)}) copy-start(bf16[256]{0:T(256)(128)(2,1)} %param.18) | copy-start | bytes 1540
  6.5 13.8 %copy-start.16 = (bf16[1,256,256]{2,1,0:T(8,128)(2,1)S(1)}, bf16[1,256,256]{2,1,0:T(8,128)(2,1)}, u32[]{:S(2)}) copy-start(bf16[1,256,256]{2,1,0:T(8,128)(2,1)} %param.11) | copy-start | bytes 393220
  6.5 81.2 %all-gather.4.cloned.1.call-start = ((), (), s32[]{:S(2)}) async-start(), calls=%async_computation | async-start | bytes 3538944 | tf_op jit(solution)/shard_map/all_gather | solution.py:564
  8.5 10.9 %collective-permute-start.8 = (bf16[256,768]{1,0:T(8,128)(2,1)S(1)}, bf16[256,768]{1,0:T(8,128)(2,1)S(1)}, u32[]{:S(2)}, u32[]{:S(2)}) collective-permute-start(bf16[256,768]{1,0:T(8,128)(2,1)S(1)} %pad_maximum_fusion.2), channel_id=1, source_target_pairs={{0,1},{1,0},{2,3},{3,2},{4,5},{5,4},{6,7},{7,6},{8,9},{9,8},{10,11... | collective-permute-start | bytes 1179656 | tf_op jit(solution)/shard_map/ppermute | solution.py:563
  19.5 0.8 copy-start.17
  20.3 158.6 %all-gather.6.cloned.1.call-start = ((), (), s32[]{:S(2)}) async-start(), calls=%async_computation.1 | async-start | bytes 8257536 | tf_op jit(solution)/shard_map/all_gather | solution.py:605
  20.4 6.6 %collective-permute-start = (bf16[264,256]{1,0:T(8,128)(2,1)S(1)}, bf16[264,256]{1,0:T(8,128)(2,1)S(1)}, u32[]{:S(2)}, u32[]{:S(2)}) collective-permute-start(bf16[264,256]{1,0:T(8,128)(2,1)S(1)} %pad_maximum_fusion.5), channel_id=1, source_target_pairs={{0,2},{2,0},{1,3},{3,1},{4,6},{6,4},{5,7},{7,5},{8,10},{10,8},{9,1... | collective-permute-start | bytes 405512 | tf_op jit(solution)/shard_map/ppermute | solution.py:555
  22.8 32.8 %copy-start = (bf16[4096,256]{1,0:T(8,128)(2,1)S(1)}, bf16[4096,256]{1,0:T(8,128)(2,1)}, u32[]{:S(2)}) copy-start(bf16[4096,256]{1,0:T(8,128)(2,1)} %refs_1_.3) | copy-start | bytes 6291460
  27.1 10.8 %copy-start.11 = (bf16[264,512]{1,0:T(8,128)(2,1)}, bf16[264,512]{1,0:T(8,128)(2,1)S(1)}, u32[]{:S(2)}) copy-start(bf16[264,512]{1,0:T(8,128)(2,1)S(1)} %maximum_select_fusion) | copy-start | bytes 811012
  28.0 9.9 %collective-permute-start.1 = (bf16[264,512]{1,0:T(8,128)(2,1)S(1)}, bf16[264,512]{1,0:T(8,128)(2,1)S(1)}, u32[]{:S(2)}, u32[]{:S(2)}) collective-permute-start(bf16[264,512]{1,0:T(8,128)(2,1)S(1)} %pad_maximum_fusion.3.refs_0_), channel_id=1, source_target_pairs={{0,28},{4,0},{8,4},{12,8},{16,12},{20,16},{24,20},{28,24},{1,29},{... | collective-permute-start | bytes 811016 | tf_op jit(solution)/shard_map/ppermute | solution.py:39
  37.9 13.5 %copy-start.1 = (bf16[264,512]{1,0:T(8,128)(2,1)}, bf16[264,512]{1,0:T(8,128)(2,1)S(1)}, u32[]{:S(2)}) copy-start(bf16[264,512]{1,0:T(8,128)(2,1)S(1)} %collective-permute-done.1.refs_1_) | copy-start | bytes 811012
  37.9 7.9 %collective-permute-start.2 = (bf16[264,512]{1,0:T(8,128)(2,1)S(1)}, bf16[264,512]{1,0:T(8,128)(2,1)S(1)}, u32[]{:S(2)}, u32[]{:S(2)}) collective-permute-start(bf16[264,512]{1,0:T(8,128)(2,1)S(1)} %collective-permute-done.1.refs_1_), channel_id=1, source_target_pairs={{0,28},{4,0},{8,4},{12,8},{16,12},{20,16},{24,20},{28,24},{1,29},{... | collective-permute-start | bytes 811016 | tf_op jit(solution)/shard_map/ppermute | solution.py:39
  45.8 21.9 %copy-start.3 = (bf16[264,512]{1,0:T(8,128)(2,1)}, bf16[264,512]{1,0:T(8,128)(2,1)S(1)}, u32[]{:S(2)}) copy-start(bf16[264,512]{1,0:T(8,128)(2,1)S(1)} %collective-permute-done.2.refs_2_) | copy-start | bytes 811012
  45.8 21.0 %collective-permute-start.3 = (bf16[264,512]{1,0:T(8,128)(2,1)S(1)}, bf16[264,512]{1,0:T(8,128)(2,1)}, u32[]{:S(2)}, u32[]{:S(2)}) collective-permute-start(bf16[264,512]{1,0:T(8,128)(2,1)S(1)} %collective-permute-done.2.refs_2_), channel_id=1, source_target_pairs={{0,28},{4,0},{8,4},{12,8},{16,12},{20,16},{24,20},{28,24},{1,29},{... | collective-permute-start | bytes 811016 | tf_op jit(solution)/shard_map/ppermute | solution.py:39
  51.4 19.2 %collective-permute-start.9 = (bf16[256,1024]{1,0:T(8,128)(2,1)}, bf16[256,1024]{1,0:T(8,128)(2,1)S(1)}, u32[]{:S(2)}, u32[]{:S(2)}) collective-permute-start(bf16[256,1024]{1,0:T(8,128)(2,1)} %constant_dynamic-slice_fusion.4), channel_id=1, source_target_pairs={{0,1},{1,0},{2,3},{3,2},{4,5},{5,4},{6,7},{7,6},{8,9},{9,8},{10,11... | collective-permute-start | bytes 1572872 | tf_op jit(solution)/shard_map/ppermute | solution.py:587
  52.9 13.9 %collective-permute-start.23 = (bf16[256,256]{1,0:T(8,128)(2,1)S(1)}, bf16[256,256]{1,0:T(8,128)(2,1)S(1)}, u32[]{:S(2)}, u32[]{:S(2)}) collective-permute-start(bf16[256,256]{1,0:T(8,128)(2,1)S(1)} %get-tuple-element.24), channel_id=1, source_target_pairs={{0,2},{2,0},{1,3},{3,1},{4,6},{6,4},{5,7},{7,5},{8,10},{10,8},{9,1... | collective-permute-start | bytes 393224 | tf_op jit(solution)/shard_map/ppermute | solution.py:591
  56.5 13.3 %collective-permute-start.5 = (bf16[264,512]{1,0:T(8,128)(2,1)S(1)}, bf16[264,512]{1,0:T(8,128)(2,1)S(1)}, u32[]{:S(2)}, u32[]{:S(2)}) collective-permute-start(bf16[264,512]{1,0:T(8,128)(2,1)S(1)} %pad_maximum_fusion.3.refs_0_), channel_id=1, source_target_pairs={{0,4},{4,8},{8,12},{12,16},{16,20},{20,24},{24,28},{28,0},{1,5},{5... | collective-permute-start | bytes 811016 | tf_op jit(solution)/shard_map/ppermute | solution.py:42
  66.8 3.1 %copy-start.15 = (bf16[256,256]{1,0:T(8,128)(2,1)}, bf16[256,256]{1,0:T(8,128)(2,1)S(1)}, u32[]{:S(2)}) copy-start(bf16[256,256]{1,0:T(8,128)(2,1)S(1)} %collective-permute-done.23) | copy-start | bytes 393220
  67.7 32.1 %collective-permute-start.24 = (bf16[1536,256]{1,0:T(8,128)(2,1)}, bf16[1536,256]{1,0:T(8,128)(2,1)}, u32[]{:S(2)}, u32[]{:S(2)}) collective-permute-start(bf16[1536,256]{1,0:T(8,128)(2,1)} %pad_maximum_fusion.1), channel_id=1, source_target_pairs={{0,1},{1,0},{2,3},{3,2},{4,5},{5,4},{6,7},{7,6},{8,9},{9,8},{10,11... | collective-permute-start | bytes 2359304 | tf_op jit(solution)/shard_map/ppermute | solution.py:595
  69.9 9.9 %collective-permute-start.6 = (bf16[264,512]{1,0:T(8,128)(2,1)S(1)}, bf16[264,512]{1,0:T(8,128)(2,1)}, u32[]{:S(2)}, u32[]{:S(2)}) collective-permute-start(bf16[264,512]{1,0:T(8,128)(2,1)S(1)} %collective-permute-done.5.refs_7_), channel_id=1, source_target_pairs={{0,4},{4,8},{8,12},{12,16},{16,20},{20,24},{24,28},{28,0},{1,5},{5... | collective-permute-start | bytes 811016 | tf_op jit(solution)/shard_map/ppermute | solution.py:42
  69.9 0.7 copy-start.5
  70.6 17.1 %collective-permute-start.10 = (bf16[256,1024]{1,0:T(8,128)(2,1)S(1)}, bf16[256,1024]{1,0:T(8,128)(2,1)S(1)}, u32[]{:S(2)}, u32[]{:S(2)}) collective-permute-start(bf16[256,1024]{1,0:T(8,128)(2,1)S(1)} %collective-permute-done.9.refs_13_.refs_2_), channel_id=1, source_target_pairs={{0,32},{32,0},{64,96},{96,64},{128,160},{160,128},{192,224},{224,1... | collective-permute-start | bytes 1572872 | tf_op jit(solution)/shard_map/ppermute | solution.py:589
  79.7 8.0 %collective-permute-start.7 = (bf16[264,512]{1,0:T(8,128)(2,1)}, bf16[264,512]{1,0:T(8,128)(2,1)}, u32[]{:S(2)}, u32[]{:S(2)}) collective-permute-start(bf16[264,512]{1,0:T(8,128)(2,1)} %collective-permute-done.6.refs_6_), channel_id=1, source_target_pairs={{0,4},{4,8},{8,12},{12,16},{16,20},{20,24},{24,28},{28,0},{1,5},{5... | collective-permute-start | bytes 811016 | tf_op jit(solution)/shard_map/ppermute | solution.py:42
  79.7 8.0 %collective-permute-start.4 = (bf16[264,512]{1,0:T(8,128)(2,1)}, bf16[264,512]{1,0:T(8,128)(2,1)}, u32[]{:S(2)}, u32[]{:S(2)}) collective-permute-start(bf16[264,512]{1,0:T(8,128)(2,1)} %collective-permute-done.3.refs_3_), channel_id=1, source_target_pairs={{0,28},{4,0},{8,4},{12,8},{16,12},{20,16},{24,20},{28,24},{1,29},{... | collective-permute-start | bytes 811016 | tf_op jit(solution)/shard_map/ppermute | solution.py:39
  87.8 1.0 copy-start.2
  88.7 1.0 copy-start.4
  89.7 1.0 copy-start.6
  98.4 0.7 copy-start.7
  99.2 0.7 copy-start.9
  99.9 2.6 %copy-start.8 = (bf16[256,512]{1,0:T(8,128)(2,1)S(1)}, bf16[256,512]{1,0:T(8,128)(2,1)}, u32[]{:S(2)}) copy-start(bf16[256,512]{1,0:T(8,128)(2,1)} %copy-done.7) | copy-start | bytes 786436
  102.1 10.3 %collective-permute-start.11 = (bf16[256,512]{1,0:T(8,128)(2,1)}, bf16[256,512]{1,0:T(8,128)(2,1)S(1)}, u32[]{:S(2)}, u32[]{:S(2)}) collective-permute-start(bf16[256,512]{1,0:T(8,128)(2,1)} %copy-done.9), channel_id=1, source_target_pairs={{0,4},{4,8},{8,12},{12,16},{16,20},{20,24},{24,28},{28,0},{1,5},{5... | collective-permute-start | bytes 786440 | tf_op jit(solution)/shard_map/ppermute | solution.py:59
  102.4 11.1 %collective-permute-start.15 = (bf16[256,512]{1,0:T(8,128)(2,1)S(1)}, bf16[256,512]{1,0:T(8,128)(2,1)S(1)}, u32[]{:S(2)}, u32[]{:S(2)}) collective-permute-start(bf16[256,512]{1,0:T(8,128)(2,1)S(1)} %copy-done.8), channel_id=1, source_target_pairs={{0,28},{4,0},{8,4},{12,8},{16,12},{20,16},{24,20},{28,24},{1,29},{... | collective-permute-start | bytes 786440 | tf_op jit(solution)/shard_map/ppermute | solution.py:61
  109.8 21.8 %copy-start.10 = (bf16[6,256,512]{2,1,0:T(8,128)(2,1)S(1)}, bf16[6,256,512]{2,1,0:T(8,128)(2,1)}, u32[]{:S(2)}) copy-start(bf16[6,256,512]{2,1,0:T(8,128)(2,1)} %out_rest.1) | copy-start | bytes 4718596
  113.5 9.2 %collective-permute-start.12 = (bf16[256,512]{1,0:T(8,128)(2,1)S(1)}, bf16[256,512]{1,0:T(8,128)(2,1)S(1)}, u32[]{:S(2)}, u32[]{:S(2)}) collective-permute-start(bf16[256,512]{1,0:T(8,128)(2,1)S(1)} %fusion.10), channel_id=1, source_target_pairs={{0,4},{4,8},{8,12},{12,16},{16,20},{20,24},{24,28},{28,0},{1,5},{5... | collective-permute-start | bytes 786440 | tf_op jit(solution)/shard_map/ppermute | solution.py:59
  123.9 23.6 %copy-start.12 = (bf16[264,512]{1,0:T(8,128)(2,1)S(1)}, bf16[264,512]{1,0:T(8,128)(2,1)}, u32[]{:S(2)}) copy-start(bf16[264,512]{1,0:T(8,128)(2,1)} %copy-done.11) | copy-start | bytes 811012
  123.9 23.6 %copy-start.18 = (f32[1,512]{1,0:T(1,128)S(1)}, f32[1,512]{1,0:T(1,128)}, u32[]{:S(2)}) copy-start(f32[1,512]{1,0:T(1,128)} %get-tuple-element.50) | copy-start | bytes 6148
  123.9 7.7 %collective-permute-start.13 = (bf16[256,512]{1,0:T(8,128)(2,1)S(1)}, bf16[256,512]{1,0:T(8,128)(2,1)S(1)}, u32[]{:S(2)}, u32[]{:S(2)}) collective-permute-start(bf16[256,512]{1,0:T(8,128)(2,1)S(1)} %get-tuple-element.41), channel_id=1, source_target_pairs={{0,4},{4,8},{8,12},{12,16},{16,20},{20,24},{24,28},{28,0},{1,5},{5... | collective-permute-start | bytes 786440 | tf_op jit(solution)/shard_map/ppermute | solution.py:59
  124.0 7.6 %collective-permute-start.16 = (bf16[256,512]{1,0:T(8,128)(2,1)S(1)}, bf16[256,512]{1,0:T(8,128)(2,1)S(1)}, u32[]{:S(2)}, u32[]{:S(2)}) collective-permute-start(bf16[256,512]{1,0:T(8,128)(2,1)S(1)} %get-tuple-element.42), channel_id=1, source_target_pairs={{0,28},{4,0},{8,4},{12,8},{16,12},{20,16},{24,20},{28,24},{1,29},{... | collective-permute-start | bytes 786440 | tf_op jit(solution)/shard_map/ppermute | solution.py:61
  131.7 7.7 %collective-permute-start.14 = (bf16[256,512]{1,0:T(8,128)(2,1)S(1)}, bf16[256,512]{1,0:T(8,128)(2,1)S(1)}, u32[]{:S(2)}, u32[]{:S(2)}) collective-permute-start(bf16[256,512]{1,0:T(8,128)(2,1)S(1)} %get-tuple-element.39), channel_id=1, source_target_pairs={{0,4},{4,8},{8,12},{12,16},{16,20},{20,24},{24,28},{28,0},{1,5},{5... | collective-permute-start | bytes 786440 | tf_op jit(solution)/shard_map/ppermute | solution.py:59
  131.8 7.6 %collective-permute-start.17 = (bf16[256,512]{1,0:T(8,128)(2,1)S(1)}, bf16[256,512]{1,0:T(8,128)(2,1)S(1)}, u32[]{:S(2)}, u32[]{:S(2)}) collective-permute-start(bf16[256,512]{1,0:T(8,128)(2,1)S(1)} %get-tuple-element.40), channel_id=1, source_target_pairs={{0,28},{4,0},{8,4},{12,8},{16,12},{20,16},{24,20},{28,24},{1,29},{... | collective-permute-start | bytes 786440 | tf_op jit(solution)/shard_map/ppermute | solution.py:61
  139.5 8.0 %collective-permute-start.18 = (bf16[256,512]{1,0:T(8,128)(2,1)S(1)}, bf16[256,512]{1,0:T(8,128)(2,1)S(1)}, u32[]{:S(2)}, u32[]{:S(2)}) collective-permute-start(bf16[256,512]{1,0:T(8,128)(2,1)S(1)} %fusion.5), channel_id=1, source_target_pairs={{0,2},{2,0},{1,3},{3,1},{4,6},{6,4},{5,7},{7,5},{8,10},{10,8},{9,1... | collective-permute-start | bytes 786440 | tf_op jit(solution)/shard_map/ppermute | solution.py:607
  147.6 27.6 %copy-start.13 = (bf16[256,512]{1,0:T(8,128)(2,1)}, bf16[256,512]{1,0:T(8,128)(2,1)S(1)}, u32[]{:S(2)}) copy-start(bf16[256,512]{1,0:T(8,128)(2,1)S(1)} %get-tuple-element.36) | copy-start | bytes 786436
  147.8 9.5 %collective-permute-start.19 = (bf16[264,512]{1,0:T(8,128)(2,1)S(1)}, bf16[264,512]{1,0:T(8,128)(2,1)S(1)}, u32[]{:S(2)}, u32[]{:S(2)}) collective-permute-start(bf16[264,512]{1,0:T(8,128)(2,1)S(1)} %pad_maximum_fusion.4.refs_0_), channel_id=1, source_target_pairs={{0,28},{4,0},{8,4},{12,8},{16,12},{20,16},{24,20},{28,24},{1,29},{... | collective-permute-start | bytes 811016 | tf_op jit(solution)/shard_map/ppermute | solution.py:39
  151.2 9.8 %collective-permute-start.25 = (bf16[264,512]{1,0:T(8,128)(2,1)S(1)}, bf16[264,512]{1,0:T(8,128)(2,1)S(1)}, u32[]{:S(2)}, u32[]{:S(2)}) collective-permute-start(bf16[264,512]{1,0:T(8,128)(2,1)S(1)} %pad_maximum_fusion.4.refs_0_), channel_id=1, source_target_pairs={{0,4},{4,8},{8,12},{12,16},{16,20},{20,24},{24,28},{28,0},{1,5},{5... | collective-permute-start | bytes 811016 | tf_op jit(solution)/shard_map/ppermute | solution.py:42
  157.3 10.2 %collective-permute-start.20 = (bf16[264,512]{1,0:T(8,128)(2,1)S(1)}, bf16[264,512]{1,0:T(8,128)(2,1)S(1)}, u32[]{:S(2)}, u32[]{:S(2)}) collective-permute-start(bf16[264,512]{1,0:T(8,128)(2,1)S(1)} %collective-permute-done.19.refs_1_), channel_id=1, source_target_pairs={{0,28},{4,0},{8,4},{12,8},{16,12},{20,16},{24,20},{28,24},{1,29},{... | collective-permute-start | bytes 811016 | tf_op jit(solution)/shard_map/ppermute | solution.py:39
  161.0 10.2 %collective-permute-start.26 = (bf16[264,512]{1,0:T(8,128)(2,1)S(1)}, bf16[264,512]{1,0:T(8,128)(2,1)}, u32[]{:S(2)}, u32[]{:S(2)}) collective-permute-start(bf16[264,512]{1,0:T(8,128)(2,1)S(1)} %collective-permute-done.25.refs_2_), channel_id=1, source_target_pairs={{0,4},{4,8},{8,12},{12,16},{16,20},{20,24},{24,28},{28,0},{1,5},{5... | collective-permute-start | bytes 811016 | tf_op jit(solution)/shard_map/ppermute | solution.py:42
  167.5 7.7 %collective-permute-start.21 = (bf16[264,512]{1,0:T(8,128)(2,1)S(1)}, bf16[264,512]{1,0:T(8,128)(2,1)S(1)}, u32[]{:S(2)}, u32[]{:S(2)}) collective-permute-start(bf16[264,512]{1,0:T(8,128)(2,1)S(1)} %collective-permute-done.20.refs_0_), channel_id=1, source_target_pairs={{0,28},{4,0},{8,4},{12,8},{16,12},{20,16},{24,20},{28,24},{1,29},{... | collective-permute-start | bytes 811016 | tf_op jit(solution)/shard_map/ppermute | solution.py:39
  171.2 13.5 %collective-permute-start.27 = (bf16[264,512]{1,0:T(8,128)(2,1)}, bf16[264,512]{1,0:T(8,128)(2,1)}, u32[]{:S(2)}, u32[]{:S(2)}) collective-permute-start(bf16[264,512]{1,0:T(8,128)(2,1)} %collective-permute-done.26.refs_1_), channel_id=1, source_target_pairs={{0,4},{4,8},{8,12},{12,16},{16,20},{20,24},{24,28},{28,0},{1,5},{5... | collective-permute-start | bytes 811016 | tf_op jit(solution)/shard_map/ppermute | solution.py:42
  175.1 12.1 %collective-permute-start.22 = (bf16[264,512]{1,0:T(8,128)(2,1)S(1)}, bf16[264,512]{1,0:T(8,128)(2,1)}, u32[]{:S(2)}, u32[]{:S(2)}) collective-permute-start(bf16[264,512]{1,0:T(8,128)(2,1)S(1)} %collective-permute-done.21.refs_0_), channel_id=1, source_target_pairs={{0,28},{4,0},{8,4},{12,8},{16,12},{20,16},{24,20},{28,24},{1,29},{... | collective-permute-start | bytes 811016 | tf_op jit(solution)/shard_map/ppermute | solution.py:39
  189.1 8.0 %collective-permute-start.28 = (bf16[256,512]{1,0:T(8,128)(2,1)S(1)}, bf16[256,512]{1,0:T(8,128)(2,1)S(1)}, u32[]{:S(2)}, u32[]{:S(2)}) collective-permute-start(bf16[256,512]{1,0:T(8,128)(2,1)S(1)} %hidden.1.mine_ref), channel_id=1, source_target_pairs={{0,2},{2,0},{1,3},{3,1},{4,6},{6,4},{5,7},{7,5},{8,10},{10,8},{9,1... | collective-permute-start | bytes 786440 | tf_op jit(solution)/shard_map/ppermute | solution.py:499
  199.0 7.4 %collective-permute-start.29 = (bf16[256,256]{1,0:T(8,128)(2,1)S(1)}, bf16[256,256]{1,0:T(8,128)(2,1)S(1)}, u32[]{:S(2)}, u32[]{:S(2)}) collective-permute-start(bf16[256,256]{1,0:T(8,128)(2,1)S(1)} %get-tuple-element.33), channel_id=1, source_target_pairs={{0,4},{4,8},{8,12},{12,16},{16,20},{20,24},{24,28},{28,0},{1,5},{5... | collective-permute-start | bytes 393224 | tf_op jit(solution)/shard_map/ppermute | solution.py:59
  199.0 7.4 %collective-permute-start.33 = (bf16[256,256]{1,0:T(8,128)(2,1)S(1)}, bf16[256,256]{1,0:T(8,128)(2,1)S(1)}, u32[]{:S(2)}, u32[]{:S(2)}) collective-permute-start(bf16[256,256]{1,0:T(8,128)(2,1)S(1)} %get-tuple-element.34), channel_id=1, source_target_pairs={{0,28},{4,0},{8,4},{12,8},{16,12},{20,16},{24,20},{28,24},{1,29},{... | collective-permute-start | bytes 393224 | tf_op jit(solution)/shard_map/ppermute | solution.py:61
  206.3 19.0 %copy-start.14 = (bf16[256,512]{1,0:T(8,128)(2,1)S(1)}, bf16[256,512]{1,0:T(8,128)(2,1)}, u32[]{:S(2)}) copy-start(bf16[256,512]{1,0:T(8,128)(2,1)} %copy-done.13) | copy-start | bytes 786436
  206.4 6.3 %collective-permute-start.30 = (bf16[256,256]{1,0:T(8,128)(2,1)S(1)}, bf16[256,256]{1,0:T(8,128)(2,1)S(1)}, u32[]{:S(2)}, u32[]{:S(2)}) collective-permute-start(bf16[256,256]{1,0:T(8,128)(2,1)S(1)} %fusion.17), channel_id=1, source_target_pairs={{0,4},{4,8},{8,12},{12,16},{16,20},{20,24},{24,28},{28,0},{1,5},{5... | collective-permute-start | bytes 393224 | tf_op jit(solution)/shard_map/ppermute | solution.py:59
  212.7 6.3 %collective-permute-start.31 = (bf16[256,256]{1,0:T(8,128)(2,1)S(1)}, bf16[256,256]{1,0:T(8,128)(2,1)S(1)}, u32[]{:S(2)}, u32[]{:S(2)}) collective-permute-start(bf16[256,256]{1,0:T(8,128)(2,1)S(1)} %get-tuple-element.45), channel_id=1, source_target_pairs={{0,4},{4,8},{8,12},{12,16},{16,20},{20,24},{24,28},{28,0},{1,5},{5... | collective-permute-start | bytes 393224 | tf_op jit(solution)/shard_map/ppermute | solution.py:59
  212.8 6.2 %collective-permute-start.34 = (bf16[256,256]{1,0:T(8,128)(2,1)S(1)}, bf16[256,256]{1,0:T(8,128)(2,1)S(1)}, u32[]{:S(2)}, u32[]{:S(2)}) collective-permute-start(bf16[256,256]{1,0:T(8,128)(2,1)S(1)} %get-tuple-element.46), channel_id=1, source_target_pairs={{0,28},{4,0},{8,4},{12,8},{16,12},{20,16},{24,20},{28,24},{1,29},{... | collective-permute-start | bytes 393224 | tf_op jit(solution)/shard_map/ppermute | solution.py:61
  219.0 6.3 %collective-permute-start.32 = (bf16[256,256]{1,0:T(8,128)(2,1)S(1)}, bf16[256,256]{1,0:T(8,128)(2,1)S(1)}, u32[]{:S(2)}, u32[]{:S(2)}) collective-permute-start(bf16[256,256]{1,0:T(8,128)(2,1)S(1)} %get-tuple-element.43), channel_id=1, source_target_pairs={{0,4},{4,8},{8,12},{12,16},{16,20},{20,24},{24,28},{28,0},{1,5},{5... | collective-permute-start | bytes 393224 | tf_op jit(solution)/shard_map/ppermute | solution.py:59
  219.1 6.2 %collective-permute-start.35 = (bf16[256,256]{1,0:T(8,128)(2,1)S(1)}, bf16[256,256]{1,0:T(8,128)(2,1)S(1)}, u32[]{:S(2)}, u32[]{:S(2)}) collective-permute-start(bf16[256,256]{1,0:T(8,128)(2,1)S(1)} %get-tuple-element.44), channel_id=1, source_target_pairs={{0,28},{4,0},{8,4},{12,8},{16,12},{20,16},{24,20},{28,24},{1,29},{... | collective-permute-start | bytes 393224 | tf_op jit(solution)/shard_map/ppermute | solution.py:61
Sparse Core Ops, SparseCore 0:
  20.4 33.0 all-gather.3
  102.3 45.4 all-gather.5
